TPU v7x, 128 devices: a whole 4x4x4 slice. The times are simulated.
128 devices in a mesh: row: 8 (over x, y_lo), col: 16 (over z, y_hi, core).
Axes of the slice: x: 4, y: 4 (y_hi: 2, y_lo: 2; y = y_hi * 2 + y_lo), z: 4, core: 2. Of those that a mesh axis runs over, the one named last changes fastest.
Arguments:
- source_blocks: float32 [16384, 24576], P('row', 'col'), may hold values from -6 to 6
Outputs:
- target_blocks: float32 [8192, 49152], P('row', 'col')
- column_sums: float32 [49152], P('col')
- frobenius: float32 [], replicated
All inputs are finite; a program needn't handle non-finite values.
Results may differ from a plain program's by a relative error of at most 0.00002.
Values sent between devices are 32-bit elements; how exact they have to be, the bound alone decides.
A program may use at most 128 MiB of HBM per device.

v0:
```python
import math

import jax.numpy as jnp

N_ROW = 8
N_COL = 16
N = 24576
SB = 128
RB = 2
TB = 512
M = 16384
E = 6


def reference(source_blocks):
    row_count = N_ROW
    col_count = N_COL
    cells = source_blocks.reshape(
        row_count, M // row_count // SB, SB, col_count, N // col_count // SB, SB
    )
    matrix = cells.transpose(1, 0, 2, 4, 3, 5).reshape(M, N)
    pieces = matrix.reshape(RB, 2, 4, row_count // 4, TB, E, 2, col_count // 4, TB)
    target_blocks = pieces.transpose(3, 2, 0, 4, 7, 1, 6, 5, 8).reshape(M // 2, 2 * N)
    scale = 1.0 / math.sqrt(M)
    totals = jnp.sum(matrix, axis=0) * scale
    grouped = totals.reshape(E, 2, col_count // 4, TB).transpose(2, 1, 0, 3)
    column_sums = jnp.broadcast_to(grouped[:, None], (col_count // 4, 2, 2, E, TB)).reshape(2 * N)
    frobenius = jnp.sqrt(jnp.sum(matrix * matrix) / (M * N))
    return (target_blocks, column_sums, frobenius)


def solution(mesh):
    return reference
```

profile of v0, /device:TPU:8, one launch (start us, length us, event | category | flops | bytes accessed | tf_op | source)
XLA Modules:
  0.0 468.2 jit_solution(3884616431100555667)
XLA Ops:
  0.6 15.1 %reshape.33 = f32[2,2,4,1,1,128,6,2,1,1,1,128]{11,7,6,5,2,1,0,10,9,8,4,3:T(2,128)} reshape(f32[2048,1536]{1,0:T(8,128)} %param) | data formatting | bytes 25165824 | tf_op jit(solution)/reshape;jit(solution)/reshape | solution.py:22
  15.7 11.1 %copy.11 = f32[4,2,2,2,1,1,128,6,1,1,1,128]{11,6,10,9,8,7,5,4,3,2,1,0:T(8,128)} copy(f32[4,2,2,2,1,1,128,6,1,1,1,128]{11,1,7,6,0,3,2,10,9,8,5,4:T(2,128)} %bitcast.19) | data formatting | bytes 25165824 | tf_op jit(solution)/reshape;jit(solution)/reshape | solution.py:22
  26.8 5.6 %all-to-all-start = ((f32[8,2,2,1,1,128,6,1,1,1,128]{10,5,9,8,7,6,4,3,2,1,0:T(8,128)}), f32[8,2,2,1,1,128,6,1,1,1,128]{10,5,9,8,7,6,4,3,2,1,0:T(8,128)}, u32[]{:S(2)}, u32[]{:S(2)}) async-start(f32[8,2,2,1,1,128,6,1,1,1,128]{10,5,9,8,7,6,4,3,2,1,0:T(8,128)} %bitcast.17), calls=%async_computation | async-start | bytes 25165824 | tf_op jit(solution)/reshape;jit(solution)/reshape | solution.py:22
  32.4 8.4 %multiply_reduce_fusion = (f32[]{:T(128)}, f32[1536]{0:T(1024)S(1)}) fusion(f32[2048,1536]{1,0:T(8,128)} %param), kind=kLoop, calls=%fused_computation | loop fusion | flops 9435647 | bytes 12589060 | tf_op jit(solution)/reduce_sum | solution.py:28
  40.8 139.6 %all-reduce = f32[12,1,128]{2,1,0:T(1,128)S(1)} all-reduce(f32[12,1,128]{2,1,0:T(1,128)S(1)} %reshape.83), channel_id=3, replica_groups=mesh['row'=8,'col'=16] {'row'}, use_global_device_ids=true, to_apply=%region_0.0.clone | all-reduce | flops 1536 | bytes 12288 | tf_op jit(solution)/reduce_sum | solution.py:25
  180.4 0.6 copy.15
  181.0 0.0 all-to-all-done
  181.0 3.2 all-to-all-start.2
  184.2 21.1 %copy.12 = f32[2,2,1,1,4,128,6,1,1,1,2,128]{11,10,9,6,5,4,1,0,8,7,3,2:T(2,128)S(1)} copy(f32[2,2,1,1,4,128,6,1,1,1,2,128]{11,5,9,8,7,6,3,2,1,0,10,4:T(8,128)} %bitcast.3) | data formatting | bytes 25165824 | tf_op jit(solution)/reshape;jit(solution)/reshape | solution.py:22
  205.3 10.5 %copy.13 = f32[2,2,1,1,1,512,6,1,1,256]{9,8,6,5,0,7,4,3,2,1:T(1,128)} copy(f32[2,2,1,1,1,512,6,1,1,256]{9,8,6,5,1,0,7,4,3,2:T(1,128)S(1)} %bitcast.18) | data formatting | bytes 25165824 | tf_op jit(solution)/reshape;jit(solution)/reshape | solution.py:22
  215.8 0.0 all-to-all-done.2
  215.8 8.4 %all-to-all-start.1 = ((f32[2,2,1,1,1,512,6,1,1,256]{9,8,6,5,0,7,4,3,2,1:T(1,128)}), f32[2,2,1,1,1,512,6,1,1,256]{9,8,6,5,0,7,4,3,2,1:T(1,128)}, u32[]{:S(2)}, u32[]{:S(2)}) async-start(f32[2,2,1,1,1,512,6,1,1,256]{9,8,6,5,0,7,4,3,2,1:T(1,128)} %copy.13), calls=%async_computation.1 | async-start | bytes 25165824 | tf_op jit(solution)/reshape;jit(solution)/reshape | solution.py:22
  224.2 197.0 %all-reduce.1 = f32[]{:T(128)} all-reduce(f32[]{:T(128)} %get-tuple-element), channel_id=6, replica_groups=mesh['row'=8,'col'=16] {'row','col'}, use_global_device_ids=true, to_apply=%region_1.0.clone | all-reduce | flops 1 | bytes 8 | tf_op jit(solution)/reduce_sum | solution.py:28
  421.2 6.0 %all-gather = f32[1,1,6,512]{3,1,2,0:T(1,128)S(1)} all-gather(f32[1,1,6,256]{3,1,2,0:T(1,128)S(1)} %bitcast.23), channel_id=5, replica_groups=[64,2]<=[8,4,2,2]T(1,3,0,2), dimensions={3}, use_global_device_ids=true | all-gather | bytes 18432 | tf_op jit(solution)/transpose | solution.py:26
  427.9 0.0 all-to-all-done.1
  427.9 22.2 %copy.14 = f32[2,1,1,1,512,6,1,1,2,256]{9,8,5,4,0,7,6,3,2,1:T(2,128)} copy(f32[2,1,1,1,512,6,1,1,2,256]{9,7,5,4,0,6,3,2,1,8:T(1,128)} %bitcast.5) | data formatting | bytes 25165824 | tf_op jit(solution)/reshape;jit(solution)/reshape | solution.py:22
  450.1 16.4 %reshape.52 = f32[1024,3072]{1,0:T(8,128)} reshape(f32[2,1,1,1,512,6,1,1,2,256]{9,8,5,4,0,7,6,3,2,1:T(2,128)} %copy.14) | data formatting | bytes 25165824 | tf_op jit(solution)/reshape | solution.py:23
  466.5 0.6 copy.18
  (3 shorter events, 0.0 us)
Async XLA Ops:
  26.8 154.2 %all-to-all-start = ((f32[8,2,2,1,1,128,6,1,1,1,128]{10,5,9,8,7,6,4,3,2,1,0:T(8,128)}), f32[8,2,2,1,1,128,6,1,1,1,128]{10,5,9,8,7,6,4,3,2,1,0:T(8,128)}, u32[]{:S(2)}, u32[]{:S(2)}) async-start(f32[8,2,2,1,1,128,6,1,1,1,128]{10,5,9,8,7,6,4,3,2,1,0:T(8,128)} %bitcast.17), calls=%async_computation | async-start | bytes 25165824 | tf_op jit(solution)/reshape;jit(solution)/reshape | solution.py:22
  181.0 34.8 %all-to-all-start.2 = ((f32[1,2,1,6,1,128]{5,4,3,2,0,1:T(1,128)}), f32[1,2,1,6,1,128]{5,4,3,2,0,1:T(1,128)S(1)}, u32[]{:S(2)}, u32[]{:S(2)}) async-start(f32[1,2,1,6,1,128]{5,4,3,2,0,1:T(1,128)} %copy.15), calls=%async_computation.2 | async-start | bytes 12288 | tf_op jit(solution)/transpose | solution.py:26
  215.8 212.1 %all-to-all-start.1 = ((f32[2,2,1,1,1,512,6,1,1,256]{9,8,6,5,0,7,4,3,2,1:T(1,128)}), f32[2,2,1,1,1,512,6,1,1,256]{9,8,6,5,0,7,4,3,2,1:T(1,128)}, u32[]{:S(2)}, u32[]{:S(2)}) async-start(f32[2,2,1,1,1,512,6,1,1,256]{9,8,6,5,0,7,4,3,2,1:T(1,128)} %copy.13), calls=%async_computation.1 | async-start | bytes 25165824 | tf_op jit(solution)/reshape;jit(solution)/reshape | solution.py:22
where the time goes:
time: 469 us; the launch traced here: 468 us
  blocking collectives  343 us (73%)
  local copies, waits for them, and re-layouts  97.5 us (21%)
  starting transfers between devices  17.2 us (4%)
  other arithmetic  8.42 us (2%)
    reduce_sum x1, blocking collectives, reference(): frobenius = jnp.sqrt(jnp.sum(matrix * matrix) / (M * N))  197 us
    reduce_sum x1, blocking collectives, reference(): totals = jnp.sum(matrix, axis=0) * scale  140 us
    reshape x5, local copies, waits for them, and re-layouts, reference(): matrix.reshape(RB, 2, 4, row_count // 4, TB, E, 2, col_count // 4, TB)  79.9 us
    reshape x1, local copies, waits for them, and re-layouts, reference(): pieces.transpose(3, 2, 0, 4, 7, 1, 6, 5, 8).reshape(M // 2, 2 * N)  16.4 us
    reshape x2, starting transfers between devices, reference(): matrix.reshape(RB, 2, 4, row_count // 4, TB, E, 2, col_count // 4, TB)  14 us
  transfers between devices with their start and end apart: 3, of which 0 were waited for; matrix products, arithmetic and copies ran while one was open for 9% of the time, Pallas kernels for 0%

commit v1 on v0

v1 whole, which is shorter than its diff:
```python
import functools

import jax
import jax.numpy as jnp
from jax import lax
from jax.experimental import pallas as pl
from jax.experimental.pallas import tpu as pltpu
from jax.sharding import PartitionSpec as P

MESH = pl.DeviceIdType.MESH
ROWS, COLS = 16384, 24576
HALVES, ROW_PARTS, TILES, E, COL_PARTS = 2, 4, 16, 6, 4
F32 = jnp.float32
PARTNERS = [(dx, dy, dc) for dx in (0, 1) for dy in range(4) for dc in (0, 1)][1:]
SLOTS = 4
CHUNKS = HALVES * 8


def exchange(x_ref, o_ref, sums_ref, square_ref, chunk, part, parts, plane, other, mine, squares,
             own_sem, chunk_sem, send_sem, recv_sem, part_send, part_recv, far_send, far_recv, z_send, z_recv):
    row, col = lax.axis_index("row"), lax.axis_index("col")
    x1, x0, y_lo = row // 4, (row // 2) % 2, row % 2
    z, y_hi, core = col // 4, (col // 2) % 2, col % 2
    y = y_hi * 2 + y_lo
    row_part, col_part = x0 * 2 + y_lo, y_hi * 2 + core

    def partner(dx, dy, dc):
        y2 = (y + dy) % 4
        return (x0 + dx) % 2, y2 // 2, y2 % 2, (core + dc) % 2

    def device(p):
        return (x1 * 4 + p[0] * 2 + p[2], z * 4 + p[1] * 2 + p[3])

    across = ((1 - x1) * 4 + (1 - x0) * 2 + y_lo, col)
    stacked = [(row, ((z + dz) % 4) * 4 + col_part) for dz in (1, 2, 3)]
    partners = [partner(*p) for p in PARTNERS]

    barrier = pltpu.get_barrier_semaphore()
    for other_device in [device(p) for p in partners] + [across] + stacked:
        pl.semaphore_signal(barrier, inc=1, device_id=other_device, device_id_type=MESH)
    pl.semaphore_wait(barrier, len(PARTNERS) + 4)

    def bulk(c, i):
        p = partners[i]
        return pltpu.make_async_remote_copy(
            x_ref.at[c, p[1] * 4 + p[0] * 2 + p[2], :, :, p[3]],
            o_ref.at[c, row_part, :, :, col_part],
            send_sem.at[c, i], recv_sem.at[c, i], device_id=device(p), device_id_type=MESH)

    copies = []
    for i in range(len(PARTNERS)):
        copies.append(bulk(0, i))
        copies[-1].start()

    def load(n):
        return pltpu.make_async_copy(x_ref.at[n // 8, n % 8], chunk.at[n % SLOTS], chunk_sem.at[n % SLOTS])

    for n in range(SLOTS - 1):
        load(n).start()
    own = [
        pltpu.make_async_copy(
            x_ref.at[c, y_hi * 4 + row_part, :, :, core], o_ref.at[c, row_part, :, :, col_part], own_sem.at[c])
        for c in range(HALVES)
    ]
    for copy in own:
        copy.start()

    totals = (jnp.zeros((E, 2, 8, 128), F32), jnp.zeros((E, 2, 8, 128), F32))
    for n in range(CHUNKS):
        if n + SLOTS - 1 < CHUNKS:
            load(n + SLOTS - 1).start()
        load(n).wait()

        def add(t, totals, n=n):
            v = chunk[n % SLOTS, t]
            return totals[0] + v, totals[1] + v * v

        totals = lax.fori_loop(0, TILES, add, totals)
    by_column = jnp.sum(totals[0], axis=2)
    square = jnp.sum(totals[1], axis=(0, 1, 2), keepdims=True).reshape(1, 128)
    for c in range(2):
        part[c, 0:E, :] = by_column[:, c]
        part[c, E:E + 1, :] = square
        part[c, E + 1:E + 2, :] = jnp.zeros((1, 128), F32)
    parts[col_part, row_part] = part[core]

    smalls = []
    for i, p in enumerate(partners):
        smalls.append(pltpu.make_async_remote_copy(
            part.at[p[3]], parts.at[col_part, row_part], part_send.at[i], part_recv.at[i],
            device_id=device(p), device_id_type=MESH))
        smalls[-1].start()
    for i in range(len(PARTNERS)):
        copies.append(bulk(1, i))
        copies[-1].start()

    for copy in smalls:
        copy.wait()
    group = parts[:, 0] + parts[:, 1] + parts[:, 2] + parts[:, 3]
    plane[...] = group
    far = pltpu.make_async_remote_copy(plane, other, far_send.at[0], far_recv.at[0], device_id=across, device_id_type=MESH)
    far.start()
    far.wait()
    whole = group + other[...]
    for e in range(E):
        sums_ref[e * COL_PARTS:(e + 1) * COL_PARTS, :] = whole[:, e] * (1.0 / 128.0)
    own_square = jnp.broadcast_to(whole[0, E] + whole[1, E] + whole[2, E] + whole[3, E], (8, 128))
    mine[...] = own_square
    squares[z] = own_square
    hops = [
        pltpu.make_async_remote_copy(mine, squares.at[z], z_send.at[i], z_recv.at[i], device_id=d, device_id_type=MESH)
        for i, d in enumerate(stacked)
    ]
    for copy in hops:
        copy.start()
    for copy in hops:
        copy.wait()
    square_ref[...] = squares[0] + squares[1] + squares[2] + squares[3]

    for copy in own + copies:
        copy.wait()


def write(o_ref, sums_ref, square_ref, out_ref, columns_ref, norm_ref, sem):
    copies = []
    for c in range(HALVES):
        for r in range(ROW_PARTS):
            copies.append(pltpu.make_async_copy(o_ref.at[c, r], out_ref.at[c, r], sem.at[c, r]))
            copies[-1].start()
    columns_ref[...] = sums_ref[...]
    total = jnp.sum(square_ref[0:1, :])
    norm_ref[0, 0] = jnp.max(jnp.sqrt(jnp.full((8, 128), total / (ROWS * COLS), F32)))
    for copy in copies:
        copy.wait()


def solution(mesh):
    big = (HALVES, ROW_PARTS, TILES, E, COL_PARTS, 8, 128)
    vmem = pl.BlockSpec(memory_space=pltpu.VMEM)
    anywhere = pl.BlockSpec(memory_space=pl.ANY)
    n = len(PARTNERS)

    def body(source):
        x = source.reshape(HALVES, 8, TILES, 8, E, 2, 128).transpose(0, 1, 2, 4, 5, 3, 6)
        o, sums, square = pl.pallas_call(
            exchange,
            name="exchange",
            out_shape=(pltpu.VMEM(big, F32), pltpu.VMEM((E * COL_PARTS, 128), F32), pltpu.VMEM((8, 128), F32)),
            in_specs=[anywhere],
            out_specs=(vmem, vmem, vmem),
            scratch_shapes=[
                pltpu.VMEM((SLOTS, TILES, E, 2, 8, 128), F32),
                pltpu.VMEM((2, 8, 128), F32),
                pltpu.VMEM((COL_PARTS, ROW_PARTS, 8, 128), F32),
                pltpu.VMEM((COL_PARTS, 8, 128), F32),
                pltpu.VMEM((COL_PARTS, 8, 128), F32),
                pltpu.VMEM((8, 128), F32),
                pltpu.VMEM((4, 8, 128), F32),
                pltpu.SemaphoreType.DMA((HALVES,)),
                pltpu.SemaphoreType.DMA((SLOTS,)),
                pltpu.SemaphoreType.DMA((HALVES, n)),
                pltpu.SemaphoreType.DMA((HALVES, n)),
                pltpu.SemaphoreType.DMA((n,)),
                pltpu.SemaphoreType.DMA((n,)),
                pltpu.SemaphoreType.DMA((1,)),
                pltpu.SemaphoreType.DMA((1,)),
                pltpu.SemaphoreType.DMA((3,)),
                pltpu.SemaphoreType.DMA((3,)),
            ],
            compiler_params=pltpu.CompilerParams(collective_id=0, has_side_effects=True, vmem_limit_bytes=40 << 20),
        )(x)
        out, columns, norm = pl.pallas_call(
            write,
            name="write",
            out_shape=(jax.ShapeDtypeStruct(big, F32), jax.ShapeDtypeStruct((E * COL_PARTS, 128), F32),
                       jax.ShapeDtypeStruct((1, 1), F32)),
            in_specs=[vmem, vmem, vmem],
            out_specs=(anywhere, vmem, pl.BlockSpec(memory_space=pltpu.SMEM)),
            scratch_shapes=[pltpu.SemaphoreType.DMA((HALVES, ROW_PARTS))],
            compiler_params=pltpu.CompilerParams(vmem_limit_bytes=40 << 20),
        )(o, sums, square)
        return out.transpose(0, 1, 2, 5, 3, 4, 6).reshape(1024, 3072), columns.reshape(3072), norm.reshape(())

    return jax.shard_map(body, mesh=mesh, in_specs=P("row", "col"), out_specs=(P("row", "col"), P("col"), P()),
                         check_vma=False)
```

time: 469 us -> 152 us (0.32)
  blocking collectives: 343 us -> 0 us
  Pallas kernels: 0 us -> 149 us
  local copies, waits for them, and re-layouts: 97.5 us -> 0 us
  starting transfers between devices: 17.2 us -> 0 us
  other arithmetic: 8.42 us -> 0 us
    reduce_sum x2 -> x0, blocking collectives: 337 us -> none  [the longest x1 197 us: reference(): frobenius = jnp.sqrt(jnp.sum(matrix * matrix) / (M * N))]
    pallas_call x0 -> x2, Pallas kernels: none -> 149 us  [the longest x1 144 us: body(): pl.pallas_call(exchange, name='exchange', out_shape=(pltpu.VMEM(big, F32)...]
    reshape x6 -> x0, local copies, waits for them, and re-layouts: 96.3 us -> none  [the longest x5 79.9 us: reference(): matrix.reshape(RB, 2, 4, row_count // 4, TB, E, 2, col_count // 4, TB)]
    reshape x2 -> x0, starting transfers between devices: 14 us -> none  [reference(): matrix.reshape(RB, 2, 4, row_count // 4, TB, E, 2, col_count // 4, TB)]
    reduce_sum x1 -> x0, other arithmetic: 8.41 us -> none  [reference(): frobenius = jnp.sqrt(jnp.sum(matrix * matrix) / (M * N))]
    transpose x1 -> x0, blocking collectives: 5.97 us -> none  [reference(): grouped = totals.reshape(E, 2, col_count // 4, TB).transpose(2, 1, 0, 3)]
  transfers between devices with their start and end apart: 3 -> 0, of which waited for: 0 -> 0; matrix products, arithmetic and copies ran while one was open for 9% -> 0% of each run, Pallas kernels for 0% -> 0%
where the time goes in v1:
time: 152 us; the launch traced here: 150 us
  Pallas kernels  149 us (98%)
    pallas_call x1, Pallas kernels, body(): pl.pallas_call(exchange, name='exchange', out_shape=(pltpu.VMEM(big, F32)...  144 us
    pallas_call x1, Pallas kernels, body(): pl.pallas_call(write, name='write', out_shape=(jax.ShapeDtypeStruct(big,...  5.27 us

profile of v1, /device:TPU:8, one launch (start us, length us, event | category | flops | bytes accessed | tf_op | source)
XLA Modules:
  0.0 150.0 jit_solution(13851568944193939895)
XLA Ops:
  0.6 144.1 %exchange.1 = (f32[2,4,16,6,4,8,128]{6,5,4,3,2,1,0:T(8,128)S(1)}, f32[24,128]{1,0:T(8,128)S(1)}, f32[8,128]{1,0:T(8,128)S(1)}) custom-call(f32[2,8,16,6,2,8,128]{6,5,4,3,2,1,0:T(8,128)} %bitcast.8), custom_call_target="tpu_custom_call" | custom-call | tf_op jit(solution)/shard_map/exchange/pallas_call | solution.py:145
  144.7 5.3 %write.1 = (f32[2,4,16,6,4,8,128]{6,5,4,3,2,1,0:T(8,128)}, f32[24,128]{1,0:T(8,128)}, f32[1,1]{1,0:T(1,128)}) custom-call(f32[2,4,16,6,4,8,128]{6,5,4,3,2,1,0:T(8,128)S(1)} %get-tuple-element.9.o_ref, f32[24,128]{1,0:T(8,128)S(1)} %get-tuple-element.10.sums_ref, f32[8,128]{1,0:T(8,128)S(1)} %get-tuple-element.11.square_ref), custom_call_target="tpu_custom_call" | custom-call | tf_op jit(solution)/shard_map/write/pallas_call | solution.py:172

commit v2 on v0

v2 whole, which is shorter than its diff:
```python
import functools

import jax
import jax.numpy as jnp
from jax import lax
from jax.experimental import pallas as pl
from jax.experimental.pallas import tpu as pltpu
from jax.sharding import PartitionSpec as P


AXES = ("row", "col")
ROWS, COLS = 16384, 24576
N_ROW, N_COL = 8, 16
HALVES, ROW_PARTS, TILES, E, COL_PARTS = 2, 4, 16, 6, 4
F32 = jnp.float32
WHOLE, UPPER, LOWER = (0, 1), (0,), (1,)
FIRST = [(1, 0, 0, WHOLE), (0, 1, 0, WHOLE), (0, 3, 0, WHOLE)]
SECOND = [(1, 0, 1, WHOLE), (0, 1, 1, UPPER), (0, 3, 1, UPPER)]
THIRD = [(1, 1, 0, WHOLE), (0, 1, 1, LOWER), (0, 3, 1, LOWER), (0, 2, 0, WHOLE), (0, 2, 1, WHOLE), (1, 3, 0, WHOLE),
         (1, 1, 1, WHOLE), (1, 3, 1, WHOLE), (0, 0, 1, WHOLE), (1, 2, 0, WHOLE), (1, 2, 1, WHOLE)]
NEAR = [(0, 1, 0), (0, 3, 0), (0, 2, 0), (1, 0, 0), (1, 1, 0), (1, 3, 0), (1, 2, 0)]
LATE = [(0, 1, 1, LOWER), (0, 3, 1, LOWER), (0, 2, 0, WHOLE), (0, 2, 1, WHOLE), (1, 2, 1, WHOLE)]
MIDDLE = [(1, 2, 0, WHOLE)]
SOON = [f for f in FIRST + SECOND + THIRD if f not in LATE + MIDDLE]
SLOTS = 4
CHUNKS = HALVES * 8
VMEM = pl.BlockSpec(memory_space=pltpu.VMEM)
HBM = pl.BlockSpec(memory_space=pltpu.HBM)
SMALL = (8, 128)
BIG = (HALVES, ROW_PARTS, TILES, E, COL_PARTS, 8, 128)


def place(row, col):
    return {"x1": row // 4, "x0": (row // 2) % 2, "y": (col // 2) % 2 * 2 + row % 2, "z": col // 4, "core": col % 2}


def here():
    return place(lax.axis_index("row"), lax.axis_index("col"))


def shifted(at, flow, sign):
    dx, dy, dc = flow[:3]
    core = (at["core"] + dc) % 2
    turn = 1 - 2 * (at["core"] if sign > 0 else core)
    return at | {"x0": (at["x0"] + dx) % 2, "y": (at["y"] + sign * turn * dy + 4) % 4, "core": core}


def device(at):
    return at["x1"] * 4 + at["x0"] * 2 + at["y"] % 2, at["z"] * 4 + at["y"] // 2 * 2 + at["core"]


def row_part(at):
    return at["x0"] * 2 + at["y"] % 2


def col_part(at):
    return at["y"] // 2 * 2 + at["core"]


def slab(at):
    return at["y"] // 2 * 4 + at["x0"] * 2 + at["y"] % 2


def moved(target):
    pairs = []
    for row in range(N_ROW):
        for col in range(N_COL):
            to_row, to_col = device(target(place(row, col)))
            pairs.append((row * N_COL + col, to_row * N_COL + to_col))
    return pairs


def permutation(flow):
    return moved(lambda at: shifted(at, flow, 1))


def half(piece, i):
    return piece.at[i * TILES:(i + 1) * TILES]


def pack(flows, x_ref, *refs):
    n = len(flows)
    sem, outs = refs[-1], refs[len(refs) - 1 - n:-1]
    at = here()
    copies = []
    for k, flow in enumerate(flows):
        to = shifted(at, flow, 1)
        for i, c in enumerate(flow[3]):
            copies.append(pltpu.make_async_copy(x_ref.at[c, slab(to), :, :, to["core"]], half(outs[k], i), sem.at[i, k]))
            copies[-1].start()
    for copy in copies:
        copy.wait()


def reduce(x_ref, _, part_ref, chunk, sem):
    def load(n):
        return pltpu.make_async_copy(x_ref.at[n // 8, n % 8], chunk.at[n % SLOTS], sem.at[n % SLOTS])

    for n in range(SLOTS - 1):
        load(n).start()
    totals = (jnp.zeros((E, 2, 8, 128), F32), jnp.zeros((E, 2, 8, 128), F32))
    for n in range(CHUNKS):
        if n + SLOTS - 1 < CHUNKS:
            load(n + SLOTS - 1).start()
        load(n).wait()

        def add(t, totals, n=n):
            v = chunk[n % SLOTS, t]
            return totals[0] + v, totals[1] + v * v

        totals = lax.fori_loop(0, TILES, add, totals)
    by_column = jnp.sum(totals[0], axis=2)
    square = jnp.sum(totals[1], axis=(0, 1, 2), keepdims=True).reshape(1, 128)
    for c in range(2):
        part_ref[c, 0:E, :] = by_column[:, c]
        part_ref[c, E:E + 1, :] = square
        part_ref[c, E + 1:E + 2, :] = jnp.zeros((1, 128), F32)


def write(at, flows, pieces, out_ref, sem):
    copies = []
    for k, flow in enumerate(flows):
        by = shifted(at, flow, -1)
        for i, c in enumerate(flow[3]):
            copies.append(pltpu.make_async_copy(
                half(pieces[k], i), out_ref.at[c, row_part(by), :, :, col_part(by)], sem.at[i, k]))
            copies[-1].start()
    return copies


def pair(part, twin, both_ref):
    core = lax.axis_index("col") % 2
    both_ref[0] = part[core]
    both_ref[1] = twin[core]


def gather(*refs):
    plane_ref, parts = refs[-2:]
    at = here()
    for flow, both in zip([(0, 0, 0)] + NEAR, refs):
        by = shifted(at, flow, -1)
        parts[col_part(by), row_part(by)] = both[0]
        parts[col_part(by | {"core": 1 - at["core"]}), row_part(by)] = both[1]
    plane_ref[...] = parts[:, 0] + parts[:, 1] + parts[:, 2] + parts[:, 3]


def write_soon(x_ref, *refs):
    n = len(SOON)
    pieces, (out_ref, own, own_sem, sem) = refs[:n], refs[n:]
    at = here()
    load = pltpu.make_async_copy(x_ref.at[:, slab(at), :, :, at["core"]], own, own_sem.at[0])
    load.start()
    copies = write(at, SOON, pieces, out_ref, sem)
    load.wait()
    copies.append(pltpu.make_async_copy(own, out_ref.at[:, row_part(at), :, :, col_part(at)], own_sem.at[1]))
    copies[-1].start()
    for copy in copies:
        copy.wait()


def write_middle(_, *refs):
    n = len(MIDDLE)
    pieces, (out_ref, sem) = refs[:n], refs[n:]
    for copy in write(here(), MIDDLE, pieces, out_ref, sem):
        copy.wait()


def combine(plane_ref, other_ref, sums_ref, square_ref):
    whole = plane_ref[...] + other_ref[...]
    for e in range(E):
        sums_ref[e * COL_PARTS:(e + 1) * COL_PARTS, :] = whole[:, e] * (1.0 / 128.0)
    square_ref[...] = jnp.broadcast_to(whole[0, E] + whole[1, E] + whole[2, E] + whole[3, E], SMALL)


def write_late(_, sums_ref, square_ref, z1, z2, z3, *refs):
    n = len(LATE)
    pieces, (out_ref, columns_ref, norm_ref, squares, sem) = refs[:n], refs[n:]
    at = here()
    copies = write(at, LATE, pieces, out_ref, sem)
    columns_ref[...] = sums_ref[...]
    for dz, ref in enumerate((square_ref, z1, z2, z3)):
        squares[(at["z"] - dz + 4) % 4] = ref[...]
    total = jnp.sum((squares[0] + squares[1] + squares[2] + squares[3])[0:1, :])
    norm_ref[0, 0] = jnp.max(jnp.sqrt(jnp.full(SMALL, total / (ROWS * COLS), F32)))
    for copy in copies:
        copy.wait()


FLOPS_PER_US = 10_000_000


def plain(kernel, outs, in_specs, out_specs, scratch, us, **kw):
    return pl.pallas_call(
        kernel, out_shape=outs, in_specs=in_specs, out_specs=out_specs, scratch_shapes=scratch,
        cost_estimate=pl.CostEstimate(flops=int(us * FLOPS_PER_US), bytes_accessed=1 << 20, transcendentals=0),
        compiler_params=pltpu.CompilerParams(vmem_limit_bytes=12 << 20), **kw)


def body(source):
    dma = pltpu.SemaphoreType.DMA
    x = source.reshape(HALVES, 8, TILES, 8, E, 2, 128).transpose(0, 1, 2, 4, 5, 3, 6)
    x = pltpu.with_memory_space_constraint(x, pltpu.HBM)
    landed = {}

    def permute(value, pairs):
        return lax.ppermute(value, AXES, pairs)

    def go(flows, *before):
        n = len(flows)
        pieces = plain(
            functools.partial(pack, flows), tuple(pltpu.VMEM((len(f[3]) * TILES, E, 8, 128), F32) for f in flows),
            [HBM] + [VMEM] * len(before), (VMEM,) * n, [dma((HALVES, n))], 1 + n / 3)(x, *before)
        for flow, piece in zip(flows, pieces):
            landed[flow] = permute(piece, permutation(flow))
        return pieces

    pieces = go(FIRST)
    pieces = go(SECOND, pieces[0])
    pieces = go(THIRD, pieces[0])
    tiles = functools.partial(pltpu.VMEM, dtype=F32)
    part = plain(reduce, tiles((2, *SMALL)), [HBM, VMEM], VMEM,
                 [pltpu.VMEM((SLOTS, TILES, E, 2, 8, 128), F32), dma((SLOTS,))], 7)(x, pieces[0])
    twin = permute(part, permutation((0, 0, 1)))
    both = plain(pair, tiles((2, *SMALL)), [VMEM] * 2, VMEM, [], 1)(part, twin)
    near = [permute(both, permutation(f)) for f in NEAR]
    plane = plain(gather, tiles((COL_PARTS, *SMALL)), [VMEM] * (1 + len(NEAR)), VMEM,
                  [tiles((COL_PARTS, ROW_PARTS, *SMALL))], 1)(both, *near)
    other = permute(plane, moved(lambda at: at | {"x1": 1 - at["x1"], "x0": 1 - at["x0"]}))
    sums, square = plain(
        combine, (tiles((E * COL_PARTS, 128)), tiles(SMALL)), [VMEM] * 2, (VMEM,) * 2, [], 1)(plane, other)
    stacked = [
        permute(square, moved(lambda at: at | {"z": (at["z"] + dz) % 4})) for dz in (1, 2, 3)]
    n = len(SOON)
    out = plain(
        write_soon, jax.ShapeDtypeStruct(BIG, F32), [HBM] + [VMEM] * n, HBM,
        [pltpu.VMEM((HALVES, TILES, E, 8, 128), F32), dma((2,)), dma((HALVES, n))], 5,
    )(x, *[landed[f] for f in SOON])
    n = len(MIDDLE)
    out = plain(
        write_middle, jax.ShapeDtypeStruct(BIG, F32), [HBM] + [VMEM] * n, HBM,
        [dma((HALVES, n))], 2, input_output_aliases={0: 0})(out, *[landed[f] for f in MIDDLE])
    n = len(LATE)
    out, columns, norm = plain(
        write_late,
        (jax.ShapeDtypeStruct(BIG, F32), jax.ShapeDtypeStruct((E * COL_PARTS, 128), F32),
         jax.ShapeDtypeStruct((1, 1), F32)),
        [HBM] + [VMEM] * (n + 5), (HBM, VMEM, pl.BlockSpec(memory_space=pltpu.SMEM)),
        [pltpu.VMEM((4, *SMALL), F32), dma((HALVES, n))], 2, input_output_aliases={0: 0},
    )(out, sums, square, *stacked, *[landed[f] for f in LATE])
    return out.transpose(0, 1, 2, 5, 3, 4, 6).reshape(1024, 3072), columns.reshape(3072), norm.reshape(())


def solution(mesh):
    return jax.shard_map(body, mesh=mesh, in_specs=P("row", "col"), out_specs=(P("row", "col"), P("col"), P()),
                         check_vma=False)
```

time: 469 us -> 222 us (0.47)
  blocking collectives: 343 us -> 0 us
  waiting for transfers between devices: 0.01 us -> 145 us
  local copies, waits for them, and re-layouts: 97.5 us -> 0 us
  starting transfers between devices: 17.2 us -> 52.1 us
  Pallas kernels: 0 us -> 20.1 us
  other arithmetic: 8.42 us -> 0 us
    reduce_sum x2 -> x0, blocking collectives: 337 us -> none  [the longest x1 197 us: reference(): frobenius = jnp.sqrt(jnp.sum(matrix * matrix) / (M * N))]
    ppermute x0 -> x29, waiting for transfers between devices: none -> 145 us  [permute(): return lax.ppermute(value, AXES, pairs)]
    reshape x6 -> x0, local copies, waits for them, and re-layouts: 96.3 us -> none  [the longest x5 79.9 us: reference(): matrix.reshape(RB, 2, 4, row_count // 4, TB, E, 2, col_count // 4, TB)]
    ppermute x0 -> x29, starting transfers between devices: none -> 52.1 us  [permute(): return lax.ppermute(value, AXES, pairs)]
    pallas_call x0 -> x10, Pallas kernels: none -> 20.1 us  [the longest x3 6.61 us: go(): plain(functools.partial(pack, flows), tuple((pltpu.VMEM((len(f[3]) * TILE...]
    reshape x2 -> x0, starting transfers between devices: 14 us -> none  [reference(): matrix.reshape(RB, 2, 4, row_count // 4, TB, E, 2, col_count // 4, TB)]
    reduce_sum x1 -> x0, other arithmetic: 8.41 us -> none  [reference(): frobenius = jnp.sqrt(jnp.sum(matrix * matrix) / (M * N))]
    transpose x1 -> x0, blocking collectives: 5.97 us -> none  [reference(): grouped = totals.reshape(E, 2, col_count // 4, TB).transpose(2, 1, 0, 3)]
  transfers between devices with their start and end apart: 3 -> 29, of which waited for: 0 -> 14; matrix products, arithmetic and copies ran while one was open for 9% -> 0% of each run, Pallas kernels for 0% -> 2%
where the time goes in v2:
time: 222 us; the launch traced here: 218 us
  waiting for transfers between devices  145 us (65%)
  starting transfers between devices  52.1 us (23%)
  Pallas kernels  20.1 us (9%)
    ppermute x29, waiting for transfers between devices, permute(): return lax.ppermute(value, AXES, pairs)  145 us
    ppermute x29, starting transfers between devices, permute(): return lax.ppermute(value, AXES, pairs)  52.1 us
    pallas_call x3, Pallas kernels, go(): plain(functools.partial(pack, flows), tuple((pltpu.VMEM((len(f[3]) * TILE...  6.61 us
    pallas_call x1, Pallas kernels, body(): plain(reduce, tiles((2, *SMALL)), [HBM, VMEM], VMEM, [pltpu.VMEM((SLOTS,...  6.5 us
  transfers between devices with their start and end apart: 29, of which 14 were waited for; matrix products, arithmetic and copies ran while one was open for 0% of the time, Pallas kernels for 2%

profile of v2, /device:TPU:8, one launch (start us, length us, event | category | flops | bytes accessed | tf_op | source)
XLA Modules:
  0.0 217.7 jit_solution(18090434534060748098)
XLA Ops:
  3.8 3.5 %shard_map.40 = (f32[32,6,8,128]{3,2,1,0:T(8,128)S(1)}, f32[16,6,8,128]{3,2,1,0:T(8,128)S(1)}, f32[16,6,8,128]{3,2,1,0:T(8,128)S(1)}, f32[32,6,8,128]{3,2,1,0:T(...) custom-call(f32[2,8,16,6,2,8,128]{6,5,4,3,2,1,0:T(8,128)} %bitcast.1, ...), custom_call_target="tpu_custom_call" | custom-call | flops 46666664 | bytes 1048576 | tf_op jit(solution)/shard_map/pallas_call | solution.py:210
  7.3 6.5 %shard_map.43.part = f32[2,8,128]{2,1,0:T(8,128)S(1)} custom-call(f32[2,8,16,6,2,8,128]{6,5,4,3,2,1,0:T(8,128)} %bitcast.11, f32[32,6,8,128]{3,2,1,0:T(8,128)S(1)} %get-tuple-element.31._), custom_call_target="tpu_custom_call" | custom-call | flops 70000000 | bytes 1048576 | tf_op jit(solution)/shard_map/pallas_call | solution.py:221
  15.0 3.3 %collective-permute-start.19 = (f32[2,8,128]{2,1,0:T(8,128)S(1)}, f32[2,8,128]{2,1,0:T(8,128)S(1)}, u32[]{:S(2)}, u32[]{:S(2)}) collective-permute-start(f32[2,8,128]{2,1,0:T(8,128)S(1)} %shard_map.44.refs_0_), channel_id=1, source_target_pairs={{0,34},{1,35},{2,32},{3,33},{4,38},{5,39},{6,36},{7,37},{8,42},{9,... | collective-permute-start | bytes 24584 | tf_op jit(solution)/shard_map/ppermute | solution.py:206
  21.7 2.4 %collective-permute-start.15 = (f32[2,8,128]{2,1,0:T(8,128)S(1)}, f32[2,8,128]{2,1,0:T(8,128)S(1)}, u32[]{:S(2)}, u32[]{:S(2)}) collective-permute-start(f32[2,8,128]{2,1,0:T(8,128)S(1)} %shard_map.44.refs_0_), channel_id=1, source_target_pairs={{0,2},{1,3},{2,0},{3,1},{4,6},{5,7},{6,4},{7,5},{8,10},{9,11},{10,... | collective-permute-start | bytes 24584 | tf_op jit(solution)/shard_map/ppermute | solution.py:206
  24.2 2.0 collective-permute-start.13
  28.1 2.9 %collective-permute-start.20 = (f32[4,8,128]{2,1,0:T(8,128)S(1)}, f32[4,8,128]{2,1,0:T(8,128)S(1)}, u32[]{:S(2)}, u32[]{:S(2)}) collective-permute-start(f32[4,8,128]{2,1,0:T(8,128)S(1)} %shard_map.45.plane_ref), channel_id=1, source_target_pairs={{0,96},{1,97},{2,98},{3,99},{4,100},{5,101},{6,102},{7,103},{8,104... | collective-permute-start | bytes 49160 | tf_op jit(solution)/shard_map/ppermute | solution.py:206
  31.0 2.1 collective-permute-done.20.other_ref
  33.1 4.1 %collective-permute-start.23 = (f32[8,128]{1,0:T(8,128)S(1)}, f32[8,128]{1,0:T(8,128)S(1)}, u32[]{:S(2)}, u32[]{:S(2)}) collective-permute-start(f32[8,128]{1,0:T(8,128)S(1)} %get-tuple-element.38.square_ref), channel_id=1, source_target_pairs={{0,12},{1,13},{2,14},{3,15},{4,0},{5,1},{6,2},{7,3},{8,4},{9,5},{1... | collective-permute-start | bytes 12296 | tf_op jit(solution)/shard_map/ppermute | solution.py:206
  40.3 4.4 %collective-permute-start.5 = (f32[16,6,8,128]{3,2,1,0:T(8,128)S(1)}, f32[16,6,8,128]{3,2,1,0:T(8,128)S(1)}, u32[]{:S(2)}, u32[]{:S(2)}) collective-permute-start(f32[16,6,8,128]{3,2,1,0:T(8,128)S(1)} %get-tuple-element.30), channel_id=1, source_target_pairs={{0,19},{1,16},{2,17},{3,18},{4,23},{5,20},{6,21},{7,22},{8,27},{9,... | collective-permute-start | bytes 1179656 | tf_op jit(solution)/shard_map/ppermute | solution.py:206
  45.9 19.9 %collective-permute-done.4.refs_4_ = f32[16,6,8,128]{3,2,1,0:T(8,128)S(1)} collective-permute-done((f32[16,6,8,128]{3,2,1,0:T(8,128)S(1)}, f32[16,6,8,128]{3,2,1,0:T(8,128)S(1)}, u32[]{:S(2)}, u32[]{:S(2)}) %collective-permute-start.4) | collective-permute-done | bytes 393248 | tf_op jit(solution)/shard_map/ppermute | solution.py:206
  65.8 6.4 %collective-permute-start.7 = (f32[32,6,8,128]{3,2,1,0:T(8,128)S(1)}, f32[32,6,8,128]{3,2,1,0:T(8,128)S(1)}, u32[]{:S(2)}, u32[]{:S(2)}) collective-permute-start(f32[32,6,8,128]{3,2,1,0:T(8,128)S(1)} %get-tuple-element.32), channel_id=1, source_target_pairs={{0,50},{1,49},{2,48},{3,51},{4,54},{5,53},{6,52},{7,55},{8,58},{9,... | collective-permute-start | bytes 2359304 | tf_op jit(solution)/shard_map/ppermute | solution.py:206
  73.9 11.6 %collective-permute-done.3.refs_3_ = f32[32,6,8,128]{3,2,1,0:T(8,128)S(1)} collective-permute-done((f32[32,6,8,128]{3,2,1,0:T(8,128)S(1)}, f32[32,6,8,128]{3,2,1,0:T(8,128)S(1)}, u32[]{:S(2)}, u32[]{:S(2)}) %collective-permute-start.3) | collective-permute-done | bytes 786464 | tf_op jit(solution)/shard_map/ppermute | solution.py:206
  85.5 3.5 %collective-permute-start.11 = (f32[32,6,8,128]{3,2,1,0:T(8,128)S(1)}, f32[32,6,8,128]{3,2,1,0:T(8,128)S(1)}, u32[]{:S(2)}, u32[]{:S(2)}) collective-permute-start(f32[32,6,8,128]{3,2,1,0:T(8,128)S(1)} %get-tuple-element.36), channel_id=1, source_target_pairs={{0,34},{1,35},{2,32},{3,33},{4,38},{5,39},{6,36},{7,37},{8,42},{9,... | collective-permute-start | bytes 2359304 | tf_op jit(solution)/shard_map/ppermute | solution.py:206
  89.0 15.3 %collective-permute-done.7.refs_7_ = f32[32,6,8,128]{3,2,1,0:T(8,128)S(1)} collective-permute-done((f32[32,6,8,128]{3,2,1,0:T(8,128)S(1)}, f32[32,6,8,128]{3,2,1,0:T(8,128)S(1)}, u32[]{:S(2)}, u32[]{:S(2)}) %collective-permute-start.7) | collective-permute-done | bytes 786464 | tf_op jit(solution)/shard_map/ppermute | solution.py:206
  104.4 2.0 collective-permute-start.6
  106.4 11.0 %collective-permute-done.8.refs_8_ = f32[32,6,8,128]{3,2,1,0:T(8,128)S(1)} collective-permute-done((f32[32,6,8,128]{3,2,1,0:T(8,128)S(1)}, f32[32,6,8,128]{3,2,1,0:T(8,128)S(1)}, u32[]{:S(2)}, u32[]{:S(2)}) %collective-permute-start.8) | collective-permute-done | bytes 786464 | tf_op jit(solution)/shard_map/ppermute | solution.py:206
  117.4 5.0 %collective-permute-start.26 = (f32[32,6,8,128]{3,2,1,0:T(8,128)S(1)}, f32[32,6,8,128]{3,2,1,0:T(8,128)S(1)}, u32[]{:S(2)}, u32[]{:S(2)}) collective-permute-start(f32[32,6,8,128]{3,2,1,0:T(8,128)S(1)} %get-tuple-element.41), channel_id=1, source_target_pairs={{0,2},{1,3},{2,0},{3,1},{4,6},{5,7},{6,4},{7,5},{8,10},{9,11},{10,... | collective-permute-start | bytes 2359304 | tf_op jit(solution)/shard_map/ppermute | solution.py:206
  122.4 14.8 %collective-permute-done.9.refs_9_ = f32[32,6,8,128]{3,2,1,0:T(8,128)S(1)} collective-permute-done((f32[32,6,8,128]{3,2,1,0:T(8,128)S(1)}, f32[32,6,8,128]{3,2,1,0:T(8,128)S(1)}, u32[]{:S(2)}, u32[]{:S(2)}) %collective-permute-start.9) | collective-permute-done | bytes 786464 | tf_op jit(solution)/shard_map/ppermute | solution.py:206
  137.2 6.6 %collective-permute-start.27 = (f32[32,6,8,128]{3,2,1,0:T(8,128)S(1)}, f32[32,6,8,128]{3,2,1,0:T(8,128)S(1)}, u32[]{:S(2)}, u32[]{:S(2)}) collective-permute-start(f32[32,6,8,128]{3,2,1,0:T(8,128)S(1)} %get-tuple-element.42), channel_id=1, source_target_pairs={{0,3},{1,2},{2,1},{3,0},{4,7},{5,6},{6,5},{7,4},{8,11},{9,10},{10,... | collective-permute-start | bytes 2359304 | tf_op jit(solution)/shard_map/ppermute | solution.py:206
  143.8 11.8 %collective-permute-done.11.refs_0_ = f32[32,6,8,128]{3,2,1,0:T(8,128)S(1)} collective-permute-done((f32[32,6,8,128]{3,2,1,0:T(8,128)S(1)}, f32[32,6,8,128]{3,2,1,0:T(8,128)S(1)}, u32[]{:S(2)}, u32[]{:S(2)}) %collective-permute-start.11) | collective-permute-done | bytes 786464 | tf_op jit(solution)/shard_map/ppermute | solution.py:206
  155.6 19.2 %collective-permute-done.6.refs_6_ = f32[32,6,8,128]{3,2,1,0:T(8,128)S(1)} collective-permute-done((f32[32,6,8,128]{3,2,1,0:T(8,128)S(1)}, f32[32,6,8,128]{3,2,1,0:T(8,128)S(1)}, u32[]{:S(2)}, u32[]{:S(2)}) %collective-permute-start.6) | collective-permute-done | bytes 786464 | tf_op jit(solution)/shard_map/ppermute | solution.py:206
  174.8 3.6 %shard_map.41._ = f32[2,4,16,6,4,8,128]{6,5,4,3,2,1,0:T(8,128)} custom-call(f32[2,8,16,6,2,8,128]{6,5,4,3,2,1,0:T(8,128)} %bitcast.12, f32[32,6,8,128]{3,2,1,0:T(8,128)S(1)} %collective-permute-done.refs_0_, f32[32,6,8,128]{3,2,1,0:T(8,128)S(1)} %collective-permute-done.1.refs_1_, f32[32,6,8,128]{3,2,1,0:T(8,128)S(1)} %collective-permute-done.2.refs_2_, ...), custom_call_target="tpu_custom_call" | custom-call | flops 50000000 | bytes 1048576 | tf_op jit(solution)/shard_map/pallas_call | solution.py:234
  179.4 34.4 %collective-permute-done.24.refs_0_ = f32[16,6,8,128]{3,2,1,0:T(8,128)S(1)} collective-permute-done((f32[16,6,8,128]{3,2,1,0:T(8,128)S(1)}, f32[16,6,8,128]{3,2,1,0:T(8,128)S(1)}, u32[]{:S(2)}, u32[]{:S(2)}) %collective-permute-start.24) | collective-permute-done | bytes 393248 | tf_op jit(solution)/shard_map/ppermute | solution.py:206
  215.3 2.4 %shard_map.47 = (f32[2,4,16,6,4,8,128]{6,5,4,3,2,1,0:T(8,128)}, f32[24,128]{1,0:T(8,128)}, f32[1,1]{1,0:T(1,128)}) custom-call(f32[2,4,16,6,4,8,128]{6,5,4,3,2,1,0:T(8,128)} %shard_map.42._, f32[24,128]{1,0:T(8,128)S(1)} %get-tuple-element.37.sums_ref, f32[8,128]{1,0:T(8,128)S(1)} %get-tuple-element.38.square_ref, ...), custom_call_target="tpu_custom_call", output_to_operand_aliasing={{0}: (0, {})} | custom-call | flops 20000000 | bytes 1048576 | tf_op jit(solution)/shard_map/pallas_call | solution.py:243
  (44 shorter events, 18.1 us)
Async XLA Ops:
  15.0 9.1 %collective-permute-start.19 = (f32[2,8,128]{2,1,0:T(8,128)S(1)}, f32[2,8,128]{2,1,0:T(8,128)S(1)}, u32[]{:S(2)}, u32[]{:S(2)}) collective-permute-start(f32[2,8,128]{2,1,0:T(8,128)S(1)} %shard_map.44.refs_0_), channel_id=1, source_target_pairs={{0,34},{1,35},{2,32},{3,33},{4,38},{5,39},{6,36},{7,37},{8,42},{9,... | collective-permute-start | bytes 24584 | tf_op jit(solution)/shard_map/ppermute | solution.py:206
  18.3 5.9 %collective-permute-start.18 = (f32[2,8,128]{2,1,0:T(8,128)S(1)}, f32[2,8,128]{2,1,0:T(8,128)S(1)}, u32[]{:S(2)}, u32[]{:S(2)}) collective-permute-start(f32[2,8,128]{2,1,0:T(8,128)S(1)} %shard_map.44.refs_0_), channel_id=1, source_target_pairs={{0,50},{1,49},{2,48},{3,51},{4,54},{5,53},{6,52},{7,55},{8,58},{9,... | collective-permute-start | bytes 24584 | tf_op jit(solution)/shard_map/ppermute | solution.py:206
  19.6 6.6 %collective-permute-start.17 = (f32[2,8,128]{2,1,0:T(8,128)S(1)}, f32[2,8,128]{2,1,0:T(8,128)S(1)}, u32[]{:S(2)}, u32[]{:S(2)}) collective-permute-start(f32[2,8,128]{2,1,0:T(8,128)S(1)} %shard_map.44.refs_0_), channel_id=1, source_target_pairs={{0,48},{1,51},{2,50},{3,49},{4,52},{5,55},{6,54},{7,53},{8,56},{9,... | collective-permute-start | bytes 24584 | tf_op jit(solution)/shard_map/ppermute | solution.py:206
  21.7 5.2 %collective-permute-start.15 = (f32[2,8,128]{2,1,0:T(8,128)S(1)}, f32[2,8,128]{2,1,0:T(8,128)S(1)}, u32[]{:S(2)}, u32[]{:S(2)}) collective-permute-start(f32[2,8,128]{2,1,0:T(8,128)S(1)} %shard_map.44.refs_0_), channel_id=1, source_target_pairs={{0,2},{1,3},{2,0},{3,1},{4,6},{5,7},{6,4},{7,5},{8,10},{9,11},{10,... | collective-permute-start | bytes 24584 | tf_op jit(solution)/shard_map/ppermute | solution.py:206
  33.1 7.2 %collective-permute-start.23 = (f32[8,128]{1,0:T(8,128)S(1)}, f32[8,128]{1,0:T(8,128)S(1)}, u32[]{:S(2)}, u32[]{:S(2)}) collective-permute-start(f32[8,128]{1,0:T(8,128)S(1)} %get-tuple-element.38.square_ref), channel_id=1, source_target_pairs={{0,12},{1,13},{2,14},{3,15},{4,0},{5,1},{6,2},{7,3},{8,4},{9,5},{1... | collective-permute-start | bytes 12296 | tf_op jit(solution)/shard_map/ppermute | solution.py:206
  37.2 7.5 %collective-permute-start.22 = (f32[8,128]{1,0:T(8,128)S(1)}, f32[8,128]{1,0:T(8,128)S(1)}, u32[]{:S(2)}, u32[]{:S(2)}) collective-permute-start(f32[8,128]{1,0:T(8,128)S(1)} %get-tuple-element.38.square_ref), channel_id=1, source_target_pairs={{0,8},{1,9},{2,10},{3,11},{4,12},{5,13},{6,14},{7,15},{8,0},{9,1},... | collective-permute-start | bytes 12296 | tf_op jit(solution)/shard_map/ppermute | solution.py:206
  37.2 8.3 %collective-permute-start.21 = (f32[8,128]{1,0:T(8,128)S(1)}, f32[8,128]{1,0:T(8,128)S(1)}, u32[]{:S(2)}, u32[]{:S(2)}) collective-permute-start(f32[8,128]{1,0:T(8,128)S(1)} %get-tuple-element.38.square_ref), channel_id=1, source_target_pairs={{0,4},{1,5},{2,6},{3,7},{4,8},{5,9},{6,10},{7,11},{8,12},{9,13},{1... | collective-permute-start | bytes 12296 | tf_op jit(solution)/shard_map/ppermute | solution.py:206
  38.5 33.7 %collective-permute-start.1 = (f32[32,6,8,128]{3,2,1,0:T(8,128)S(1)}, f32[32,6,8,128]{3,2,1,0:T(8,128)S(1)}, u32[]{:S(2)}, u32[]{:S(2)}) collective-permute-start(f32[32,6,8,128]{3,2,1,0:T(8,128)S(1)} %get-tuple-element.26), channel_id=1, source_target_pairs={{0,16},{1,19},{2,18},{3,17},{4,20},{5,23},{6,22},{7,21},{8,24},{9,... | collective-permute-start | bytes 2359304 | tf_op jit(solution)/shard_map/ppermute | solution.py:206
  40.3 25.5 %collective-permute-start.4 = (f32[16,6,8,128]{3,2,1,0:T(8,128)S(1)}, f32[16,6,8,128]{3,2,1,0:T(8,128)S(1)}, u32[]{:S(2)}, u32[]{:S(2)}) collective-permute-start(f32[16,6,8,128]{3,2,1,0:T(8,128)S(1)} %get-tuple-element.29), channel_id=1, source_target_pairs={{0,17},{1,18},{2,19},{3,16},{4,21},{5,22},{6,23},{7,20},{8,25},{9,... | collective-permute-start | bytes 1179656 | tf_op jit(solution)/shard_map/ppermute | solution.py:206
  40.3 25.5 %collective-permute-start.5 = (f32[16,6,8,128]{3,2,1,0:T(8,128)S(1)}, f32[16,6,8,128]{3,2,1,0:T(8,128)S(1)}, u32[]{:S(2)}, u32[]{:S(2)}) collective-permute-start(f32[16,6,8,128]{3,2,1,0:T(8,128)S(1)} %get-tuple-element.30), channel_id=1, source_target_pairs={{0,19},{1,16},{2,17},{3,18},{4,23},{5,20},{6,21},{7,22},{8,27},{9,... | collective-permute-start | bytes 1179656 | tf_op jit(solution)/shard_map/ppermute | solution.py:206
  44.7 27.5 %collective-permute-start.2 = (f32[32,6,8,128]{3,2,1,0:T(8,128)S(1)}, f32[32,6,8,128]{3,2,1,0:T(8,128)S(1)}, u32[]{:S(2)}, u32[]{:S(2)}) collective-permute-start(f32[32,6,8,128]{3,2,1,0:T(8,128)S(1)} %get-tuple-element.27), channel_id=1, source_target_pairs={{0,18},{1,17},{2,16},{3,19},{4,22},{5,21},{6,20},{7,23},{8,26},{9,... | collective-permute-start | bytes 2359304 | tf_op jit(solution)/shard_map/ppermute | solution.py:206
  45.6 26.8 %collective-permute-start = (f32[32,6,8,128]{3,2,1,0:T(8,128)S(1)}, f32[32,6,8,128]{3,2,1,0:T(8,128)S(1)}, u32[]{:S(2)}, u32[]{:S(2)}) collective-permute-start(f32[32,6,8,128]{3,2,1,0:T(8,128)S(1)} %get-tuple-element.25.refs_0_), channel_id=1, source_target_pairs={{0,32},{1,33},{2,34},{3,35},{4,36},{5,37},{6,38},{7,39},{8,40},{9,... | collective-permute-start | bytes 2359304 | tf_op jit(solution)/shard_map/ppermute | solution.py:206
  65.8 19.7 %collective-permute-start.3 = (f32[32,6,8,128]{3,2,1,0:T(8,128)S(1)}, f32[32,6,8,128]{3,2,1,0:T(8,128)S(1)}, u32[]{:S(2)}, u32[]{:S(2)}) collective-permute-start(f32[32,6,8,128]{3,2,1,0:T(8,128)S(1)} %get-tuple-element.28.refs_0_), channel_id=1, source_target_pairs={{0,33},{1,32},{2,35},{3,34},{4,37},{5,36},{6,39},{7,38},{8,41},{9,... | collective-permute-start | bytes 2359304 | tf_op jit(solution)/shard_map/ppermute | solution.py:206
  65.8 38.6 %collective-permute-start.7 = (f32[32,6,8,128]{3,2,1,0:T(8,128)S(1)}, f32[32,6,8,128]{3,2,1,0:T(8,128)S(1)}, u32[]{:S(2)}, u32[]{:S(2)}) collective-permute-start(f32[32,6,8,128]{3,2,1,0:T(8,128)S(1)} %get-tuple-element.32), channel_id=1, source_target_pairs={{0,50},{1,49},{2,48},{3,51},{4,54},{5,53},{6,52},{7,55},{8,58},{9,... | collective-permute-start | bytes 2359304 | tf_op jit(solution)/shard_map/ppermute | solution.py:206
  72.2 45.2 %collective-permute-start.8 = (f32[32,6,8,128]{3,2,1,0:T(8,128)S(1)}, f32[32,6,8,128]{3,2,1,0:T(8,128)S(1)}, u32[]{:S(2)}, u32[]{:S(2)}) collective-permute-start(f32[32,6,8,128]{3,2,1,0:T(8,128)S(1)} %get-tuple-element.33), channel_id=1, source_target_pairs={{0,49},{1,50},{2,51},{3,48},{4,53},{5,54},{6,55},{7,52},{8,57},{9,... | collective-permute-start | bytes 2359304 | tf_op jit(solution)/shard_map/ppermute | solution.py:206
  72.2 65.0 %collective-permute-start.9 = (f32[32,6,8,128]{3,2,1,0:T(8,128)S(1)}, f32[32,6,8,128]{3,2,1,0:T(8,128)S(1)}, u32[]{:S(2)}, u32[]{:S(2)}) collective-permute-start(f32[32,6,8,128]{3,2,1,0:T(8,128)S(1)} %get-tuple-element.34), channel_id=1, source_target_pairs={{0,51},{1,48},{2,49},{3,50},{4,55},{5,52},{6,53},{7,54},{8,59},{9,... | collective-permute-start | bytes 2359304 | tf_op jit(solution)/shard_map/ppermute | solution.py:206
  72.4 71.4 %collective-permute-start.10 = (f32[32,6,8,128]{3,2,1,0:T(8,128)S(1)}, f32[32,6,8,128]{3,2,1,0:T(8,128)S(1)}, u32[]{:S(2)}, u32[]{:S(2)}) collective-permute-start(f32[32,6,8,128]{3,2,1,0:T(8,128)S(1)} %get-tuple-element.35), channel_id=1, source_target_pairs={{0,1},{1,0},{2,3},{3,2},{4,5},{5,4},{6,7},{7,6},{8,9},{9,8},{10,11... | collective-permute-start | bytes 2359304 | tf_op jit(solution)/shard_map/ppermute | solution.py:206
  85.5 70.1 %collective-permute-start.11 = (f32[32,6,8,128]{3,2,1,0:T(8,128)S(1)}, f32[32,6,8,128]{3,2,1,0:T(8,128)S(1)}, u32[]{:S(2)}, u32[]{:S(2)}) collective-permute-start(f32[32,6,8,128]{3,2,1,0:T(8,128)S(1)} %get-tuple-element.36), channel_id=1, source_target_pairs={{0,34},{1,35},{2,32},{3,33},{4,38},{5,39},{6,36},{7,37},{8,42},{9,... | collective-permute-start | bytes 2359304 | tf_op jit(solution)/shard_map/ppermute | solution.py:206
  104.4 70.5 %collective-permute-start.6 = (f32[32,6,8,128]{3,2,1,0:T(8,128)S(1)}, f32[32,6,8,128]{3,2,1,0:T(8,128)S(1)}, u32[]{:S(2)}, u32[]{:S(2)}) collective-permute-start(f32[32,6,8,128]{3,2,1,0:T(8,128)S(1)} %get-tuple-element.31._), channel_id=1, source_target_pairs={{0,48},{1,51},{2,50},{3,49},{4,52},{5,55},{6,54},{7,53},{8,56},{9,... | collective-permute-start | bytes 2359304 | tf_op jit(solution)/shard_map/ppermute | solution.py:206
  117.4 97.9 %collective-permute-start.26 = (f32[32,6,8,128]{3,2,1,0:T(8,128)S(1)}, f32[32,6,8,128]{3,2,1,0:T(8,128)S(1)}, u32[]{:S(2)}, u32[]{:S(2)}) collective-permute-start(f32[32,6,8,128]{3,2,1,0:T(8,128)S(1)} %get-tuple-element.41), channel_id=1, source_target_pairs={{0,2},{1,3},{2,0},{3,1},{4,6},{5,7},{6,4},{7,5},{8,10},{9,11},{10,... | collective-permute-start | bytes 2359304 | tf_op jit(solution)/shard_map/ppermute | solution.py:206
  137.2 78.1 %collective-permute-start.27 = (f32[32,6,8,128]{3,2,1,0:T(8,128)S(1)}, f32[32,6,8,128]{3,2,1,0:T(8,128)S(1)}, u32[]{:S(2)}, u32[]{:S(2)}) collective-permute-start(f32[32,6,8,128]{3,2,1,0:T(8,128)S(1)} %get-tuple-element.42), channel_id=1, source_target_pairs={{0,3},{1,2},{2,1},{3,0},{4,7},{5,6},{6,5},{7,4},{8,11},{9,10},{10,... | collective-permute-start | bytes 2359304 | tf_op jit(solution)/shard_map/ppermute | solution.py:206
  143.8 71.5 %collective-permute-start.28 = (f32[32,6,8,128]{3,2,1,0:T(8,128)S(1)}, f32[32,6,8,128]{3,2,1,0:T(8,128)S(1)}, u32[]{:S(2)}, u32[]{:S(2)}) collective-permute-start(f32[32,6,8,128]{3,2,1,0:T(8,128)S(1)} %get-tuple-element.43), channel_id=1, source_target_pairs={{0,35},{1,34},{2,33},{3,32},{4,39},{5,38},{6,37},{7,36},{8,43},{9,... | collective-permute-start | bytes 2359304 | tf_op jit(solution)/shard_map/ppermute | solution.py:206
  155.6 58.2 %collective-permute-start.24 = (f32[16,6,8,128]{3,2,1,0:T(8,128)S(1)}, f32[16,6,8,128]{3,2,1,0:T(8,128)S(1)}, u32[]{:S(2)}, u32[]{:S(2)}) collective-permute-start(f32[16,6,8,128]{3,2,1,0:T(8,128)S(1)} %get-tuple-element.39), channel_id=1, source_target_pairs={{0,17},{1,18},{2,19},{3,16},{4,21},{5,22},{6,23},{7,20},{8,25},{9,... | collective-permute-start | bytes 1179656 | tf_op jit(solution)/shard_map/ppermute | solution.py:206
  174.8 40.5 %collective-permute-start.25 = (f32[16,6,8,128]{3,2,1,0:T(8,128)S(1)}, f32[16,6,8,128]{3,2,1,0:T(8,128)S(1)}, u32[]{:S(2)}, u32[]{:S(2)}) collective-permute-start(f32[16,6,8,128]{3,2,1,0:T(8,128)S(1)} %get-tuple-element.40), channel_id=1, source_target_pairs={{0,19},{1,16},{2,17},{3,18},{4,23},{5,20},{6,21},{7,22},{8,27},{9,... | collective-permute-start | bytes 1179656 | tf_op jit(solution)/shard_map/ppermute | solution.py:206
  (5 other events, 18.8 us)

commit v3 on v2

--- a/solution.py
+++ b/solution.py
@@ -14,14 +14,13 @@
 HALVES, ROW_PARTS, TILES, E, COL_PARTS = 2, 4, 16, 6, 4
 F32 = jnp.float32
 WHOLE, UPPER, LOWER = (0, 1), (0,), (1,)
-FIRST = [(1, 0, 0, WHOLE), (0, 1, 0, WHOLE), (0, 3, 0, WHOLE)]
-SECOND = [(1, 0, 1, WHOLE), (0, 1, 1, UPPER), (0, 3, 1, UPPER)]
+FIRST = [(1, 0, 0, WHOLE), (0, 1, 0, WHOLE)]
+SECOND = [(0, 3, 0, WHOLE), (1, 0, 1, WHOLE), (0, 1, 1, UPPER), (0, 3, 1, UPPER)]
 THIRD = [(1, 1, 0, WHOLE), (0, 1, 1, LOWER), (0, 3, 1, LOWER), (0, 2, 0, WHOLE), (0, 2, 1, WHOLE), (1, 3, 0, WHOLE),
          (1, 1, 1, WHOLE), (1, 3, 1, WHOLE), (0, 0, 1, WHOLE), (1, 2, 0, WHOLE), (1, 2, 1, WHOLE)]
 NEAR = [(0, 1, 0), (0, 3, 0), (0, 2, 0), (1, 0, 0), (1, 1, 0), (1, 3, 0), (1, 2, 0)]
-LATE = [(0, 1, 1, LOWER), (0, 3, 1, LOWER), (0, 2, 0, WHOLE), (0, 2, 1, WHOLE), (1, 2, 1, WHOLE)]
-MIDDLE = [(1, 2, 0, WHOLE)]
-SOON = [f for f in FIRST + SECOND + THIRD if f not in LATE + MIDDLE]
+GROUPS = [[(1, 2, 0, WHOLE)], [(0, 1, 1, LOWER), (0, 3, 1, LOWER), (0, 2, 0, WHOLE)], [(0, 2, 1, WHOLE), (1, 2, 1, WHOLE)]]
+SOON = [f for f in FIRST + SECOND + THIRD if f not in sum(GROUPS, [])]
 SLOTS = 4
 CHUNKS = HALVES * 8
 VMEM = pl.BlockSpec(memory_space=pltpu.VMEM)
@@ -158,10 +157,9 @@
         copy.wait()
 
 
-def write_middle(_, *refs):
-    n = len(MIDDLE)
-    pieces, (out_ref, sem) = refs[:n], refs[n:]
-    for copy in write(here(), MIDDLE, pieces, out_ref, sem):
+def write_group(flows, _, *refs):
+    pieces, (out_ref, sem) = refs[:len(flows)], refs[len(flows):]
+    for copy in write(here(), flows, pieces, out_ref, sem):
         copy.wait()
 
 
@@ -172,18 +170,13 @@
     square_ref[...] = jnp.broadcast_to(whole[0, E] + whole[1, E] + whole[2, E] + whole[3, E], SMALL)
 
 
-def write_late(_, sums_ref, square_ref, z1, z2, z3, *refs):
-    n = len(LATE)
-    pieces, (out_ref, columns_ref, norm_ref, squares, sem) = refs[:n], refs[n:]
-    at = here()
-    copies = write(at, LATE, pieces, out_ref, sem)
+def finish(sums_ref, square_ref, z1, z2, z3, columns_ref, norm_ref, squares):
+    z = lax.axis_index("col") // 4
     columns_ref[...] = sums_ref[...]
     for dz, ref in enumerate((square_ref, z1, z2, z3)):
-        squares[(at["z"] - dz + 4) % 4] = ref[...]
+        squares[(z - dz + 4) % 4] = ref[...]
     total = jnp.sum((squares[0] + squares[1] + squares[2] + squares[3])[0:1, :])
     norm_ref[0, 0] = jnp.max(jnp.sqrt(jnp.full(SMALL, total / (ROWS * COLS), F32)))
-    for copy in copies:
-        copy.wait()
 
 
 FLOPS_PER_US = 10_000_000
@@ -235,18 +228,14 @@
         write_soon, jax.ShapeDtypeStruct(BIG, F32), [HBM] + [VMEM] * n, HBM,
         [pltpu.VMEM((HALVES, TILES, E, 8, 128), F32), dma((2,)), dma((HALVES, n))], 5,
     )(x, *[landed[f] for f in SOON])
-    n = len(MIDDLE)
-    out = plain(
-        write_middle, jax.ShapeDtypeStruct(BIG, F32), [HBM] + [VMEM] * n, HBM,
-        [dma((HALVES, n))], 2, input_output_aliases={0: 0})(out, *[landed[f] for f in MIDDLE])
-    n = len(LATE)
-    out, columns, norm = plain(
-        write_late,
-        (jax.ShapeDtypeStruct(BIG, F32), jax.ShapeDtypeStruct((E * COL_PARTS, 128), F32),
-         jax.ShapeDtypeStruct((1, 1), F32)),
-        [HBM] + [VMEM] * (n + 5), (HBM, VMEM, pl.BlockSpec(memory_space=pltpu.SMEM)),
-        [pltpu.VMEM((4, *SMALL), F32), dma((HALVES, n))], 2, input_output_aliases={0: 0},
-    )(out, sums, square, *stacked, *[landed[f] for f in LATE])
+    columns, norm = plain(
+        finish, (jax.ShapeDtypeStruct((E * COL_PARTS, 128), F32), jax.ShapeDtypeStruct((1, 1), F32)),
+        [VMEM] * 5, (VMEM, pl.BlockSpec(memory_space=pltpu.SMEM)), [tiles((4, *SMALL))], 1)(sums, square, *stacked)
+    for flows in GROUPS:
+        n = len(flows)
+        out = plain(
+            functools.partial(write_group, flows), jax.ShapeDtypeStruct(BIG, F32), [HBM] + [VMEM] * n, HBM,
+            [dma((HALVES, n))], 1, input_output_aliases={0: 0})(out, *[landed[f] for f in flows])
     return out.transpose(0, 1, 2, 5, 3, 4, 6).reshape(1024, 3072), columns.reshape(3072), norm.reshape(())
 
 

time: 222 us -> 214 us (0.964)
  starting transfers between devices: 52.1 us -> 46.6 us
    ppermute x29, starting transfers between devices: 52.1 us -> 46.6 us  [permute(): return lax.ppermute(value, AXES, pairs)]
  transfers between devices with their start and end apart: 29 -> 29, of which waited for: 14 -> 14; matrix products, arithmetic and copies ran while one was open for 0% -> 0% of each run, Pallas kernels for 2% -> 3%
where the time goes in v3:
time: 214 us; the launch traced here: 211 us
  waiting for transfers between devices  143 us (67%)
  starting transfers between devices  46.6 us (22%)
  Pallas kernels  20.8 us (10%)
    ppermute x29, waiting for transfers between devices, permute(): return lax.ppermute(value, AXES, pairs)  143 us
    ppermute x29, starting transfers between devices, permute(): return lax.ppermute(value, AXES, pairs)  46.6 us
    pallas_call x3, Pallas kernels, go(): plain(functools.partial(pack, flows), tuple((pltpu.VMEM((len(f[3]) * TILE...  6.61 us
    pallas_call x1, Pallas kernels, body(): plain(reduce, tiles((2, *SMALL)), [HBM, VMEM], VMEM, [pltpu.VMEM((SLOTS,...  6.5 us
  transfers between devices with their start and end apart: 29, of which 14 were waited for; matrix products, arithmetic and copies ran while one was open for 0% of the time, Pallas kernels for 3%

profile of v3, /device:TPU:8, one launch (start us, length us, event | category | flops | bytes accessed | tf_op | source)
XLA Modules:
  0.0 211.3 jit_solution(129664136586085114)
XLA Ops:
  3.8 3.5 %shard_map.40 = (f32[32,6,8,128]{3,2,1,0:T(8,128)S(1)}, f32[16,6,8,128]{3,2,1,0:T(8,128)S(1)}, f32[16,6,8,128]{3,2,1,0:T(8,128)S(1)}, f32[32,6,8,128]{3,2,1,0:T(...) custom-call(f32[2,8,16,6,2,8,128]{6,5,4,3,2,1,0:T(8,128)} %bitcast.1, ...), custom_call_target="tpu_custom_call" | custom-call | flops 46666664 | bytes 1048576 | tf_op jit(solution)/shard_map/pallas_call | solution.py:203
  7.3 6.5 %shard_map.45.part = f32[2,8,128]{2,1,0:T(8,128)S(1)} custom-call(f32[2,8,16,6,2,8,128]{6,5,4,3,2,1,0:T(8,128)} %bitcast.11, f32[32,6,8,128]{3,2,1,0:T(8,128)S(1)} %get-tuple-element.30._), custom_call_target="tpu_custom_call" | custom-call | flops 70000000 | bytes 1048576 | tf_op jit(solution)/shard_map/pallas_call | solution.py:214
  15.0 3.3 %collective-permute-start.24 = (f32[2,8,128]{2,1,0:T(8,128)S(1)}, f32[2,8,128]{2,1,0:T(8,128)S(1)}, u32[]{:S(2)}, u32[]{:S(2)}) collective-permute-start(f32[2,8,128]{2,1,0:T(8,128)S(1)} %shard_map.46.refs_0_), channel_id=1, source_target_pairs={{0,34},{1,35},{2,32},{3,33},{4,38},{5,39},{6,36},{7,37},{8,42},{9,... | collective-permute-start | bytes 24584 | tf_op jit(solution)/shard_map/ppermute | solution.py:199
  21.7 2.4 %collective-permute-start.20 = (f32[2,8,128]{2,1,0:T(8,128)S(1)}, f32[2,8,128]{2,1,0:T(8,128)S(1)}, u32[]{:S(2)}, u32[]{:S(2)}) collective-permute-start(f32[2,8,128]{2,1,0:T(8,128)S(1)} %shard_map.46.refs_0_), channel_id=1, source_target_pairs={{0,2},{1,3},{2,0},{3,1},{4,6},{5,7},{6,4},{7,5},{8,10},{9,11},{10,... | collective-permute-start | bytes 24584 | tf_op jit(solution)/shard_map/ppermute | solution.py:199
  24.2 2.0 collective-permute-start.18
  28.1 2.9 %collective-permute-start.25 = (f32[4,8,128]{2,1,0:T(8,128)S(1)}, f32[4,8,128]{2,1,0:T(8,128)S(1)}, u32[]{:S(2)}, u32[]{:S(2)}) collective-permute-start(f32[4,8,128]{2,1,0:T(8,128)S(1)} %shard_map.47.plane_ref), channel_id=1, source_target_pairs={{0,96},{1,97},{2,98},{3,99},{4,100},{5,101},{6,102},{7,103},{8,104... | collective-permute-start | bytes 49160 | tf_op jit(solution)/shard_map/ppermute | solution.py:199
  31.0 2.1 %collective-permute-done.25.other_ref = f32[4,8,128]{2,1,0:T(8,128)S(1)} collective-permute-done((f32[4,8,128]{2,1,0:T(8,128)S(1)}, f32[4,8,128]{2,1,0:T(8,128)S(1)}, u32[]{:S(2)}, u32[]{:S(2)}) %collective-permute-start.25) | collective-permute-done | bytes 16416 | tf_op jit(solution)/shard_map/ppermute | solution.py:199
  33.1 4.1 %collective-permute-start.28 = (f32[8,128]{1,0:T(8,128)S(1)}, f32[8,128]{1,0:T(8,128)S(1)}, u32[]{:S(2)}, u32[]{:S(2)}) collective-permute-start(f32[8,128]{1,0:T(8,128)S(1)} %get-tuple-element.42.square_ref), channel_id=1, source_target_pairs={{0,12},{1,13},{2,14},{3,15},{4,0},{5,1},{6,2},{7,3},{8,4},{9,5},{1... | collective-permute-start | bytes 12296 | tf_op jit(solution)/shard_map/ppermute | solution.py:199
  38.5 3.0 %collective-permute-start.5 = (f32[16,6,8,128]{3,2,1,0:T(8,128)S(1)}, f32[16,6,8,128]{3,2,1,0:T(8,128)S(1)}, u32[]{:S(2)}, u32[]{:S(2)}) collective-permute-start(f32[16,6,8,128]{3,2,1,0:T(8,128)S(1)} %get-tuple-element.29), channel_id=1, source_target_pairs={{0,19},{1,16},{2,17},{3,18},{4,23},{5,20},{6,21},{7,22},{8,27},{9,... | collective-permute-start | bytes 1179656 | tf_op jit(solution)/shard_map/ppermute | solution.py:199
  41.5 2.0 collective-permute-start.1
  43.8 2.5 %collective-permute-done.4.refs_4_ = f32[16,6,8,128]{3,2,1,0:T(8,128)S(1)} collective-permute-done((f32[16,6,8,128]{3,2,1,0:T(8,128)S(1)}, f32[16,6,8,128]{3,2,1,0:T(8,128)S(1)}, u32[]{:S(2)}, u32[]{:S(2)}) %collective-permute-start.4) | collective-permute-done | bytes 393248 | tf_op jit(solution)/shard_map/ppermute | solution.py:199
  46.4 6.4 %collective-permute-start.2 = (f32[32,6,8,128]{3,2,1,0:T(8,128)S(1)}, f32[32,6,8,128]{3,2,1,0:T(8,128)S(1)}, u32[]{:S(2)}, u32[]{:S(2)}) collective-permute-start(f32[32,6,8,128]{3,2,1,0:T(8,128)S(1)} %get-tuple-element.26.refs_0_), channel_id=1, source_target_pairs={{0,18},{1,17},{2,16},{3,19},{4,22},{5,21},{6,20},{7,23},{8,26},{9,... | collective-permute-start | bytes 2359304 | tf_op jit(solution)/shard_map/ppermute | solution.py:199
  54.1 11.2 %collective-permute-done.1.refs_1_ = f32[32,6,8,128]{3,2,1,0:T(8,128)S(1)} collective-permute-done((f32[32,6,8,128]{3,2,1,0:T(8,128)S(1)}, f32[32,6,8,128]{3,2,1,0:T(8,128)S(1)}, u32[]{:S(2)}, u32[]{:S(2)}) %collective-permute-start.1) | collective-permute-done | bytes 786464 | tf_op jit(solution)/shard_map/ppermute | solution.py:199
  65.3 2.6 %collective-permute-start.9 = (f32[32,6,8,128]{3,2,1,0:T(8,128)S(1)}, f32[32,6,8,128]{3,2,1,0:T(8,128)S(1)}, u32[]{:S(2)}, u32[]{:S(2)}) collective-permute-start(f32[32,6,8,128]{3,2,1,0:T(8,128)S(1)} %get-tuple-element.33), channel_id=1, source_target_pairs={{0,51},{1,48},{2,49},{3,50},{4,55},{5,52},{6,53},{7,54},{8,59},{9,... | collective-permute-start | bytes 2359304 | tf_op jit(solution)/shard_map/ppermute | solution.py:199
  67.9 10.7 %collective-permute-done.3.refs_3_ = f32[32,6,8,128]{3,2,1,0:T(8,128)S(1)} collective-permute-done((f32[32,6,8,128]{3,2,1,0:T(8,128)S(1)}, f32[32,6,8,128]{3,2,1,0:T(8,128)S(1)}, u32[]{:S(2)}, u32[]{:S(2)}) %collective-permute-start.3) | collective-permute-done | bytes 786464 | tf_op jit(solution)/shard_map/ppermute | solution.py:199
  81.5 16.2 %collective-permute-done.7.refs_7_ = f32[32,6,8,128]{3,2,1,0:T(8,128)S(1)} collective-permute-done((f32[32,6,8,128]{3,2,1,0:T(8,128)S(1)}, f32[32,6,8,128]{3,2,1,0:T(8,128)S(1)}, u32[]{:S(2)}, u32[]{:S(2)}) %collective-permute-start.7) | collective-permute-done | bytes 786464 | tf_op jit(solution)/shard_map/ppermute | solution.py:199
  98.5 13.8 %collective-permute-done.8.refs_8_ = f32[32,6,8,128]{3,2,1,0:T(8,128)S(1)} collective-permute-done((f32[32,6,8,128]{3,2,1,0:T(8,128)S(1)}, f32[32,6,8,128]{3,2,1,0:T(8,128)S(1)}, u32[]{:S(2)}, u32[]{:S(2)}) %collective-permute-start.8) | collective-permute-done | bytes 786464 | tf_op jit(solution)/shard_map/ppermute | solution.py:199
  112.3 2.3 %collective-permute-start.14 = (f32[32,6,8,128]{3,2,1,0:T(8,128)S(1)}, f32[32,6,8,128]{3,2,1,0:T(8,128)S(1)}, u32[]{:S(2)}, u32[]{:S(2)}) collective-permute-start(f32[32,6,8,128]{3,2,1,0:T(8,128)S(1)} %get-tuple-element.38), channel_id=1, source_target_pairs={{0,2},{1,3},{2,0},{3,1},{4,6},{5,7},{6,4},{7,5},{8,10},{9,11},{10,... | collective-permute-start | bytes 2359304 | tf_op jit(solution)/shard_map/ppermute | solution.py:199
  114.6 14.8 %collective-permute-done.9.refs_9_ = f32[32,6,8,128]{3,2,1,0:T(8,128)S(1)} collective-permute-done((f32[32,6,8,128]{3,2,1,0:T(8,128)S(1)}, f32[32,6,8,128]{3,2,1,0:T(8,128)S(1)}, u32[]{:S(2)}, u32[]{:S(2)}) %collective-permute-start.9) | collective-permute-done | bytes 786464 | tf_op jit(solution)/shard_map/ppermute | solution.py:199
  129.4 5.3 %collective-permute-start.15 = (f32[32,6,8,128]{3,2,1,0:T(8,128)S(1)}, f32[32,6,8,128]{3,2,1,0:T(8,128)S(1)}, u32[]{:S(2)}, u32[]{:S(2)}) collective-permute-start(f32[32,6,8,128]{3,2,1,0:T(8,128)S(1)} %get-tuple-element.39), channel_id=1, source_target_pairs={{0,3},{1,2},{2,1},{3,0},{4,7},{5,6},{6,5},{7,4},{8,11},{9,10},{10,... | collective-permute-start | bytes 2359304 | tf_op jit(solution)/shard_map/ppermute | solution.py:199
  134.7 14.4 %collective-permute-done.11.refs_0_ = f32[32,6,8,128]{3,2,1,0:T(8,128)S(1)} collective-permute-done((f32[32,6,8,128]{3,2,1,0:T(8,128)S(1)}, f32[32,6,8,128]{3,2,1,0:T(8,128)S(1)}, u32[]{:S(2)}, u32[]{:S(2)}) %collective-permute-start.11) | collective-permute-done | bytes 786464 | tf_op jit(solution)/shard_map/ppermute | solution.py:199
  149.1 17.5 %collective-permute-done.6.refs_6_ = f32[32,6,8,128]{3,2,1,0:T(8,128)S(1)} collective-permute-done((f32[32,6,8,128]{3,2,1,0:T(8,128)S(1)}, f32[32,6,8,128]{3,2,1,0:T(8,128)S(1)}, u32[]{:S(2)}, u32[]{:S(2)}) %collective-permute-start.6) | collective-permute-done | bytes 786464 | tf_op jit(solution)/shard_map/ppermute | solution.py:199
  167.3 3.6 %shard_map.41._ = f32[2,4,16,6,4,8,128]{6,5,4,3,2,1,0:T(8,128)} custom-call(f32[2,8,16,6,2,8,128]{6,5,4,3,2,1,0:T(8,128)} %bitcast.12, f32[32,6,8,128]{3,2,1,0:T(8,128)S(1)} %collective-permute-done.refs_0_, f32[32,6,8,128]{3,2,1,0:T(8,128)S(1)} %collective-permute-done.1.refs_1_, f32[32,6,8,128]{3,2,1,0:T(8,128)S(1)} %collective-permute-done.2.refs_2_, ...), custom_call_target="tpu_custom_call" | custom-call | flops 50000000 | bytes 1048576 | tf_op jit(solution)/shard_map/pallas_call | solution.py:227
  171.9 37.0 %collective-permute-done.12.refs_0_ = f32[16,6,8,128]{3,2,1,0:T(8,128)S(1)} collective-permute-done((f32[16,6,8,128]{3,2,1,0:T(8,128)S(1)}, f32[16,6,8,128]{3,2,1,0:T(8,128)S(1)}, u32[]{:S(2)}, u32[]{:S(2)}) %collective-permute-start.12) | collective-permute-done | bytes 393248 | tf_op jit(solution)/shard_map/ppermute | solution.py:199
  (46 shorter events, 20.4 us)
Async XLA Ops:
  15.0 9.1 %collective-permute-start.24 = (f32[2,8,128]{2,1,0:T(8,128)S(1)}, f32[2,8,128]{2,1,0:T(8,128)S(1)}, u32[]{:S(2)}, u32[]{:S(2)}) collective-permute-start(f32[2,8,128]{2,1,0:T(8,128)S(1)} %shard_map.46.refs_0_), channel_id=1, source_target_pairs={{0,34},{1,35},{2,32},{3,33},{4,38},{5,39},{6,36},{7,37},{8,42},{9,... | collective-permute-start | bytes 24584 | tf_op jit(solution)/shard_map/ppermute | solution.py:199
  18.3 5.9 %collective-permute-start.23 = (f32[2,8,128]{2,1,0:T(8,128)S(1)}, f32[2,8,128]{2,1,0:T(8,128)S(1)}, u32[]{:S(2)}, u32[]{:S(2)}) collective-permute-start(f32[2,8,128]{2,1,0:T(8,128)S(1)} %shard_map.46.refs_0_), channel_id=1, source_target_pairs={{0,50},{1,49},{2,48},{3,51},{4,54},{5,53},{6,52},{7,55},{8,58},{9,... | collective-permute-start | bytes 24584 | tf_op jit(solution)/shard_map/ppermute | solution.py:199
  19.6 6.6 %collective-permute-start.22 = (f32[2,8,128]{2,1,0:T(8,128)S(1)}, f32[2,8,128]{2,1,0:T(8,128)S(1)}, u32[]{:S(2)}, u32[]{:S(2)}) collective-permute-start(f32[2,8,128]{2,1,0:T(8,128)S(1)} %shard_map.46.refs_0_), channel_id=1, source_target_pairs={{0,48},{1,51},{2,50},{3,49},{4,52},{5,55},{6,54},{7,53},{8,56},{9,... | collective-permute-start | bytes 24584 | tf_op jit(solution)/shard_map/ppermute | solution.py:199
  21.7 5.2 %collective-permute-start.20 = (f32[2,8,128]{2,1,0:T(8,128)S(1)}, f32[2,8,128]{2,1,0:T(8,128)S(1)}, u32[]{:S(2)}, u32[]{:S(2)}) collective-permute-start(f32[2,8,128]{2,1,0:T(8,128)S(1)} %shard_map.46.refs_0_), channel_id=1, source_target_pairs={{0,2},{1,3},{2,0},{3,1},{4,6},{5,7},{6,4},{7,5},{8,10},{9,11},{10,... | collective-permute-start | bytes 24584 | tf_op jit(solution)/shard_map/ppermute | solution.py:199
  33.1 8.3 %collective-permute-start.28 = (f32[8,128]{1,0:T(8,128)S(1)}, f32[8,128]{1,0:T(8,128)S(1)}, u32[]{:S(2)}, u32[]{:S(2)}) collective-permute-start(f32[8,128]{1,0:T(8,128)S(1)} %get-tuple-element.42.square_ref), channel_id=1, source_target_pairs={{0,12},{1,13},{2,14},{3,15},{4,0},{5,1},{6,2},{7,3},{8,4},{9,5},{1... | collective-permute-start | bytes 12296 | tf_op jit(solution)/shard_map/ppermute | solution.py:199
  37.2 6.2 %collective-permute-start.27 = (f32[8,128]{1,0:T(8,128)S(1)}, f32[8,128]{1,0:T(8,128)S(1)}, u32[]{:S(2)}, u32[]{:S(2)}) collective-permute-start(f32[8,128]{1,0:T(8,128)S(1)} %get-tuple-element.42.square_ref), channel_id=1, source_target_pairs={{0,8},{1,9},{2,10},{3,11},{4,12},{5,13},{6,14},{7,15},{8,0},{9,1},... | collective-permute-start | bytes 12296 | tf_op jit(solution)/shard_map/ppermute | solution.py:199
  37.2 6.6 %collective-permute-start.26 = (f32[8,128]{1,0:T(8,128)S(1)}, f32[8,128]{1,0:T(8,128)S(1)}, u32[]{:S(2)}, u32[]{:S(2)}) collective-permute-start(f32[8,128]{1,0:T(8,128)S(1)} %get-tuple-element.42.square_ref), channel_id=1, source_target_pairs={{0,4},{1,5},{2,6},{3,7},{4,8},{5,9},{6,10},{7,11},{8,12},{9,13},{1... | collective-permute-start | bytes 12296 | tf_op jit(solution)/shard_map/ppermute | solution.py:199
  38.5 7.9 %collective-permute-start.4 = (f32[16,6,8,128]{3,2,1,0:T(8,128)S(1)}, f32[16,6,8,128]{3,2,1,0:T(8,128)S(1)}, u32[]{:S(2)}, u32[]{:S(2)}) collective-permute-start(f32[16,6,8,128]{3,2,1,0:T(8,128)S(1)} %get-tuple-element.28), channel_id=1, source_target_pairs={{0,17},{1,18},{2,19},{3,16},{4,21},{5,22},{6,23},{7,20},{8,25},{9,... | collective-permute-start | bytes 1179656 | tf_op jit(solution)/shard_map/ppermute | solution.py:199
  38.5 14.3 %collective-permute-start.5 = (f32[16,6,8,128]{3,2,1,0:T(8,128)S(1)}, f32[16,6,8,128]{3,2,1,0:T(8,128)S(1)}, u32[]{:S(2)}, u32[]{:S(2)}) collective-permute-start(f32[16,6,8,128]{3,2,1,0:T(8,128)S(1)} %get-tuple-element.29), channel_id=1, source_target_pairs={{0,19},{1,16},{2,17},{3,18},{4,23},{5,20},{6,21},{7,22},{8,27},{9,... | collective-permute-start | bytes 1179656 | tf_op jit(solution)/shard_map/ppermute | solution.py:199
  41.5 23.8 %collective-permute-start.1 = (f32[32,6,8,128]{3,2,1,0:T(8,128)S(1)}, f32[32,6,8,128]{3,2,1,0:T(8,128)S(1)}, u32[]{:S(2)}, u32[]{:S(2)}) collective-permute-start(f32[32,6,8,128]{3,2,1,0:T(8,128)S(1)} %get-tuple-element.25), channel_id=1, source_target_pairs={{0,16},{1,19},{2,18},{3,17},{4,20},{5,23},{6,22},{7,21},{8,24},{9,... | collective-permute-start | bytes 2359304 | tf_op jit(solution)/shard_map/ppermute | solution.py:199
  43.5 21.8 %collective-permute-start = (f32[32,6,8,128]{3,2,1,0:T(8,128)S(1)}, f32[32,6,8,128]{3,2,1,0:T(8,128)S(1)}, u32[]{:S(2)}, u32[]{:S(2)}) collective-permute-start(f32[32,6,8,128]{3,2,1,0:T(8,128)S(1)} %get-tuple-element.24.refs_0_), channel_id=1, source_target_pairs={{0,32},{1,33},{2,34},{3,35},{4,36},{5,37},{6,38},{7,39},{8,40},{9,... | collective-permute-start | bytes 2359304 | tf_op jit(solution)/shard_map/ppermute | solution.py:199
  43.8 34.8 %collective-permute-start.3 = (f32[32,6,8,128]{3,2,1,0:T(8,128)S(1)}, f32[32,6,8,128]{3,2,1,0:T(8,128)S(1)}, u32[]{:S(2)}, u32[]{:S(2)}) collective-permute-start(f32[32,6,8,128]{3,2,1,0:T(8,128)S(1)} %get-tuple-element.27), channel_id=1, source_target_pairs={{0,33},{1,32},{2,35},{3,34},{4,37},{5,36},{6,39},{7,38},{8,41},{9,... | collective-permute-start | bytes 2359304 | tf_op jit(solution)/shard_map/ppermute | solution.py:199
  46.4 34.2 %collective-permute-start.2 = (f32[32,6,8,128]{3,2,1,0:T(8,128)S(1)}, f32[32,6,8,128]{3,2,1,0:T(8,128)S(1)}, u32[]{:S(2)}, u32[]{:S(2)}) collective-permute-start(f32[32,6,8,128]{3,2,1,0:T(8,128)S(1)} %get-tuple-element.26.refs_0_), channel_id=1, source_target_pairs={{0,18},{1,17},{2,16},{3,19},{4,22},{5,21},{6,20},{7,23},{8,26},{9,... | collective-permute-start | bytes 2359304 | tf_op jit(solution)/shard_map/ppermute | solution.py:199
  52.8 44.9 %collective-permute-start.7 = (f32[32,6,8,128]{3,2,1,0:T(8,128)S(1)}, f32[32,6,8,128]{3,2,1,0:T(8,128)S(1)}, u32[]{:S(2)}, u32[]{:S(2)}) collective-permute-start(f32[32,6,8,128]{3,2,1,0:T(8,128)S(1)} %get-tuple-element.31), channel_id=1, source_target_pairs={{0,50},{1,49},{2,48},{3,51},{4,54},{5,53},{6,52},{7,55},{8,58},{9,... | collective-permute-start | bytes 2359304 | tf_op jit(solution)/shard_map/ppermute | solution.py:199
  65.3 47.0 %collective-permute-start.8 = (f32[32,6,8,128]{3,2,1,0:T(8,128)S(1)}, f32[32,6,8,128]{3,2,1,0:T(8,128)S(1)}, u32[]{:S(2)}, u32[]{:S(2)}) collective-permute-start(f32[32,6,8,128]{3,2,1,0:T(8,128)S(1)} %get-tuple-element.32), channel_id=1, source_target_pairs={{0,49},{1,50},{2,51},{3,48},{4,53},{5,54},{6,55},{7,52},{8,57},{9,... | collective-permute-start | bytes 2359304 | tf_op jit(solution)/shard_map/ppermute | solution.py:199
  65.3 64.1 %collective-permute-start.9 = (f32[32,6,8,128]{3,2,1,0:T(8,128)S(1)}, f32[32,6,8,128]{3,2,1,0:T(8,128)S(1)}, u32[]{:S(2)}, u32[]{:S(2)}) collective-permute-start(f32[32,6,8,128]{3,2,1,0:T(8,128)S(1)} %get-tuple-element.33), channel_id=1, source_target_pairs={{0,51},{1,48},{2,49},{3,50},{4,55},{5,52},{6,53},{7,54},{8,59},{9,... | collective-permute-start | bytes 2359304 | tf_op jit(solution)/shard_map/ppermute | solution.py:199
  78.6 56.1 %collective-permute-start.10 = (f32[32,6,8,128]{3,2,1,0:T(8,128)S(1)}, f32[32,6,8,128]{3,2,1,0:T(8,128)S(1)}, u32[]{:S(2)}, u32[]{:S(2)}) collective-permute-start(f32[32,6,8,128]{3,2,1,0:T(8,128)S(1)} %get-tuple-element.34), channel_id=1, source_target_pairs={{0,1},{1,0},{2,3},{3,2},{4,5},{5,4},{6,7},{7,6},{8,9},{9,8},{10,11... | collective-permute-start | bytes 2359304 | tf_op jit(solution)/shard_map/ppermute | solution.py:199
  80.6 68.5 %collective-permute-start.11 = (f32[32,6,8,128]{3,2,1,0:T(8,128)S(1)}, f32[32,6,8,128]{3,2,1,0:T(8,128)S(1)}, u32[]{:S(2)}, u32[]{:S(2)}) collective-permute-start(f32[32,6,8,128]{3,2,1,0:T(8,128)S(1)} %get-tuple-element.35), channel_id=1, source_target_pairs={{0,34},{1,35},{2,32},{3,33},{4,38},{5,39},{6,36},{7,37},{8,42},{9,... | collective-permute-start | bytes 2359304 | tf_op jit(solution)/shard_map/ppermute | solution.py:199
  97.7 68.9 %collective-permute-start.6 = (f32[32,6,8,128]{3,2,1,0:T(8,128)S(1)}, f32[32,6,8,128]{3,2,1,0:T(8,128)S(1)}, u32[]{:S(2)}, u32[]{:S(2)}) collective-permute-start(f32[32,6,8,128]{3,2,1,0:T(8,128)S(1)} %get-tuple-element.30._), channel_id=1, source_target_pairs={{0,48},{1,51},{2,50},{3,49},{4,52},{5,55},{6,54},{7,53},{8,56},{9,... | collective-permute-start | bytes 2359304 | tf_op jit(solution)/shard_map/ppermute | solution.py:199
  112.3 96.5 %collective-permute-start.14 = (f32[32,6,8,128]{3,2,1,0:T(8,128)S(1)}, f32[32,6,8,128]{3,2,1,0:T(8,128)S(1)}, u32[]{:S(2)}, u32[]{:S(2)}) collective-permute-start(f32[32,6,8,128]{3,2,1,0:T(8,128)S(1)} %get-tuple-element.38), channel_id=1, source_target_pairs={{0,2},{1,3},{2,0},{3,1},{4,6},{5,7},{6,4},{7,5},{8,10},{9,11},{10,... | collective-permute-start | bytes 2359304 | tf_op jit(solution)/shard_map/ppermute | solution.py:199
  129.4 80.7 %collective-permute-start.15 = (f32[32,6,8,128]{3,2,1,0:T(8,128)S(1)}, f32[32,6,8,128]{3,2,1,0:T(8,128)S(1)}, u32[]{:S(2)}, u32[]{:S(2)}) collective-permute-start(f32[32,6,8,128]{3,2,1,0:T(8,128)S(1)} %get-tuple-element.39), channel_id=1, source_target_pairs={{0,3},{1,2},{2,1},{3,0},{4,7},{5,6},{6,5},{7,4},{8,11},{9,10},{10,... | collective-permute-start | bytes 2359304 | tf_op jit(solution)/shard_map/ppermute | solution.py:199
  134.7 75.4 %collective-permute-start.16 = (f32[32,6,8,128]{3,2,1,0:T(8,128)S(1)}, f32[32,6,8,128]{3,2,1,0:T(8,128)S(1)}, u32[]{:S(2)}, u32[]{:S(2)}) collective-permute-start(f32[32,6,8,128]{3,2,1,0:T(8,128)S(1)} %get-tuple-element.40), channel_id=1, source_target_pairs={{0,35},{1,34},{2,33},{3,32},{4,39},{5,38},{6,37},{7,36},{8,43},{9,... | collective-permute-start | bytes 2359304 | tf_op jit(solution)/shard_map/ppermute | solution.py:199
  149.1 59.8 %collective-permute-start.12 = (f32[16,6,8,128]{3,2,1,0:T(8,128)S(1)}, f32[16,6,8,128]{3,2,1,0:T(8,128)S(1)}, u32[]{:S(2)}, u32[]{:S(2)}) collective-permute-start(f32[16,6,8,128]{3,2,1,0:T(8,128)S(1)} %get-tuple-element.36), channel_id=1, source_target_pairs={{0,17},{1,18},{2,19},{3,16},{4,21},{5,22},{6,23},{7,20},{8,25},{9,... | collective-permute-start | bytes 1179656 | tf_op jit(solution)/shard_map/ppermute | solution.py:199
  166.6 42.3 %collective-permute-start.13 = (f32[16,6,8,128]{3,2,1,0:T(8,128)S(1)}, f32[16,6,8,128]{3,2,1,0:T(8,128)S(1)}, u32[]{:S(2)}, u32[]{:S(2)}) collective-permute-start(f32[16,6,8,128]{3,2,1,0:T(8,128)S(1)} %get-tuple-element.37), channel_id=1, source_target_pairs={{0,19},{1,16},{2,17},{3,18},{4,23},{5,20},{6,21},{7,22},{8,27},{9,... | collective-permute-start | bytes 1179656 | tf_op jit(solution)/shard_map/ppermute | solution.py:199
  (5 other events, 18.8 us)

commit v4 on v3

--- a/solution.py
+++ b/solution.py
@@ -13,13 +13,12 @@
 N_ROW, N_COL = 8, 16
 HALVES, ROW_PARTS, TILES, E, COL_PARTS = 2, 4, 16, 6, 4
 F32 = jnp.float32
-WHOLE, UPPER, LOWER = (0, 1), (0,), (1,)
-FIRST = [(1, 0, 0, WHOLE), (0, 1, 0, WHOLE)]
-SECOND = [(0, 3, 0, WHOLE), (1, 0, 1, WHOLE), (0, 1, 1, UPPER), (0, 3, 1, UPPER)]
-THIRD = [(1, 1, 0, WHOLE), (0, 1, 1, LOWER), (0, 3, 1, LOWER), (0, 2, 0, WHOLE), (0, 2, 1, WHOLE), (1, 3, 0, WHOLE),
-         (1, 1, 1, WHOLE), (1, 3, 1, WHOLE), (0, 0, 1, WHOLE), (1, 2, 0, WHOLE), (1, 2, 1, WHOLE)]
+WHOLE = (0, 1)
+FIRST = [(1, 2, 0, WHOLE), (0, 1, 0, WHOLE)]
+SECOND = [(0, 3, 0, WHOLE)]
+THIRD = [(1, 1, 0, WHOLE), (1, 3, 0, WHOLE), (0, 1, 1, WHOLE), (0, 3, 1, WHOLE), (1, 1, 1, WHOLE), (0, 2, 0, WHOLE), (0, 2, 1, WHOLE), (1, 3, 1, WHOLE), (0, 0, 1, WHOLE), (1, 2, 1, WHOLE), (1, 0, 0, WHOLE), (1, 0, 1, WHOLE)]
 NEAR = [(0, 1, 0), (0, 3, 0), (0, 2, 0), (1, 0, 0), (1, 1, 0), (1, 3, 0), (1, 2, 0)]
-GROUPS = [[(1, 2, 0, WHOLE)], [(0, 1, 1, LOWER), (0, 3, 1, LOWER), (0, 2, 0, WHOLE)], [(0, 2, 1, WHOLE), (1, 2, 1, WHOLE)]]
+GROUPS = [[(1, 0, 0, WHOLE), (0, 1, 1, WHOLE)], [(0, 3, 1, WHOLE), (0, 2, 0, WHOLE), (0, 2, 1, WHOLE), (1, 0, 1, WHOLE)]]
 SOON = [f for f in FIRST + SECOND + THIRD if f not in sum(GROUPS, [])]
 SLOTS = 4
 CHUNKS = HALVES * 8

time: 214 us -> 190 us (0.89)
  waiting for transfers between devices: 143 us -> 122 us
    ppermute x29 -> x27, waiting for transfers between devices: 143 us -> 122 us  [permute(): return lax.ppermute(value, AXES, pairs)]
    ppermute x29 -> x27, starting transfers between devices: 46.6 us -> 45.2 us  [permute(): return lax.ppermute(value, AXES, pairs)]
  transfers between devices with their start and end apart: 29 -> 27, of which waited for: 14 -> 12; matrix products, arithmetic and copies ran while one was open for 0% -> 0% of each run, Pallas kernels for 3% -> 3%
where the time goes in v4:
time: 190 us; the launch traced here: 188 us
  waiting for transfers between devices  122 us (64%)
  starting transfers between devices  45.2 us (24%)
  Pallas kernels  20.1 us (11%)
    ppermute x27, waiting for transfers between devices, permute(): return lax.ppermute(value, AXES, pairs)  122 us
    ppermute x27, starting transfers between devices, permute(): return lax.ppermute(value, AXES, pairs)  45.2 us
    pallas_call x3, Pallas kernels, go(): plain(functools.partial(pack, flows), tuple((pltpu.VMEM((len(f[3]) * TILE...  6.54 us
    pallas_call x1, Pallas kernels, body(): plain(reduce, tiles((2, *SMALL)), [HBM, VMEM], VMEM, [pltpu.VMEM((SLOTS,...  6.5 us
  transfers between devices with their start and end apart: 27, of which 12 were waited for; matrix products, arithmetic and copies ran while one was open for 0% of the time, Pallas kernels for 3%

profile of v4, /device:TPU:8, one launch (start us, length us, event | category | flops | bytes accessed | tf_op | source)
XLA Modules:
  0.0 187.7 jit_solution(624187997823449161)
XLA Ops:
  3.3 3.9 %shard_map.40 = (f32[32,6,8,128]{3,2,1,0:T(8,128)S(1)}, f32[32,6,8,128]{3,2,1,0:T(8,128)S(1)}, f32[32,6,8,128]{3,2,1,0:T(8,128)S(1)}, f32[32,6,8,128]{3,2,1,0:T(...) custom-call(f32[2,8,16,6,2,8,128]{6,5,4,3,2,1,0:T(8,128)} %bitcast.1, ...), custom_call_target="tpu_custom_call" | custom-call | flops 50000000 | bytes 1048576 | tf_op jit(solution)/shard_map/pallas_call | solution.py:202
  7.2 6.5 %shard_map.44.part = f32[2,8,128]{2,1,0:T(8,128)S(1)} custom-call(f32[2,8,16,6,2,8,128]{6,5,4,3,2,1,0:T(8,128)} %bitcast.11, f32[32,6,8,128]{3,2,1,0:T(8,128)S(1)} %get-tuple-element.23._), custom_call_target="tpu_custom_call" | custom-call | flops 70000000 | bytes 1048576 | tf_op jit(solution)/shard_map/pallas_call | solution.py:213
  15.0 3.2 %collective-permute-start.22 = (f32[2,8,128]{2,1,0:T(8,128)S(1)}, f32[2,8,128]{2,1,0:T(8,128)S(1)}, u32[]{:S(2)}, u32[]{:S(2)}) collective-permute-start(f32[2,8,128]{2,1,0:T(8,128)S(1)} %shard_map.45.refs_0_), channel_id=1, source_target_pairs={{0,34},{1,35},{2,32},{3,33},{4,38},{5,39},{6,36},{7,37},{8,42},{9,... | collective-permute-start | bytes 24584 | tf_op jit(solution)/shard_map/ppermute | solution.py:198
  21.6 2.4 %collective-permute-start.18 = (f32[2,8,128]{2,1,0:T(8,128)S(1)}, f32[2,8,128]{2,1,0:T(8,128)S(1)}, u32[]{:S(2)}, u32[]{:S(2)}) collective-permute-start(f32[2,8,128]{2,1,0:T(8,128)S(1)} %shard_map.45.refs_0_), channel_id=1, source_target_pairs={{0,2},{1,3},{2,0},{3,1},{4,6},{5,7},{6,4},{7,5},{8,10},{9,11},{10,... | collective-permute-start | bytes 24584 | tf_op jit(solution)/shard_map/ppermute | solution.py:198
  24.1 2.0 %collective-permute-start.16 = (f32[2,8,128]{2,1,0:T(8,128)S(1)}, f32[2,8,128]{2,1,0:T(8,128)S(1)}, u32[]{:S(2)}, u32[]{:S(2)}) collective-permute-start(f32[2,8,128]{2,1,0:T(8,128)S(1)} %shard_map.45.refs_0_), channel_id=1, source_target_pairs={{0,16},{1,19},{2,18},{3,17},{4,20},{5,23},{6,22},{7,21},{8,24},{9,... | collective-permute-start | bytes 24584 | tf_op jit(solution)/shard_map/ppermute | solution.py:198
  28.0 2.8 %collective-permute-start.23 = (f32[4,8,128]{2,1,0:T(8,128)S(1)}, f32[4,8,128]{2,1,0:T(8,128)S(1)}, u32[]{:S(2)}, u32[]{:S(2)}) collective-permute-start(f32[4,8,128]{2,1,0:T(8,128)S(1)} %shard_map.46.plane_ref), channel_id=1, source_target_pairs={{0,96},{1,97},{2,98},{3,99},{4,100},{5,101},{6,102},{7,103},{8,104... | collective-permute-start | bytes 49160 | tf_op jit(solution)/shard_map/ppermute | solution.py:198
  30.8 2.2 %collective-permute-done.23.other_ref = f32[4,8,128]{2,1,0:T(8,128)S(1)} collective-permute-done((f32[4,8,128]{2,1,0:T(8,128)S(1)}, f32[4,8,128]{2,1,0:T(8,128)S(1)}, u32[]{:S(2)}, u32[]{:S(2)}) %collective-permute-start.23) | collective-permute-done | bytes 16416 | tf_op jit(solution)/shard_map/ppermute | solution.py:198
  33.1 4.1 %collective-permute-start.26 = (f32[8,128]{1,0:T(8,128)S(1)}, f32[8,128]{1,0:T(8,128)S(1)}, u32[]{:S(2)}, u32[]{:S(2)}) collective-permute-start(f32[8,128]{1,0:T(8,128)S(1)} %get-tuple-element.36.square_ref), channel_id=1, source_target_pairs={{0,12},{1,13},{2,14},{3,15},{4,0},{5,1},{6,2},{7,3},{8,4},{9,5},{1... | collective-permute-start | bytes 12296 | tf_op jit(solution)/shard_map/ppermute | solution.py:198
  38.4 3.2 %collective-permute-start.2 = (f32[32,6,8,128]{3,2,1,0:T(8,128)S(1)}, f32[32,6,8,128]{3,2,1,0:T(8,128)S(1)}, u32[]{:S(2)}, u32[]{:S(2)}) collective-permute-start(f32[32,6,8,128]{3,2,1,0:T(8,128)S(1)} %shard_map.39.refs_0_), channel_id=1, source_target_pairs={{0,18},{1,17},{2,16},{3,19},{4,22},{5,21},{6,20},{7,23},{8,26},{9,... | collective-permute-start | bytes 2359304 | tf_op jit(solution)/shard_map/ppermute | solution.py:198
  41.7 1.8 collective-permute-start
  43.5 1.8 collective-permute-start.4
  45.2 44.0 %collective-permute-done.2.refs_2_ = f32[32,6,8,128]{3,2,1,0:T(8,128)S(1)} collective-permute-done((f32[32,6,8,128]{3,2,1,0:T(8,128)S(1)}, f32[32,6,8,128]{3,2,1,0:T(8,128)S(1)}, u32[]{:S(2)}, u32[]{:S(2)}) %collective-permute-start.2) | collective-permute-done | bytes 786464 | tf_op jit(solution)/shard_map/ppermute | solution.py:198
  90.8 2.3 %collective-permute-start.8 = (f32[32,6,8,128]{3,2,1,0:T(8,128)S(1)}, f32[32,6,8,128]{3,2,1,0:T(8,128)S(1)}, u32[]{:S(2)}, u32[]{:S(2)}) collective-permute-start(f32[32,6,8,128]{3,2,1,0:T(8,128)S(1)} %get-tuple-element.28), channel_id=1, source_target_pairs={{0,35},{1,34},{2,33},{3,32},{4,39},{5,38},{6,37},{7,36},{8,43},{9,... | collective-permute-start | bytes 2359304 | tf_op jit(solution)/shard_map/ppermute | solution.py:198
  94.9 15.1 %collective-permute-done.6.refs_6_ = f32[32,6,8,128]{3,2,1,0:T(8,128)S(1)} collective-permute-done((f32[32,6,8,128]{3,2,1,0:T(8,128)S(1)}, f32[32,6,8,128]{3,2,1,0:T(8,128)S(1)}, u32[]{:S(2)}, u32[]{:S(2)}) %collective-permute-start.6) | collective-permute-done | bytes 786464 | tf_op jit(solution)/shard_map/ppermute | solution.py:198
  109.9 3.7 %collective-permute-start.11 = (f32[32,6,8,128]{3,2,1,0:T(8,128)S(1)}, f32[32,6,8,128]{3,2,1,0:T(8,128)S(1)}, u32[]{:S(2)}, u32[]{:S(2)}) collective-permute-start(f32[32,6,8,128]{3,2,1,0:T(8,128)S(1)} %get-tuple-element.31), channel_id=1, source_target_pairs={{0,19},{1,16},{2,17},{3,18},{4,23},{5,20},{6,21},{7,22},{8,27},{9,... | collective-permute-start | bytes 2359304 | tf_op jit(solution)/shard_map/ppermute | solution.py:198
  113.7 14.3 %collective-permute-done.8.refs_8_ = f32[32,6,8,128]{3,2,1,0:T(8,128)S(1)} collective-permute-done((f32[32,6,8,128]{3,2,1,0:T(8,128)S(1)}, f32[32,6,8,128]{3,2,1,0:T(8,128)S(1)}, u32[]{:S(2)}, u32[]{:S(2)}) %collective-permute-start.8) | collective-permute-done | bytes 786464 | tf_op jit(solution)/shard_map/ppermute | solution.py:198
  127.9 2.1 %collective-permute-start.12 = (f32[32,6,8,128]{3,2,1,0:T(8,128)S(1)}, f32[32,6,8,128]{3,2,1,0:T(8,128)S(1)}, u32[]{:S(2)}, u32[]{:S(2)}) collective-permute-start(f32[32,6,8,128]{3,2,1,0:T(8,128)S(1)} %get-tuple-element.32), channel_id=1, source_target_pairs={{0,2},{1,3},{2,0},{3,1},{4,6},{5,7},{6,4},{7,5},{8,10},{9,11},{10,... | collective-permute-start | bytes 2359304 | tf_op jit(solution)/shard_map/ppermute | solution.py:198
  130.1 10.4 %collective-permute-done.9.refs_0_ = f32[32,6,8,128]{3,2,1,0:T(8,128)S(1)} collective-permute-done((f32[32,6,8,128]{3,2,1,0:T(8,128)S(1)}, f32[32,6,8,128]{3,2,1,0:T(8,128)S(1)}, u32[]{:S(2)}, u32[]{:S(2)}) %collective-permute-start.9) | collective-permute-done | bytes 786464 | tf_op jit(solution)/shard_map/ppermute | solution.py:198
  140.5 4.6 %collective-permute-start.13 = (f32[32,6,8,128]{3,2,1,0:T(8,128)S(1)}, f32[32,6,8,128]{3,2,1,0:T(8,128)S(1)}, u32[]{:S(2)}, u32[]{:S(2)}) collective-permute-start(f32[32,6,8,128]{3,2,1,0:T(8,128)S(1)} %get-tuple-element.33), channel_id=1, source_target_pairs={{0,3},{1,2},{2,1},{3,0},{4,7},{5,6},{6,5},{7,4},{8,11},{9,10},{10,... | collective-permute-start | bytes 2359304 | tf_op jit(solution)/shard_map/ppermute | solution.py:198
  145.1 13.3 %collective-permute-done.3.refs_3_ = f32[32,6,8,128]{3,2,1,0:T(8,128)S(1)} collective-permute-done((f32[32,6,8,128]{3,2,1,0:T(8,128)S(1)}, f32[32,6,8,128]{3,2,1,0:T(8,128)S(1)}, u32[]{:S(2)}, u32[]{:S(2)}) %collective-permute-start.3) | collective-permute-done | bytes 786464 | tf_op jit(solution)/shard_map/ppermute | solution.py:198
  158.4 2.8 %collective-permute-start.14 = (f32[32,6,8,128]{3,2,1,0:T(8,128)S(1)}, f32[32,6,8,128]{3,2,1,0:T(8,128)S(1)}, u32[]{:S(2)}, u32[]{:S(2)}) collective-permute-start(f32[32,6,8,128]{3,2,1,0:T(8,128)S(1)} %get-tuple-element.34), channel_id=1, source_target_pairs={{0,33},{1,32},{2,35},{3,34},{4,37},{5,36},{6,39},{7,38},{8,41},{9,... | collective-permute-start | bytes 2359304 | tf_op jit(solution)/shard_map/ppermute | solution.py:198
  161.9 3.4 %shard_map.41._ = f32[2,4,16,6,4,8,128]{6,5,4,3,2,1,0:T(8,128)} custom-call(f32[2,8,16,6,2,8,128]{6,5,4,3,2,1,0:T(8,128)} %bitcast.12, f32[32,6,8,128]{3,2,1,0:T(8,128)S(1)} %collective-permute-done.refs_0_, f32[32,6,8,128]{3,2,1,0:T(8,128)S(1)} %collective-permute-done.1.refs_1_, f32[32,6,8,128]{3,2,1,0:T(8,128)S(1)} %collective-permute-done.2.refs_2_, ...), custom_call_target="tpu_custom_call" | custom-call | flops 50000000 | bytes 1048576 | tf_op jit(solution)/shard_map/pallas_call | solution.py:226
  166.5 2.7 %collective-permute-done.12.refs_1_ = f32[32,6,8,128]{3,2,1,0:T(8,128)S(1)} collective-permute-done((f32[32,6,8,128]{3,2,1,0:T(8,128)S(1)}, f32[32,6,8,128]{3,2,1,0:T(8,128)S(1)}, u32[]{:S(2)}, u32[]{:S(2)}) %collective-permute-start.12) | collective-permute-done | bytes 786464 | tf_op jit(solution)/shard_map/ppermute | solution.py:198
  169.2 16.8 %collective-permute-done.13.refs_2_ = f32[32,6,8,128]{3,2,1,0:T(8,128)S(1)} collective-permute-done((f32[32,6,8,128]{3,2,1,0:T(8,128)S(1)}, f32[32,6,8,128]{3,2,1,0:T(8,128)S(1)}, u32[]{:S(2)}, u32[]{:S(2)}) %collective-permute-start.13) | collective-permute-done | bytes 786464 | tf_op jit(solution)/shard_map/ppermute | solution.py:198
  (41 shorter events, 17.5 us)
Async XLA Ops:
  15.0 9.1 %collective-permute-start.22 = (f32[2,8,128]{2,1,0:T(8,128)S(1)}, f32[2,8,128]{2,1,0:T(8,128)S(1)}, u32[]{:S(2)}, u32[]{:S(2)}) collective-permute-start(f32[2,8,128]{2,1,0:T(8,128)S(1)} %shard_map.45.refs_0_), channel_id=1, source_target_pairs={{0,34},{1,35},{2,32},{3,33},{4,38},{5,39},{6,36},{7,37},{8,42},{9,... | collective-permute-start | bytes 24584 | tf_op jit(solution)/shard_map/ppermute | solution.py:198
  18.2 5.9 %collective-permute-start.21 = (f32[2,8,128]{2,1,0:T(8,128)S(1)}, f32[2,8,128]{2,1,0:T(8,128)S(1)}, u32[]{:S(2)}, u32[]{:S(2)}) collective-permute-start(f32[2,8,128]{2,1,0:T(8,128)S(1)} %shard_map.45.refs_0_), channel_id=1, source_target_pairs={{0,50},{1,49},{2,48},{3,51},{4,54},{5,53},{6,52},{7,55},{8,58},{9,... | collective-permute-start | bytes 24584 | tf_op jit(solution)/shard_map/ppermute | solution.py:198
  19.5 6.6 %collective-permute-start.20 = (f32[2,8,128]{2,1,0:T(8,128)S(1)}, f32[2,8,128]{2,1,0:T(8,128)S(1)}, u32[]{:S(2)}, u32[]{:S(2)}) collective-permute-start(f32[2,8,128]{2,1,0:T(8,128)S(1)} %shard_map.45.refs_0_), channel_id=1, source_target_pairs={{0,48},{1,51},{2,50},{3,49},{4,52},{5,55},{6,54},{7,53},{8,56},{9,... | collective-permute-start | bytes 24584 | tf_op jit(solution)/shard_map/ppermute | solution.py:198
  21.1 5.0 %collective-permute-start.19 = (f32[2,8,128]{2,1,0:T(8,128)S(1)}, f32[2,8,128]{2,1,0:T(8,128)S(1)}, u32[]{:S(2)}, u32[]{:S(2)}) collective-permute-start(f32[2,8,128]{2,1,0:T(8,128)S(1)} %shard_map.45.refs_0_), channel_id=1, source_target_pairs={{0,32},{1,33},{2,34},{3,35},{4,36},{5,37},{6,38},{7,39},{8,40},{9,... | collective-permute-start | bytes 24584 | tf_op jit(solution)/shard_map/ppermute | solution.py:198
  21.6 5.2 %collective-permute-start.18 = (f32[2,8,128]{2,1,0:T(8,128)S(1)}, f32[2,8,128]{2,1,0:T(8,128)S(1)}, u32[]{:S(2)}, u32[]{:S(2)}) collective-permute-start(f32[2,8,128]{2,1,0:T(8,128)S(1)} %shard_map.45.refs_0_), channel_id=1, source_target_pairs={{0,2},{1,3},{2,0},{3,1},{4,6},{5,7},{6,4},{7,5},{8,10},{9,11},{10,... | collective-permute-start | bytes 24584 | tf_op jit(solution)/shard_map/ppermute | solution.py:198
  28.0 5.0 %collective-permute-start.23 = (f32[4,8,128]{2,1,0:T(8,128)S(1)}, f32[4,8,128]{2,1,0:T(8,128)S(1)}, u32[]{:S(2)}, u32[]{:S(2)}) collective-permute-start(f32[4,8,128]{2,1,0:T(8,128)S(1)} %shard_map.46.plane_ref), channel_id=1, source_target_pairs={{0,96},{1,97},{2,98},{3,99},{4,100},{5,101},{6,102},{7,103},{8,104... | collective-permute-start | bytes 49160 | tf_op jit(solution)/shard_map/ppermute | solution.py:198
  33.1 8.6 %collective-permute-start.26 = (f32[8,128]{1,0:T(8,128)S(1)}, f32[8,128]{1,0:T(8,128)S(1)}, u32[]{:S(2)}, u32[]{:S(2)}) collective-permute-start(f32[8,128]{1,0:T(8,128)S(1)} %get-tuple-element.36.square_ref), channel_id=1, source_target_pairs={{0,12},{1,13},{2,14},{3,15},{4,0},{5,1},{6,2},{7,3},{8,4},{9,5},{1... | collective-permute-start | bytes 12296 | tf_op jit(solution)/shard_map/ppermute | solution.py:198
  37.2 6.3 %collective-permute-start.25 = (f32[8,128]{1,0:T(8,128)S(1)}, f32[8,128]{1,0:T(8,128)S(1)}, u32[]{:S(2)}, u32[]{:S(2)}) collective-permute-start(f32[8,128]{1,0:T(8,128)S(1)} %get-tuple-element.36.square_ref), channel_id=1, source_target_pairs={{0,8},{1,9},{2,10},{3,11},{4,12},{5,13},{6,14},{7,15},{8,0},{9,1},... | collective-permute-start | bytes 12296 | tf_op jit(solution)/shard_map/ppermute | solution.py:198
  37.2 8.1 %collective-permute-start.24 = (f32[8,128]{1,0:T(8,128)S(1)}, f32[8,128]{1,0:T(8,128)S(1)}, u32[]{:S(2)}, u32[]{:S(2)}) collective-permute-start(f32[8,128]{1,0:T(8,128)S(1)} %get-tuple-element.36.square_ref), channel_id=1, source_target_pairs={{0,4},{1,5},{2,6},{3,7},{4,8},{5,9},{6,10},{7,11},{8,12},{9,13},{1... | collective-permute-start | bytes 12296 | tf_op jit(solution)/shard_map/ppermute | solution.py:198
  38.4 50.8 %collective-permute-start.2 = (f32[32,6,8,128]{3,2,1,0:T(8,128)S(1)}, f32[32,6,8,128]{3,2,1,0:T(8,128)S(1)}, u32[]{:S(2)}, u32[]{:S(2)}) collective-permute-start(f32[32,6,8,128]{3,2,1,0:T(8,128)S(1)} %shard_map.39.refs_0_), channel_id=1, source_target_pairs={{0,18},{1,17},{2,16},{3,19},{4,22},{5,21},{6,20},{7,23},{8,26},{9,... | collective-permute-start | bytes 2359304 | tf_op jit(solution)/shard_map/ppermute | solution.py:198
  41.7 47.6 %collective-permute-start.1 = (f32[32,6,8,128]{3,2,1,0:T(8,128)S(1)}, f32[32,6,8,128]{3,2,1,0:T(8,128)S(1)}, u32[]{:S(2)}, u32[]{:S(2)}) collective-permute-start(f32[32,6,8,128]{3,2,1,0:T(8,128)S(1)} %get-tuple-element.22), channel_id=1, source_target_pairs={{0,16},{1,19},{2,18},{3,17},{4,20},{5,23},{6,22},{7,21},{8,24},{9,... | collective-permute-start | bytes 2359304 | tf_op jit(solution)/shard_map/ppermute | solution.py:198
  41.7 49.1 %collective-permute-start = (f32[32,6,8,128]{3,2,1,0:T(8,128)S(1)}, f32[32,6,8,128]{3,2,1,0:T(8,128)S(1)}, u32[]{:S(2)}, u32[]{:S(2)}) collective-permute-start(f32[32,6,8,128]{3,2,1,0:T(8,128)S(1)} %get-tuple-element.21.refs_0_), channel_id=1, source_target_pairs={{0,34},{1,35},{2,32},{3,33},{4,38},{5,39},{6,36},{7,37},{8,42},{9,... | collective-permute-start | bytes 2359304 | tf_op jit(solution)/shard_map/ppermute | solution.py:198
  43.5 49.6 %collective-permute-start.4 = (f32[32,6,8,128]{3,2,1,0:T(8,128)S(1)}, f32[32,6,8,128]{3,2,1,0:T(8,128)S(1)}, u32[]{:S(2)}, u32[]{:S(2)}) collective-permute-start(f32[32,6,8,128]{3,2,1,0:T(8,128)S(1)} %get-tuple-element.24), channel_id=1, source_target_pairs={{0,50},{1,49},{2,48},{3,51},{4,54},{5,53},{6,52},{7,55},{8,58},{9,... | collective-permute-start | bytes 2359304 | tf_op jit(solution)/shard_map/ppermute | solution.py:198
  45.2 48.4 %collective-permute-start.5 = (f32[32,6,8,128]{3,2,1,0:T(8,128)S(1)}, f32[32,6,8,128]{3,2,1,0:T(8,128)S(1)}, u32[]{:S(2)}, u32[]{:S(2)}) collective-permute-start(f32[32,6,8,128]{3,2,1,0:T(8,128)S(1)} %get-tuple-element.25), channel_id=1, source_target_pairs={{0,49},{1,50},{2,51},{3,48},{4,53},{5,54},{6,55},{7,52},{8,57},{9,... | collective-permute-start | bytes 2359304 | tf_op jit(solution)/shard_map/ppermute | solution.py:198
  89.2 20.7 %collective-permute-start.6 = (f32[32,6,8,128]{3,2,1,0:T(8,128)S(1)}, f32[32,6,8,128]{3,2,1,0:T(8,128)S(1)}, u32[]{:S(2)}, u32[]{:S(2)}) collective-permute-start(f32[32,6,8,128]{3,2,1,0:T(8,128)S(1)} %get-tuple-element.26), channel_id=1, source_target_pairs={{0,51},{1,48},{2,49},{3,50},{4,55},{5,52},{6,53},{7,54},{8,59},{9,... | collective-permute-start | bytes 2359304 | tf_op jit(solution)/shard_map/ppermute | solution.py:198
  89.2 20.7 %collective-permute-start.7 = (f32[32,6,8,128]{3,2,1,0:T(8,128)S(1)}, f32[32,6,8,128]{3,2,1,0:T(8,128)S(1)}, u32[]{:S(2)}, u32[]{:S(2)}) collective-permute-start(f32[32,6,8,128]{3,2,1,0:T(8,128)S(1)} %get-tuple-element.27), channel_id=1, source_target_pairs={{0,1},{1,0},{2,3},{3,2},{4,5},{5,4},{6,7},{7,6},{8,9},{9,8},{10,11... | collective-permute-start | bytes 2359304 | tf_op jit(solution)/shard_map/ppermute | solution.py:198
  90.8 37.2 %collective-permute-start.8 = (f32[32,6,8,128]{3,2,1,0:T(8,128)S(1)}, f32[32,6,8,128]{3,2,1,0:T(8,128)S(1)}, u32[]{:S(2)}, u32[]{:S(2)}) collective-permute-start(f32[32,6,8,128]{3,2,1,0:T(8,128)S(1)} %get-tuple-element.28), channel_id=1, source_target_pairs={{0,35},{1,34},{2,33},{3,32},{4,39},{5,38},{6,37},{7,36},{8,43},{9,... | collective-permute-start | bytes 2359304 | tf_op jit(solution)/shard_map/ppermute | solution.py:198
  93.0 47.4 %collective-permute-start.9 = (f32[32,6,8,128]{3,2,1,0:T(8,128)S(1)}, f32[32,6,8,128]{3,2,1,0:T(8,128)S(1)}, u32[]{:S(2)}, u32[]{:S(2)}) collective-permute-start(f32[32,6,8,128]{3,2,1,0:T(8,128)S(1)} %get-tuple-element.29), channel_id=1, source_target_pairs={{0,32},{1,33},{2,34},{3,35},{4,36},{5,37},{6,38},{7,39},{8,40},{9,... | collective-permute-start | bytes 2359304 | tf_op jit(solution)/shard_map/ppermute | solution.py:198
  93.6 64.8 %collective-permute-start.3 = (f32[32,6,8,128]{3,2,1,0:T(8,128)S(1)}, f32[32,6,8,128]{3,2,1,0:T(8,128)S(1)}, u32[]{:S(2)}, u32[]{:S(2)}) collective-permute-start(f32[32,6,8,128]{3,2,1,0:T(8,128)S(1)} %get-tuple-element.23._), channel_id=1, source_target_pairs={{0,48},{1,51},{2,50},{3,49},{4,52},{5,55},{6,54},{7,53},{8,56},{9,... | collective-permute-start | bytes 2359304 | tf_op jit(solution)/shard_map/ppermute | solution.py:198
  109.9 55.3 %collective-permute-start.10 = (f32[32,6,8,128]{3,2,1,0:T(8,128)S(1)}, f32[32,6,8,128]{3,2,1,0:T(8,128)S(1)}, u32[]{:S(2)}, u32[]{:S(2)}) collective-permute-start(f32[32,6,8,128]{3,2,1,0:T(8,128)S(1)} %get-tuple-element.30), channel_id=1, source_target_pairs={{0,17},{1,18},{2,19},{3,16},{4,21},{5,22},{6,23},{7,20},{8,25},{9,... | collective-permute-start | bytes 2359304 | tf_op jit(solution)/shard_map/ppermute | solution.py:198
  109.9 56.5 %collective-permute-start.11 = (f32[32,6,8,128]{3,2,1,0:T(8,128)S(1)}, f32[32,6,8,128]{3,2,1,0:T(8,128)S(1)}, u32[]{:S(2)}, u32[]{:S(2)}) collective-permute-start(f32[32,6,8,128]{3,2,1,0:T(8,128)S(1)} %get-tuple-element.31), channel_id=1, source_target_pairs={{0,19},{1,16},{2,17},{3,18},{4,23},{5,20},{6,21},{7,22},{8,27},{9,... | collective-permute-start | bytes 2359304 | tf_op jit(solution)/shard_map/ppermute | solution.py:198
  127.9 41.3 %collective-permute-start.12 = (f32[32,6,8,128]{3,2,1,0:T(8,128)S(1)}, f32[32,6,8,128]{3,2,1,0:T(8,128)S(1)}, u32[]{:S(2)}, u32[]{:S(2)}) collective-permute-start(f32[32,6,8,128]{3,2,1,0:T(8,128)S(1)} %get-tuple-element.32), channel_id=1, source_target_pairs={{0,2},{1,3},{2,0},{3,1},{4,6},{5,7},{6,4},{7,5},{8,10},{9,11},{10,... | collective-permute-start | bytes 2359304 | tf_op jit(solution)/shard_map/ppermute | solution.py:198
  140.5 45.5 %collective-permute-start.13 = (f32[32,6,8,128]{3,2,1,0:T(8,128)S(1)}, f32[32,6,8,128]{3,2,1,0:T(8,128)S(1)}, u32[]{:S(2)}, u32[]{:S(2)}) collective-permute-start(f32[32,6,8,128]{3,2,1,0:T(8,128)S(1)} %get-tuple-element.33), channel_id=1, source_target_pairs={{0,3},{1,2},{2,1},{3,0},{4,7},{5,6},{6,5},{7,4},{8,11},{9,10},{10,... | collective-permute-start | bytes 2359304 | tf_op jit(solution)/shard_map/ppermute | solution.py:198
  158.4 27.6 %collective-permute-start.14 = (f32[32,6,8,128]{3,2,1,0:T(8,128)S(1)}, f32[32,6,8,128]{3,2,1,0:T(8,128)S(1)}, u32[]{:S(2)}, u32[]{:S(2)}) collective-permute-start(f32[32,6,8,128]{3,2,1,0:T(8,128)S(1)} %get-tuple-element.34), channel_id=1, source_target_pairs={{0,33},{1,32},{2,35},{3,34},{4,37},{5,36},{6,39},{7,38},{8,41},{9,... | collective-permute-start | bytes 2359304 | tf_op jit(solution)/shard_map/ppermute | solution.py:198
  (3 other events, 8.8 us)

commit v5 on v4

--- a/solution.py
+++ b/solution.py
@@ -13,12 +13,12 @@
 N_ROW, N_COL = 8, 16
 HALVES, ROW_PARTS, TILES, E, COL_PARTS = 2, 4, 16, 6, 4
 F32 = jnp.float32
-WHOLE = (0, 1)
-FIRST = [(1, 2, 0, WHOLE), (0, 1, 0, WHOLE)]
+WHOLE, UPPER, LOWER = (0, 1), (0,), (1,)
+FIRST = [(0, 1, 0, WHOLE), (1, 1, 0, WHOLE)]
 SECOND = [(0, 3, 0, WHOLE)]
-THIRD = [(1, 1, 0, WHOLE), (1, 3, 0, WHOLE), (0, 1, 1, WHOLE), (0, 3, 1, WHOLE), (1, 1, 1, WHOLE), (0, 2, 0, WHOLE), (0, 2, 1, WHOLE), (1, 3, 1, WHOLE), (0, 0, 1, WHOLE), (1, 2, 1, WHOLE), (1, 0, 0, WHOLE), (1, 0, 1, WHOLE)]
+THIRD = [(1, 2, 0, WHOLE), (1, 3, 0, WHOLE), (0, 1, 1, WHOLE), (0, 3, 1, WHOLE), (1, 1, 1, WHOLE), (0, 2, 0, WHOLE), (0, 2, 1, UPPER), (1, 3, 1, WHOLE), (0, 2, 1, LOWER), (0, 0, 1, WHOLE), (1, 2, 1, WHOLE), (1, 0, 0, WHOLE), (1, 0, 1, UPPER), (1, 0, 1, LOWER)]
 NEAR = [(0, 1, 0), (0, 3, 0), (0, 2, 0), (1, 0, 0), (1, 1, 0), (1, 3, 0), (1, 2, 0)]
-GROUPS = [[(1, 0, 0, WHOLE), (0, 1, 1, WHOLE)], [(0, 3, 1, WHOLE), (0, 2, 0, WHOLE), (0, 2, 1, WHOLE), (1, 0, 1, WHOLE)]]
+GROUPS = [[(1, 0, 0, WHOLE), (0, 1, 1, WHOLE)], [(0, 3, 1, WHOLE), (0, 2, 0, WHOLE)], [(0, 2, 1, UPPER), (1, 0, 1, UPPER)], [(0, 2, 1, LOWER), (1, 0, 1, LOWER)]]
 SOON = [f for f in FIRST + SECOND + THIRD if f not in sum(GROUPS, [])]
 SLOTS = 4
 CHUNKS = HALVES * 8

time: 190 us -> 193 us (1.016)
  starting transfers between devices: 45.2 us -> 78.5 us
  waiting for transfers between devices: 122 us -> 90.1 us
    ppermute x27 -> x29, starting transfers between devices: 45.2 us -> 78.5 us  [permute(): return lax.ppermute(value, AXES, pairs)]
    ppermute x27 -> x29, waiting for transfers between devices: 122 us -> 90.1 us  [permute(): return lax.ppermute(value, AXES, pairs)]
    pallas_call x2 -> x4, Pallas kernels: 2.93 us -> 4.35 us  [body(): plain(functools.partial(write_group, flows), jax.ShapeDtypeStruct(BIG, F3...]
  transfers between devices with their start and end apart: 27 -> 29, of which waited for: 12 -> 14; matrix products, arithmetic and copies ran while one was open for 0% -> 0% of each run, Pallas kernels for 3% -> 9%
where the time goes in v5:
time: 193 us; the launch traced here: 191 us
  waiting for transfers between devices  90.1 us (47%)
  starting transfers between devices  78.5 us (41%)
  Pallas kernels  21.4 us (11%)
    ppermute x29, waiting for transfers between devices, permute(): return lax.ppermute(value, AXES, pairs)  90.1 us
    ppermute x29, starting transfers between devices, permute(): return lax.ppermute(value, AXES, pairs)  78.5 us
    pallas_call x3, Pallas kernels, go(): plain(functools.partial(pack, flows), tuple((pltpu.VMEM((len(f[3]) * TILE...  6.51 us
    pallas_call x1, Pallas kernels, body(): plain(reduce, tiles((2, *SMALL)), [HBM, VMEM], VMEM, [pltpu.VMEM((SLOTS,...  6.5 us
    pallas_call x4, Pallas kernels, body(): plain(functools.partial(write_group, flows), jax.ShapeDtypeStruct(BIG, F3...  4.35 us
  transfers between devices with their start and end apart: 29, of which 14 were waited for; matrix products, arithmetic and copies ran while one was open for 0% of the time, Pallas kernels for 9%

profile of v5, /device:TPU:8, one launch (start us, length us, event | category | flops | bytes accessed | tf_op | source)
XLA Modules:
  0.0 190.8 jit_solution(8331666119123242933)
XLA Ops:
  3.7 2.6 %collective-permute-start.1 = (f32[32,6,8,128]{3,2,1,0:T(8,128)S(1)}, f32[32,6,8,128]{3,2,1,0:T(8,128)S(1)}, u32[]{:S(2)}, u32[]{:S(2)}) collective-permute-start(f32[32,6,8,128]{3,2,1,0:T(8,128)S(1)} %get-tuple-element.24), channel_id=1, source_target_pairs={{0,48},{1,51},{2,50},{3,49},{4,52},{5,55},{6,54},{7,53},{8,56},{9,... | collective-permute-start | bytes 2359304 | tf_op jit(solution)/shard_map/ppermute | solution.py:198
  7.8 3.9 %shard_map.40 = (f32[32,6,8,128]{3,2,1,0:T(8,128)S(1)}, f32[32,6,8,128]{3,2,1,0:T(8,128)S(1)}, f32[32,6,8,128]{3,2,1,0:T(8,128)S(1)}, f32[32,6,8,128]{3,2,1,0:T(...) custom-call(f32[2,8,16,6,2,8,128]{6,5,4,3,2,1,0:T(8,128)} %bitcast.1, ...), custom_call_target="tpu_custom_call" | custom-call | flops 56666664 | bytes 1048576 | tf_op jit(solution)/shard_map/pallas_call | solution.py:202
  11.8 6.5 %shard_map.46.part = f32[2,8,128]{2,1,0:T(8,128)S(1)} custom-call(f32[2,8,16,6,2,8,128]{6,5,4,3,2,1,0:T(8,128)} %bitcast.12, f32[32,6,8,128]{3,2,1,0:T(8,128)S(1)} %get-tuple-element.25._), custom_call_target="tpu_custom_call" | custom-call | flops 70000000 | bytes 1048576 | tf_op jit(solution)/shard_map/pallas_call | solution.py:213
  21.5 3.5 %collective-permute-start.23 = (f32[2,8,128]{2,1,0:T(8,128)S(1)}, f32[2,8,128]{2,1,0:T(8,128)S(1)}, u32[]{:S(2)}, u32[]{:S(2)}) collective-permute-start(f32[2,8,128]{2,1,0:T(8,128)S(1)} %shard_map.47.refs_0_), channel_id=1, source_target_pairs={{0,50},{1,49},{2,48},{3,51},{4,54},{5,53},{6,52},{7,55},{8,58},{9,... | collective-permute-start | bytes 24584 | tf_op jit(solution)/shard_map/ppermute | solution.py:198
  25.9 2.3 %collective-permute-start.22 = (f32[2,8,128]{2,1,0:T(8,128)S(1)}, f32[2,8,128]{2,1,0:T(8,128)S(1)}, u32[]{:S(2)}, u32[]{:S(2)}) collective-permute-start(f32[2,8,128]{2,1,0:T(8,128)S(1)} %shard_map.47.refs_0_), channel_id=1, source_target_pairs={{0,48},{1,51},{2,50},{3,49},{4,52},{5,55},{6,54},{7,53},{8,56},{9,... | collective-permute-start | bytes 24584 | tf_op jit(solution)/shard_map/ppermute | solution.py:198
  32.3 2.6 %collective-permute-start.19 = (f32[2,8,128]{2,1,0:T(8,128)S(1)}, f32[2,8,128]{2,1,0:T(8,128)S(1)}, u32[]{:S(2)}, u32[]{:S(2)}) collective-permute-start(f32[2,8,128]{2,1,0:T(8,128)S(1)} %shard_map.47.refs_0_), channel_id=1, source_target_pairs={{0,18},{1,17},{2,16},{3,19},{4,22},{5,21},{6,20},{7,23},{8,26},{9,... | collective-permute-start | bytes 24584 | tf_op jit(solution)/shard_map/ppermute | solution.py:198
  35.7 2.3 %collective-permute-start.18 = (f32[2,8,128]{2,1,0:T(8,128)S(1)}, f32[2,8,128]{2,1,0:T(8,128)S(1)}, u32[]{:S(2)}, u32[]{:S(2)}) collective-permute-start(f32[2,8,128]{2,1,0:T(8,128)S(1)} %shard_map.47.refs_0_), channel_id=1, source_target_pairs={{0,16},{1,19},{2,18},{3,17},{4,20},{5,23},{6,22},{7,21},{8,24},{9,... | collective-permute-start | bytes 24584 | tf_op jit(solution)/shard_map/ppermute | solution.py:198
  39.9 2.8 %collective-permute-start.25 = (f32[4,8,128]{2,1,0:T(8,128)S(1)}, f32[4,8,128]{2,1,0:T(8,128)S(1)}, u32[]{:S(2)}, u32[]{:S(2)}) collective-permute-start(f32[4,8,128]{2,1,0:T(8,128)S(1)} %shard_map.48.plane_ref), channel_id=1, source_target_pairs={{0,96},{1,97},{2,98},{3,99},{4,100},{5,101},{6,102},{7,103},{8,104... | collective-permute-start | bytes 49160 | tf_op jit(solution)/shard_map/ppermute | solution.py:198
  42.7 2.2 %collective-permute-done.25.other_ref = f32[4,8,128]{2,1,0:T(8,128)S(1)} collective-permute-done((f32[4,8,128]{2,1,0:T(8,128)S(1)}, f32[4,8,128]{2,1,0:T(8,128)S(1)}, u32[]{:S(2)}, u32[]{:S(2)}) %collective-permute-start.25) | collective-permute-done | bytes 16416 | tf_op jit(solution)/shard_map/ppermute | solution.py:198
  45.0 4.1 %collective-permute-start.28 = (f32[8,128]{1,0:T(8,128)S(1)}, f32[8,128]{1,0:T(8,128)S(1)}, u32[]{:S(2)}, u32[]{:S(2)}) collective-permute-start(f32[8,128]{1,0:T(8,128)S(1)} %get-tuple-element.40.square_ref), channel_id=1, source_target_pairs={{0,12},{1,13},{2,14},{3,15},{4,0},{5,1},{6,2},{7,3},{8,4},{9,5},{1... | collective-permute-start | bytes 12296 | tf_op jit(solution)/shard_map/ppermute | solution.py:198
  50.5 3.6 %collective-permute-done.27.z2 = f32[8,128]{1,0:T(8,128)S(1)} collective-permute-done((f32[8,128]{1,0:T(8,128)S(1)}, f32[8,128]{1,0:T(8,128)S(1)}, u32[]{:S(2)}, u32[]{:S(2)}) %collective-permute-start.27) | collective-permute-done | bytes 4128 | tf_op jit(solution)/shard_map/ppermute | solution.py:198
  54.2 3.0 %collective-permute-start.4 = (f32[32,6,8,128]{3,2,1,0:T(8,128)S(1)}, f32[32,6,8,128]{3,2,1,0:T(8,128)S(1)}, u32[]{:S(2)}, u32[]{:S(2)}) collective-permute-start(f32[32,6,8,128]{3,2,1,0:T(8,128)S(1)} %get-tuple-element.26), channel_id=1, source_target_pairs={{0,50},{1,49},{2,48},{3,51},{4,54},{5,53},{6,52},{7,55},{8,58},{9,... | collective-permute-start | bytes 2359304 | tf_op jit(solution)/shard_map/ppermute | solution.py:198
  59.1 3.5 %collective-permute-start.8 = (f32[32,6,8,128]{3,2,1,0:T(8,128)S(1)}, f32[32,6,8,128]{3,2,1,0:T(8,128)S(1)}, u32[]{:S(2)}, u32[]{:S(2)}) collective-permute-start(f32[32,6,8,128]{3,2,1,0:T(8,128)S(1)} %get-tuple-element.30), channel_id=1, source_target_pairs={{0,35},{1,34},{2,33},{3,32},{4,39},{5,38},{6,37},{7,36},{8,43},{9,... | collective-permute-start | bytes 2359304 | tf_op jit(solution)/shard_map/ppermute | solution.py:198
  62.5 12.9 %collective-permute-done.4.refs_4_ = f32[32,6,8,128]{3,2,1,0:T(8,128)S(1)} collective-permute-done((f32[32,6,8,128]{3,2,1,0:T(8,128)S(1)}, f32[32,6,8,128]{3,2,1,0:T(8,128)S(1)}, u32[]{:S(2)}, u32[]{:S(2)}) %collective-permute-start.4) | collective-permute-done | bytes 786464 | tf_op jit(solution)/shard_map/ppermute | solution.py:198
  76.1 15.1 %collective-permute-done.5.refs_5_ = f32[32,6,8,128]{3,2,1,0:T(8,128)S(1)} collective-permute-done((f32[32,6,8,128]{3,2,1,0:T(8,128)S(1)}, f32[32,6,8,128]{3,2,1,0:T(8,128)S(1)}, u32[]{:S(2)}, u32[]{:S(2)}) %collective-permute-start.5) | collective-permute-done | bytes 786464 | tf_op jit(solution)/shard_map/ppermute | solution.py:198
  91.2 3.4 %collective-permute-start.10 = (f32[32,6,8,128]{3,2,1,0:T(8,128)S(1)}, f32[32,6,8,128]{3,2,1,0:T(8,128)S(1)}, u32[]{:S(2)}, u32[]{:S(2)}) collective-permute-start(f32[32,6,8,128]{3,2,1,0:T(8,128)S(1)} %get-tuple-element.32), channel_id=1, source_target_pairs={{0,17},{1,18},{2,19},{3,16},{4,21},{5,22},{6,23},{7,20},{8,25},{9,... | collective-permute-start | bytes 2359304 | tf_op jit(solution)/shard_map/ppermute | solution.py:198
  94.6 13.5 %collective-permute-done.6.refs_6_ = f32[32,6,8,128]{3,2,1,0:T(8,128)S(1)} collective-permute-done((f32[32,6,8,128]{3,2,1,0:T(8,128)S(1)}, f32[32,6,8,128]{3,2,1,0:T(8,128)S(1)}, u32[]{:S(2)}, u32[]{:S(2)}) %collective-permute-start.6) | collective-permute-done | bytes 786464 | tf_op jit(solution)/shard_map/ppermute | solution.py:198
  108.1 3.4 %collective-permute-start.11 = (f32[32,6,8,128]{3,2,1,0:T(8,128)S(1)}, f32[32,6,8,128]{3,2,1,0:T(8,128)S(1)}, u32[]{:S(2)}, u32[]{:S(2)}) collective-permute-start(f32[32,6,8,128]{3,2,1,0:T(8,128)S(1)} %get-tuple-element.33), channel_id=1, source_target_pairs={{0,19},{1,16},{2,17},{3,18},{4,23},{5,20},{6,21},{7,22},{8,27},{9,... | collective-permute-start | bytes 2359304 | tf_op jit(solution)/shard_map/ppermute | solution.py:198
  111.5 13.5 %collective-permute-done.8.refs_8_ = f32[32,6,8,128]{3,2,1,0:T(8,128)S(1)} collective-permute-done((f32[32,6,8,128]{3,2,1,0:T(8,128)S(1)}, f32[32,6,8,128]{3,2,1,0:T(8,128)S(1)}, u32[]{:S(2)}, u32[]{:S(2)}) %collective-permute-start.8) | collective-permute-done | bytes 786464 | tf_op jit(solution)/shard_map/ppermute | solution.py:198
  124.9 19.1 %collective-permute-done.9.refs_0_ = f32[32,6,8,128]{3,2,1,0:T(8,128)S(1)} collective-permute-done((f32[32,6,8,128]{3,2,1,0:T(8,128)S(1)}, f32[32,6,8,128]{3,2,1,0:T(8,128)S(1)}, u32[]{:S(2)}, u32[]{:S(2)}) %collective-permute-start.9) | collective-permute-done | bytes 786464 | tf_op jit(solution)/shard_map/ppermute | solution.py:198
  144.0 3.2 %collective-permute-done.11.refs_0_ = f32[32,6,8,128]{3,2,1,0:T(8,128)S(1)} collective-permute-done((f32[32,6,8,128]{3,2,1,0:T(8,128)S(1)}, f32[32,6,8,128]{3,2,1,0:T(8,128)S(1)}, u32[]{:S(2)}, u32[]{:S(2)}) %collective-permute-start.11) | collective-permute-done | bytes 786464 | tf_op jit(solution)/shard_map/ppermute | solution.py:198
  147.2 25.9 %collective-permute-start.15 = (f32[16,6,8,128]{3,2,1,0:T(8,128)S(1)}, f32[16,6,8,128]{3,2,1,0:T(8,128)S(1)}, u32[]{:S(2)}, u32[]{:S(2)}) collective-permute-start(f32[16,6,8,128]{3,2,1,0:T(8,128)S(1)} %get-tuple-element.37), channel_id=1, source_target_pairs={{0,3},{1,2},{2,1},{3,0},{4,7},{5,6},{6,5},{7,4},{8,11},{9,10},{10,... | collective-permute-start | bytes 1179656 | tf_op jit(solution)/shard_map/ppermute | solution.py:198
  173.1 9.1 %collective-permute-start.16 = (f32[16,6,8,128]{3,2,1,0:T(8,128)S(1)}, f32[16,6,8,128]{3,2,1,0:T(8,128)S(1)}, u32[]{:S(2)}, u32[]{:S(2)}) collective-permute-start(f32[16,6,8,128]{3,2,1,0:T(8,128)S(1)} %get-tuple-element.38), channel_id=1, source_target_pairs={{0,33},{1,32},{2,35},{3,34},{4,37},{5,36},{6,39},{7,38},{8,41},{9,... | collective-permute-start | bytes 1179656 | tf_op jit(solution)/shard_map/ppermute | solution.py:198
  183.0 3.4 %shard_map.41._ = f32[2,4,16,6,4,8,128]{6,5,4,3,2,1,0:T(8,128)} custom-call(f32[2,8,16,6,2,8,128]{6,5,4,3,2,1,0:T(8,128)} %bitcast.13, f32[32,6,8,128]{3,2,1,0:T(8,128)S(1)} %collective-permute-done.refs_0_, f32[32,6,8,128]{3,2,1,0:T(8,128)S(1)} %collective-permute-done.1.refs_1_, f32[32,6,8,128]{3,2,1,0:T(8,128)S(1)} %collective-permute-done.2.refs_2_, ...), custom_call_target="tpu_custom_call" | custom-call | flops 50000000 | bytes 1048576 | tf_op jit(solution)/shard_map/pallas_call | solution.py:226
  (47 shorter events, 24.6 us)
Async XLA Ops:
  3.2 53.9 %collective-permute-start.2 = (f32[32,6,8,128]{3,2,1,0:T(8,128)S(1)}, f32[32,6,8,128]{3,2,1,0:T(8,128)S(1)}, u32[]{:S(2)}, u32[]{:S(2)}) collective-permute-start(f32[32,6,8,128]{3,2,1,0:T(8,128)S(1)} %shard_map.39.refs_0_), channel_id=1, source_target_pairs={{0,18},{1,17},{2,16},{3,19},{4,22},{5,21},{6,20},{7,23},{8,26},{9,... | collective-permute-start | bytes 2359304 | tf_op jit(solution)/shard_map/ppermute | solution.py:198
  3.7 55.4 %collective-permute-start.1 = (f32[32,6,8,128]{3,2,1,0:T(8,128)S(1)}, f32[32,6,8,128]{3,2,1,0:T(8,128)S(1)}, u32[]{:S(2)}, u32[]{:S(2)}) collective-permute-start(f32[32,6,8,128]{3,2,1,0:T(8,128)S(1)} %get-tuple-element.24), channel_id=1, source_target_pairs={{0,48},{1,51},{2,50},{3,49},{4,52},{5,55},{6,54},{7,53},{8,56},{9,... | collective-permute-start | bytes 2359304 | tf_op jit(solution)/shard_map/ppermute | solution.py:198
  6.3 52.8 %collective-permute-start = (f32[32,6,8,128]{3,2,1,0:T(8,128)S(1)}, f32[32,6,8,128]{3,2,1,0:T(8,128)S(1)}, u32[]{:S(2)}, u32[]{:S(2)}) collective-permute-start(f32[32,6,8,128]{3,2,1,0:T(8,128)S(1)} %get-tuple-element.23.refs_0_), channel_id=1, source_target_pairs={{0,16},{1,19},{2,18},{3,17},{4,20},{5,23},{6,22},{7,21},{8,24},{9,... | collective-permute-start | bytes 2359304 | tf_op jit(solution)/shard_map/ppermute | solution.py:198
  19.5 6.4 %collective-permute-start.24 = (f32[2,8,128]{2,1,0:T(8,128)S(1)}, f32[2,8,128]{2,1,0:T(8,128)S(1)}, u32[]{:S(2)}, u32[]{:S(2)}) collective-permute-start(f32[2,8,128]{2,1,0:T(8,128)S(1)} %shard_map.47.refs_0_), channel_id=1, source_target_pairs={{0,34},{1,35},{2,32},{3,33},{4,38},{5,39},{6,36},{7,37},{8,42},{9,... | collective-permute-start | bytes 24584 | tf_op jit(solution)/shard_map/ppermute | solution.py:198
  21.5 6.7 %collective-permute-start.23 = (f32[2,8,128]{2,1,0:T(8,128)S(1)}, f32[2,8,128]{2,1,0:T(8,128)S(1)}, u32[]{:S(2)}, u32[]{:S(2)}) collective-permute-start(f32[2,8,128]{2,1,0:T(8,128)S(1)} %shard_map.47.refs_0_), channel_id=1, source_target_pairs={{0,50},{1,49},{2,48},{3,51},{4,54},{5,53},{6,52},{7,55},{8,58},{9,... | collective-permute-start | bytes 24584 | tf_op jit(solution)/shard_map/ppermute | solution.py:198
  30.5 5.2 %collective-permute-start.20 = (f32[2,8,128]{2,1,0:T(8,128)S(1)}, f32[2,8,128]{2,1,0:T(8,128)S(1)}, u32[]{:S(2)}, u32[]{:S(2)}) collective-permute-start(f32[2,8,128]{2,1,0:T(8,128)S(1)} %shard_map.47.refs_0_), channel_id=1, source_target_pairs={{0,2},{1,3},{2,0},{3,1},{4,6},{5,7},{6,4},{7,5},{8,10},{9,11},{10,... | collective-permute-start | bytes 24584 | tf_op jit(solution)/shard_map/ppermute | solution.py:198
  32.3 5.7 %collective-permute-start.19 = (f32[2,8,128]{2,1,0:T(8,128)S(1)}, f32[2,8,128]{2,1,0:T(8,128)S(1)}, u32[]{:S(2)}, u32[]{:S(2)}) collective-permute-start(f32[2,8,128]{2,1,0:T(8,128)S(1)} %shard_map.47.refs_0_), channel_id=1, source_target_pairs={{0,18},{1,17},{2,16},{3,19},{4,22},{5,21},{6,20},{7,23},{8,26},{9,... | collective-permute-start | bytes 24584 | tf_op jit(solution)/shard_map/ppermute | solution.py:198
  45.0 5.4 %collective-permute-start.28 = (f32[8,128]{1,0:T(8,128)S(1)}, f32[8,128]{1,0:T(8,128)S(1)}, u32[]{:S(2)}, u32[]{:S(2)}) collective-permute-start(f32[8,128]{1,0:T(8,128)S(1)} %get-tuple-element.40.square_ref), channel_id=1, source_target_pairs={{0,12},{1,13},{2,14},{3,15},{4,0},{5,1},{6,2},{7,3},{8,4},{9,5},{1... | collective-permute-start | bytes 12296 | tf_op jit(solution)/shard_map/ppermute | solution.py:198
  49.1 5.1 %collective-permute-start.27 = (f32[8,128]{1,0:T(8,128)S(1)}, f32[8,128]{1,0:T(8,128)S(1)}, u32[]{:S(2)}, u32[]{:S(2)}) collective-permute-start(f32[8,128]{1,0:T(8,128)S(1)} %get-tuple-element.40.square_ref), channel_id=1, source_target_pairs={{0,8},{1,9},{2,10},{3,11},{4,12},{5,13},{6,14},{7,15},{8,0},{9,1},... | collective-permute-start | bytes 12296 | tf_op jit(solution)/shard_map/ppermute | solution.py:198
  50.4 6.7 %collective-permute-start.26 = (f32[8,128]{1,0:T(8,128)S(1)}, f32[8,128]{1,0:T(8,128)S(1)}, u32[]{:S(2)}, u32[]{:S(2)}) collective-permute-start(f32[8,128]{1,0:T(8,128)S(1)} %get-tuple-element.40.square_ref), channel_id=1, source_target_pairs={{0,4},{1,5},{2,6},{3,7},{4,8},{5,9},{6,10},{7,11},{8,12},{9,13},{1... | collective-permute-start | bytes 12296 | tf_op jit(solution)/shard_map/ppermute | solution.py:198
  54.2 21.3 %collective-permute-start.4 = (f32[32,6,8,128]{3,2,1,0:T(8,128)S(1)}, f32[32,6,8,128]{3,2,1,0:T(8,128)S(1)}, u32[]{:S(2)}, u32[]{:S(2)}) collective-permute-start(f32[32,6,8,128]{3,2,1,0:T(8,128)S(1)} %get-tuple-element.26), channel_id=1, source_target_pairs={{0,50},{1,49},{2,48},{3,51},{4,54},{5,53},{6,52},{7,55},{8,58},{9,... | collective-permute-start | bytes 2359304 | tf_op jit(solution)/shard_map/ppermute | solution.py:198
  57.1 34.1 %collective-permute-start.5 = (f32[32,6,8,128]{3,2,1,0:T(8,128)S(1)}, f32[32,6,8,128]{3,2,1,0:T(8,128)S(1)}, u32[]{:S(2)}, u32[]{:S(2)}) collective-permute-start(f32[32,6,8,128]{3,2,1,0:T(8,128)S(1)} %get-tuple-element.27), channel_id=1, source_target_pairs={{0,49},{1,50},{2,51},{3,48},{4,53},{5,54},{6,55},{7,52},{8,57},{9,... | collective-permute-start | bytes 2359304 | tf_op jit(solution)/shard_map/ppermute | solution.py:198
  57.1 51.0 %collective-permute-start.6 = (f32[32,6,8,128]{3,2,1,0:T(8,128)S(1)}, f32[32,6,8,128]{3,2,1,0:T(8,128)S(1)}, u32[]{:S(2)}, u32[]{:S(2)}) collective-permute-start(f32[32,6,8,128]{3,2,1,0:T(8,128)S(1)} %get-tuple-element.28), channel_id=1, source_target_pairs={{0,51},{1,48},{2,49},{3,50},{4,55},{5,52},{6,53},{7,54},{8,59},{9,... | collective-permute-start | bytes 2359304 | tf_op jit(solution)/shard_map/ppermute | solution.py:198
  59.1 52.4 %collective-permute-start.7 = (f32[32,6,8,128]{3,2,1,0:T(8,128)S(1)}, f32[32,6,8,128]{3,2,1,0:T(8,128)S(1)}, u32[]{:S(2)}, u32[]{:S(2)}) collective-permute-start(f32[32,6,8,128]{3,2,1,0:T(8,128)S(1)} %get-tuple-element.29), channel_id=1, source_target_pairs={{0,1},{1,0},{2,3},{3,2},{4,5},{5,4},{6,7},{7,6},{8,9},{9,8},{10,11... | collective-permute-start | bytes 2359304 | tf_op jit(solution)/shard_map/ppermute | solution.py:198
  59.1 65.9 %collective-permute-start.8 = (f32[32,6,8,128]{3,2,1,0:T(8,128)S(1)}, f32[32,6,8,128]{3,2,1,0:T(8,128)S(1)}, u32[]{:S(2)}, u32[]{:S(2)}) collective-permute-start(f32[32,6,8,128]{3,2,1,0:T(8,128)S(1)} %get-tuple-element.30), channel_id=1, source_target_pairs={{0,35},{1,34},{2,33},{3,32},{4,39},{5,38},{6,37},{7,36},{8,43},{9,... | collective-permute-start | bytes 2359304 | tf_op jit(solution)/shard_map/ppermute | solution.py:198
  75.5 68.5 %collective-permute-start.9 = (f32[32,6,8,128]{3,2,1,0:T(8,128)S(1)}, f32[32,6,8,128]{3,2,1,0:T(8,128)S(1)}, u32[]{:S(2)}, u32[]{:S(2)}) collective-permute-start(f32[32,6,8,128]{3,2,1,0:T(8,128)S(1)} %get-tuple-element.31), channel_id=1, source_target_pairs={{0,32},{1,33},{2,34},{3,35},{4,36},{5,37},{6,38},{7,39},{8,40},{9,... | collective-permute-start | bytes 2359304 | tf_op jit(solution)/shard_map/ppermute | solution.py:198
  91.2 52.8 %collective-permute-start.10 = (f32[32,6,8,128]{3,2,1,0:T(8,128)S(1)}, f32[32,6,8,128]{3,2,1,0:T(8,128)S(1)}, u32[]{:S(2)}, u32[]{:S(2)}) collective-permute-start(f32[32,6,8,128]{3,2,1,0:T(8,128)S(1)} %get-tuple-element.32), channel_id=1, source_target_pairs={{0,17},{1,18},{2,19},{3,16},{4,21},{5,22},{6,23},{7,20},{8,25},{9,... | collective-permute-start | bytes 2359304 | tf_op jit(solution)/shard_map/ppermute | solution.py:198
  108.1 39.2 %collective-permute-start.11 = (f32[32,6,8,128]{3,2,1,0:T(8,128)S(1)}, f32[32,6,8,128]{3,2,1,0:T(8,128)S(1)}, u32[]{:S(2)}, u32[]{:S(2)}) collective-permute-start(f32[32,6,8,128]{3,2,1,0:T(8,128)S(1)} %get-tuple-element.33), channel_id=1, source_target_pairs={{0,19},{1,16},{2,17},{3,18},{4,23},{5,20},{6,21},{7,22},{8,27},{9,... | collective-permute-start | bytes 2359304 | tf_op jit(solution)/shard_map/ppermute | solution.py:198
  111.5 61.7 %collective-permute-start.3 = (f32[32,6,8,128]{3,2,1,0:T(8,128)S(1)}, f32[32,6,8,128]{3,2,1,0:T(8,128)S(1)}, u32[]{:S(2)}, u32[]{:S(2)}) collective-permute-start(f32[32,6,8,128]{3,2,1,0:T(8,128)S(1)} %get-tuple-element.25._), channel_id=1, source_target_pairs={{0,34},{1,35},{2,32},{3,33},{4,38},{5,39},{6,36},{7,37},{8,42},{9,... | collective-permute-start | bytes 2359304 | tf_op jit(solution)/shard_map/ppermute | solution.py:198
  124.9 62.6 %collective-permute-start.12 = (f32[32,6,8,128]{3,2,1,0:T(8,128)S(1)}, f32[32,6,8,128]{3,2,1,0:T(8,128)S(1)}, u32[]{:S(2)}, u32[]{:S(2)}) collective-permute-start(f32[32,6,8,128]{3,2,1,0:T(8,128)S(1)} %get-tuple-element.34), channel_id=1, source_target_pairs={{0,2},{1,3},{2,0},{3,1},{4,6},{5,7},{6,4},{7,5},{8,10},{9,11},{10,... | collective-permute-start | bytes 2359304 | tf_op jit(solution)/shard_map/ppermute | solution.py:198
  144.0 44.8 %collective-permute-start.13 = (f32[16,6,8,128]{3,2,1,0:T(8,128)S(1)}, f32[16,6,8,128]{3,2,1,0:T(8,128)S(1)}, u32[]{:S(2)}, u32[]{:S(2)}) collective-permute-start(f32[16,6,8,128]{3,2,1,0:T(8,128)S(1)} %get-tuple-element.35), channel_id=1, source_target_pairs={{0,3},{1,2},{2,1},{3,0},{4,7},{5,6},{6,5},{7,4},{8,11},{9,10},{10,... | collective-permute-start | bytes 1179656 | tf_op jit(solution)/shard_map/ppermute | solution.py:198
  144.0 44.8 %collective-permute-start.14 = (f32[16,6,8,128]{3,2,1,0:T(8,128)S(1)}, f32[16,6,8,128]{3,2,1,0:T(8,128)S(1)}, u32[]{:S(2)}, u32[]{:S(2)}) collective-permute-start(f32[16,6,8,128]{3,2,1,0:T(8,128)S(1)} %get-tuple-element.36), channel_id=1, source_target_pairs={{0,33},{1,32},{2,35},{3,34},{4,37},{5,36},{6,39},{7,38},{8,41},{9,... | collective-permute-start | bytes 1179656 | tf_op jit(solution)/shard_map/ppermute | solution.py:198
  147.2 42.6 %collective-permute-start.15 = (f32[16,6,8,128]{3,2,1,0:T(8,128)S(1)}, f32[16,6,8,128]{3,2,1,0:T(8,128)S(1)}, u32[]{:S(2)}, u32[]{:S(2)}) collective-permute-start(f32[16,6,8,128]{3,2,1,0:T(8,128)S(1)} %get-tuple-element.37), channel_id=1, source_target_pairs={{0,3},{1,2},{2,1},{3,0},{4,7},{5,6},{6,5},{7,4},{8,11},{9,10},{10,... | collective-permute-start | bytes 1179656 | tf_op jit(solution)/shard_map/ppermute | solution.py:198
  173.1 16.7 %collective-permute-start.16 = (f32[16,6,8,128]{3,2,1,0:T(8,128)S(1)}, f32[16,6,8,128]{3,2,1,0:T(8,128)S(1)}, u32[]{:S(2)}, u32[]{:S(2)}) collective-permute-start(f32[16,6,8,128]{3,2,1,0:T(8,128)S(1)} %get-tuple-element.38), channel_id=1, source_target_pairs={{0,33},{1,32},{2,35},{3,34},{4,37},{5,36},{6,39},{7,38},{8,41},{9,... | collective-permute-start | bytes 1179656 | tf_op jit(solution)/shard_map/ppermute | solution.py:198
  (5 other events, 19.2 us)

commit v6 on v5

--- a/solution.py
+++ b/solution.py
@@ -14,11 +14,11 @@
 HALVES, ROW_PARTS, TILES, E, COL_PARTS = 2, 4, 16, 6, 4
 F32 = jnp.float32
 WHOLE, UPPER, LOWER = (0, 1), (0,), (1,)
-FIRST = [(0, 1, 0, WHOLE), (1, 1, 0, WHOLE)]
-SECOND = [(0, 3, 0, WHOLE)]
-THIRD = [(1, 2, 0, WHOLE), (1, 3, 0, WHOLE), (0, 1, 1, WHOLE), (0, 3, 1, WHOLE), (1, 1, 1, WHOLE), (0, 2, 0, WHOLE), (0, 2, 1, UPPER), (1, 3, 1, WHOLE), (0, 2, 1, LOWER), (0, 0, 1, WHOLE), (1, 2, 1, WHOLE), (1, 0, 0, WHOLE), (1, 0, 1, UPPER), (1, 0, 1, LOWER)]
+FIRST = [(0, 1, 0, UPPER), (1, 1, 0, UPPER)]
+SECOND = [(0, 3, 0, WHOLE), (1, 1, 0, LOWER), (0, 1, 0, LOWER)]
+THIRD = [(1, 2, 0, WHOLE), (1, 3, 0, WHOLE), (0, 1, 1, WHOLE), (0, 3, 1, WHOLE), (1, 1, 1, WHOLE), (0, 2, 0, WHOLE), (0, 2, 1, UPPER), (1, 3, 1, WHOLE), (0, 2, 1, LOWER), (0, 0, 1, WHOLE), (1, 2, 1, WHOLE), (1, 0, 1, WHOLE), (1, 0, 0, UPPER), (1, 0, 0, LOWER)]
 NEAR = [(0, 1, 0), (0, 3, 0), (0, 2, 0), (1, 0, 0), (1, 1, 0), (1, 3, 0), (1, 2, 0)]
-GROUPS = [[(1, 0, 0, WHOLE), (0, 1, 1, WHOLE)], [(0, 3, 1, WHOLE), (0, 2, 0, WHOLE)], [(0, 2, 1, UPPER), (1, 0, 1, UPPER)], [(0, 2, 1, LOWER), (1, 0, 1, LOWER)]]
+GROUPS = [[(1, 0, 1, WHOLE), (0, 1, 1, WHOLE)], [(0, 3, 1, WHOLE), (0, 2, 0, WHOLE)], [(0, 2, 1, UPPER), (1, 0, 0, UPPER)], [(0, 2, 1, LOWER), (1, 0, 0, LOWER)]]
 SOON = [f for f in FIRST + SECOND + THIRD if f not in sum(GROUPS, [])]
 SLOTS = 4
 CHUNKS = HALVES * 8

time: 193 us -> 195 us (1.010)
  starting transfers between devices: 78.5 us -> 97.8 us
  waiting for transfers between devices: 90.1 us -> 74.1 us
    ppermute x29 -> x31, starting transfers between devices: 78.5 us -> 97.8 us  [permute(): return lax.ppermute(value, AXES, pairs)]
    ppermute x29 -> x31, waiting for transfers between devices: 90.1 us -> 74.1 us  [permute(): return lax.ppermute(value, AXES, pairs)]
  transfers between devices with their start and end apart: 29 -> 31, of which waited for: 14 -> 14; matrix products, arithmetic and copies ran while one was open for 0% -> 0% of each run, Pallas kernels for 9% -> 4%
where the time goes in v6:
time: 195 us; the launch traced here: 194 us
  starting transfers between devices  97.8 us (50%)
  waiting for transfers between devices  74.1 us (38%)
  Pallas kernels  21.6 us (11%)
    ppermute x31, starting transfers between devices, permute(): return lax.ppermute(value, AXES, pairs)  97.8 us
    ppermute x31, waiting for transfers between devices, permute(): return lax.ppermute(value, AXES, pairs)  74.1 us
    pallas_call x3, Pallas kernels, go(): plain(functools.partial(pack, flows), tuple((pltpu.VMEM((len(f[3]) * TILE...  6.62 us
    pallas_call x1, Pallas kernels, body(): plain(reduce, tiles((2, *SMALL)), [HBM, VMEM], VMEM, [pltpu.VMEM((SLOTS,...  6.5 us
    pallas_call x4, Pallas kernels, body(): plain(functools.partial(write_group, flows), jax.ShapeDtypeStruct(BIG, F3...  4.34 us
  transfers between devices with their start and end apart: 31, of which 14 were waited for; matrix products, arithmetic and copies ran while one was open for 0% of the time, Pallas kernels for 4%

profile of v6, /device:TPU:8, one launch (start us, length us, event | category | flops | bytes accessed | tf_op | source)
XLA Modules:
  0.0 194.2 jit_solution(13092608450801065665)
XLA Ops:
  3.3 4.0 %shard_map.40 = (f32[32,6,8,128]{3,2,1,0:T(8,128)S(1)}, f32[32,6,8,128]{3,2,1,0:T(8,128)S(1)}, f32[32,6,8,128]{3,2,1,0:T(8,128)S(1)}, f32[32,6,8,128]{3,2,1,0:T(...) custom-call(f32[2,8,16,6,2,8,128]{6,5,4,3,2,1,0:T(8,128)} %bitcast.1, ...), custom_call_target="tpu_custom_call" | custom-call | flops 56666664 | bytes 1048576 | tf_op jit(solution)/shard_map/pallas_call | solution.py:202
  7.3 6.5 %shard_map.46.part = f32[2,8,128]{2,1,0:T(8,128)S(1)} custom-call(f32[2,8,16,6,2,8,128]{6,5,4,3,2,1,0:T(8,128)} %bitcast.12, f32[32,6,8,128]{3,2,1,0:T(8,128)S(1)} %get-tuple-element.31._), custom_call_target="tpu_custom_call" | custom-call | flops 70000000 | bytes 1048576 | tf_op jit(solution)/shard_map/pallas_call | solution.py:213
  15.0 3.2 %collective-permute-start.26 = (f32[2,8,128]{2,1,0:T(8,128)S(1)}, f32[2,8,128]{2,1,0:T(8,128)S(1)}, u32[]{:S(2)}, u32[]{:S(2)}) collective-permute-start(f32[2,8,128]{2,1,0:T(8,128)S(1)} %shard_map.47.refs_0_), channel_id=1, source_target_pairs={{0,34},{1,35},{2,32},{3,33},{4,38},{5,39},{6,36},{7,37},{8,42},{9,... | collective-permute-start | bytes 24584 | tf_op jit(solution)/shard_map/ppermute | solution.py:198
  21.7 2.4 %collective-permute-start.22 = (f32[2,8,128]{2,1,0:T(8,128)S(1)}, f32[2,8,128]{2,1,0:T(8,128)S(1)}, u32[]{:S(2)}, u32[]{:S(2)}) collective-permute-start(f32[2,8,128]{2,1,0:T(8,128)S(1)} %shard_map.47.refs_0_), channel_id=1, source_target_pairs={{0,2},{1,3},{2,0},{3,1},{4,6},{5,7},{6,4},{7,5},{8,10},{9,11},{10,... | collective-permute-start | bytes 24584 | tf_op jit(solution)/shard_map/ppermute | solution.py:198
  24.2 2.0 %collective-permute-start.20 = (f32[2,8,128]{2,1,0:T(8,128)S(1)}, f32[2,8,128]{2,1,0:T(8,128)S(1)}, u32[]{:S(2)}, u32[]{:S(2)}) collective-permute-start(f32[2,8,128]{2,1,0:T(8,128)S(1)} %shard_map.47.refs_0_), channel_id=1, source_target_pairs={{0,16},{1,19},{2,18},{3,17},{4,20},{5,23},{6,22},{7,21},{8,24},{9,... | collective-permute-start | bytes 24584 | tf_op jit(solution)/shard_map/ppermute | solution.py:198
  28.1 2.8 %collective-permute-start.27 = (f32[4,8,128]{2,1,0:T(8,128)S(1)}, f32[4,8,128]{2,1,0:T(8,128)S(1)}, u32[]{:S(2)}, u32[]{:S(2)}) collective-permute-start(f32[4,8,128]{2,1,0:T(8,128)S(1)} %shard_map.48.plane_ref), channel_id=1, source_target_pairs={{0,96},{1,97},{2,98},{3,99},{4,100},{5,101},{6,102},{7,103},{8,104... | collective-permute-start | bytes 49160 | tf_op jit(solution)/shard_map/ppermute | solution.py:198
  30.9 2.2 %collective-permute-done.27.other_ref = f32[4,8,128]{2,1,0:T(8,128)S(1)} collective-permute-done((f32[4,8,128]{2,1,0:T(8,128)S(1)}, f32[4,8,128]{2,1,0:T(8,128)S(1)}, u32[]{:S(2)}, u32[]{:S(2)}) %collective-permute-start.27) | collective-permute-done | bytes 16416 | tf_op jit(solution)/shard_map/ppermute | solution.py:198
  33.1 4.1 %collective-permute-start.30 = (f32[8,128]{1,0:T(8,128)S(1)}, f32[8,128]{1,0:T(8,128)S(1)}, u32[]{:S(2)}, u32[]{:S(2)}) collective-permute-start(f32[8,128]{1,0:T(8,128)S(1)} %get-tuple-element.46.square_ref), channel_id=1, source_target_pairs={{0,12},{1,13},{2,14},{3,15},{4,0},{5,1},{6,2},{7,3},{8,4},{9,5},{1... | collective-permute-start | bytes 12296 | tf_op jit(solution)/shard_map/ppermute | solution.py:198
  38.5 3.2 %collective-permute-start.2 = (f32[32,6,8,128]{3,2,1,0:T(8,128)S(1)}, f32[32,6,8,128]{3,2,1,0:T(8,128)S(1)}, u32[]{:S(2)}, u32[]{:S(2)}) collective-permute-start(f32[32,6,8,128]{3,2,1,0:T(8,128)S(1)} %get-tuple-element.28.refs_0_), channel_id=1, source_target_pairs={{0,18},{1,17},{2,16},{3,19},{4,22},{5,21},{6,20},{7,23},{8,26},{9,... | collective-permute-start | bytes 2359304 | tf_op jit(solution)/shard_map/ppermute | solution.py:198
  42.3 2.9 %collective-permute-start.3 = (f32[16,6,8,128]{3,2,1,0:T(8,128)S(1)}, f32[16,6,8,128]{3,2,1,0:T(8,128)S(1)}, u32[]{:S(2)}, u32[]{:S(2)}) collective-permute-start(f32[16,6,8,128]{3,2,1,0:T(8,128)S(1)} %get-tuple-element.29), channel_id=1, source_target_pairs={{0,48},{1,51},{2,50},{3,49},{4,52},{5,55},{6,54},{7,53},{8,56},{9,... | collective-permute-start | bytes 1179656 | tf_op jit(solution)/shard_map/ppermute | solution.py:198
  47.3 7.4 %collective-permute-done.1.refs_1_ = f32[16,6,8,128]{3,2,1,0:T(8,128)S(1)} collective-permute-done((f32[16,6,8,128]{3,2,1,0:T(8,128)S(1)}, f32[16,6,8,128]{3,2,1,0:T(8,128)S(1)}, u32[]{:S(2)}, u32[]{:S(2)}) %collective-permute-start.1) | collective-permute-done | bytes 393248 | tf_op jit(solution)/shard_map/ppermute | solution.py:198
  55.7 11.0 %collective-permute-done.refs_0_ = f32[16,6,8,128]{3,2,1,0:T(8,128)S(1)} collective-permute-done((f32[16,6,8,128]{3,2,1,0:T(8,128)S(1)}, f32[16,6,8,128]{3,2,1,0:T(8,128)S(1)}, u32[]{:S(2)}, u32[]{:S(2)}) %collective-permute-start) | collective-permute-done | bytes 393248 | tf_op jit(solution)/shard_map/ppermute | solution.py:198
  66.7 4.8 %collective-permute-start.8 = (f32[32,6,8,128]{3,2,1,0:T(8,128)S(1)}, f32[32,6,8,128]{3,2,1,0:T(8,128)S(1)}, u32[]{:S(2)}, u32[]{:S(2)}) collective-permute-start(f32[32,6,8,128]{3,2,1,0:T(8,128)S(1)} %get-tuple-element.34), channel_id=1, source_target_pairs={{0,51},{1,48},{2,49},{3,50},{4,55},{5,52},{6,53},{7,54},{8,59},{9,... | collective-permute-start | bytes 2359304 | tf_op jit(solution)/shard_map/ppermute | solution.py:198
  75.1 14.2 %collective-permute-done.7.refs_7_ = f32[32,6,8,128]{3,2,1,0:T(8,128)S(1)} collective-permute-done((f32[32,6,8,128]{3,2,1,0:T(8,128)S(1)}, f32[32,6,8,128]{3,2,1,0:T(8,128)S(1)}, u32[]{:S(2)}, u32[]{:S(2)}) %collective-permute-start.7) | collective-permute-done | bytes 786464 | tf_op jit(solution)/shard_map/ppermute | solution.py:198
  89.3 4.2 %collective-permute-start.12 = (f32[32,6,8,128]{3,2,1,0:T(8,128)S(1)}, f32[32,6,8,128]{3,2,1,0:T(8,128)S(1)}, u32[]{:S(2)}, u32[]{:S(2)}) collective-permute-start(f32[32,6,8,128]{3,2,1,0:T(8,128)S(1)} %get-tuple-element.38), channel_id=1, source_target_pairs={{0,17},{1,18},{2,19},{3,16},{4,21},{5,22},{6,23},{7,20},{8,25},{9,... | collective-permute-start | bytes 2359304 | tf_op jit(solution)/shard_map/ppermute | solution.py:198
  93.5 12.9 %collective-permute-done.8.refs_8_ = f32[32,6,8,128]{3,2,1,0:T(8,128)S(1)} collective-permute-done((f32[32,6,8,128]{3,2,1,0:T(8,128)S(1)}, f32[32,6,8,128]{3,2,1,0:T(8,128)S(1)}, u32[]{:S(2)}, u32[]{:S(2)}) %collective-permute-start.8) | collective-permute-done | bytes 786464 | tf_op jit(solution)/shard_map/ppermute | solution.py:198
  106.4 4.0 %collective-permute-start.13 = (f32[32,6,8,128]{3,2,1,0:T(8,128)S(1)}, f32[32,6,8,128]{3,2,1,0:T(8,128)S(1)}, u32[]{:S(2)}, u32[]{:S(2)}) collective-permute-start(f32[32,6,8,128]{3,2,1,0:T(8,128)S(1)} %get-tuple-element.39), channel_id=1, source_target_pairs={{0,19},{1,16},{2,17},{3,18},{4,23},{5,20},{6,21},{7,22},{8,27},{9,... | collective-permute-start | bytes 2359304 | tf_op jit(solution)/shard_map/ppermute | solution.py:198
  110.4 3.7 %collective-permute-start.5 = (f32[32,6,8,128]{3,2,1,0:T(8,128)S(1)}, f32[32,6,8,128]{3,2,1,0:T(8,128)S(1)}, u32[]{:S(2)}, u32[]{:S(2)}) collective-permute-start(f32[32,6,8,128]{3,2,1,0:T(8,128)S(1)} %get-tuple-element.31._), channel_id=1, source_target_pairs={{0,34},{1,35},{2,32},{3,33},{4,38},{5,39},{6,36},{7,37},{8,42},{9,... | collective-permute-start | bytes 2359304 | tf_op jit(solution)/shard_map/ppermute | solution.py:198
  114.1 9.2 %collective-permute-done.10.refs_10_ = f32[32,6,8,128]{3,2,1,0:T(8,128)S(1)} collective-permute-done((f32[32,6,8,128]{3,2,1,0:T(8,128)S(1)}, f32[32,6,8,128]{3,2,1,0:T(8,128)S(1)}, u32[]{:S(2)}, u32[]{:S(2)}) %collective-permute-start.10) | collective-permute-done | bytes 786464 | tf_op jit(solution)/shard_map/ppermute | solution.py:198
  123.3 4.6 %collective-permute-start.14 = (f32[32,6,8,128]{3,2,1,0:T(8,128)S(1)}, f32[32,6,8,128]{3,2,1,0:T(8,128)S(1)}, u32[]{:S(2)}, u32[]{:S(2)}) collective-permute-start(f32[32,6,8,128]{3,2,1,0:T(8,128)S(1)} %get-tuple-element.40), channel_id=1, source_target_pairs={{0,2},{1,3},{2,0},{3,1},{4,6},{5,7},{6,4},{7,5},{8,10},{9,11},{10,... | collective-permute-start | bytes 2359304 | tf_op jit(solution)/shard_map/ppermute | solution.py:198
  127.9 12.3 %collective-permute-done.11.refs_0_ = f32[32,6,8,128]{3,2,1,0:T(8,128)S(1)} collective-permute-done((f32[32,6,8,128]{3,2,1,0:T(8,128)S(1)}, f32[32,6,8,128]{3,2,1,0:T(8,128)S(1)}, u32[]{:S(2)}, u32[]{:S(2)}) %collective-permute-start.11) | collective-permute-done | bytes 786464 | tf_op jit(solution)/shard_map/ppermute | solution.py:198
  140.2 5.7 %collective-permute-start.15 = (f32[16,6,8,128]{3,2,1,0:T(8,128)S(1)}, f32[16,6,8,128]{3,2,1,0:T(8,128)S(1)}, u32[]{:S(2)}, u32[]{:S(2)}) collective-permute-start(f32[16,6,8,128]{3,2,1,0:T(8,128)S(1)} %get-tuple-element.41), channel_id=1, source_target_pairs={{0,3},{1,2},{2,1},{3,0},{4,7},{5,6},{6,5},{7,4},{8,11},{9,10},{10,... | collective-permute-start | bytes 1179656 | tf_op jit(solution)/shard_map/ppermute | solution.py:198
  146.9 37.8 %collective-permute-start.17 = (f32[16,6,8,128]{3,2,1,0:T(8,128)S(1)}, f32[16,6,8,128]{3,2,1,0:T(8,128)S(1)}, u32[]{:S(2)}, u32[]{:S(2)}) collective-permute-start(f32[16,6,8,128]{3,2,1,0:T(8,128)S(1)} %get-tuple-element.43), channel_id=1, source_target_pairs={{0,3},{1,2},{2,1},{3,0},{4,7},{5,6},{6,5},{7,4},{8,11},{9,10},{10,... | collective-permute-start | bytes 1179656 | tf_op jit(solution)/shard_map/ppermute | solution.py:198
  186.4 3.4 %shard_map.41._ = f32[2,4,16,6,4,8,128]{6,5,4,3,2,1,0:T(8,128)} custom-call(f32[2,8,16,6,2,8,128]{6,5,4,3,2,1,0:T(8,128)} %bitcast.13, f32[16,6,8,128]{3,2,1,0:T(8,128)S(1)} %collective-permute-done.refs_0_, f32[16,6,8,128]{3,2,1,0:T(8,128)S(1)} %collective-permute-done.1.refs_1_, f32[32,6,8,128]{3,2,1,0:T(8,128)S(1)} %collective-permute-done.2.refs_2_, ...), custom_call_target="tpu_custom_call" | custom-call | flops 50000000 | bytes 1048576 | tf_op jit(solution)/shard_map/pallas_call | solution.py:226
  (51 shorter events, 24.7 us)
Async XLA Ops:
  15.0 9.1 %collective-permute-start.26 = (f32[2,8,128]{2,1,0:T(8,128)S(1)}, f32[2,8,128]{2,1,0:T(8,128)S(1)}, u32[]{:S(2)}, u32[]{:S(2)}) collective-permute-start(f32[2,8,128]{2,1,0:T(8,128)S(1)} %shard_map.47.refs_0_), channel_id=1, source_target_pairs={{0,34},{1,35},{2,32},{3,33},{4,38},{5,39},{6,36},{7,37},{8,42},{9,... | collective-permute-start | bytes 24584 | tf_op jit(solution)/shard_map/ppermute | solution.py:198
  18.3 5.9 %collective-permute-start.25 = (f32[2,8,128]{2,1,0:T(8,128)S(1)}, f32[2,8,128]{2,1,0:T(8,128)S(1)}, u32[]{:S(2)}, u32[]{:S(2)}) collective-permute-start(f32[2,8,128]{2,1,0:T(8,128)S(1)} %shard_map.47.refs_0_), channel_id=1, source_target_pairs={{0,50},{1,49},{2,48},{3,51},{4,54},{5,53},{6,52},{7,55},{8,58},{9,... | collective-permute-start | bytes 24584 | tf_op jit(solution)/shard_map/ppermute | solution.py:198
  19.6 6.6 %collective-permute-start.24 = (f32[2,8,128]{2,1,0:T(8,128)S(1)}, f32[2,8,128]{2,1,0:T(8,128)S(1)}, u32[]{:S(2)}, u32[]{:S(2)}) collective-permute-start(f32[2,8,128]{2,1,0:T(8,128)S(1)} %shard_map.47.refs_0_), channel_id=1, source_target_pairs={{0,48},{1,51},{2,50},{3,49},{4,52},{5,55},{6,54},{7,53},{8,56},{9,... | collective-permute-start | bytes 24584 | tf_op jit(solution)/shard_map/ppermute | solution.py:198
  33.1 8.6 %collective-permute-start.30 = (f32[8,128]{1,0:T(8,128)S(1)}, f32[8,128]{1,0:T(8,128)S(1)}, u32[]{:S(2)}, u32[]{:S(2)}) collective-permute-start(f32[8,128]{1,0:T(8,128)S(1)} %get-tuple-element.46.square_ref), channel_id=1, source_target_pairs={{0,12},{1,13},{2,14},{3,15},{4,0},{5,1},{6,2},{7,3},{8,4},{9,5},{1... | collective-permute-start | bytes 12296 | tf_op jit(solution)/shard_map/ppermute | solution.py:198
  37.2 8.1 %collective-permute-start.28 = (f32[8,128]{1,0:T(8,128)S(1)}, f32[8,128]{1,0:T(8,128)S(1)}, u32[]{:S(2)}, u32[]{:S(2)}) collective-permute-start(f32[8,128]{1,0:T(8,128)S(1)} %get-tuple-element.46.square_ref), channel_id=1, source_target_pairs={{0,4},{1,5},{2,6},{3,7},{4,8},{5,9},{6,10},{7,11},{8,12},{9,13},{1... | collective-permute-start | bytes 12296 | tf_op jit(solution)/shard_map/ppermute | solution.py:198
  38.5 33.3 %collective-permute-start.2 = (f32[32,6,8,128]{3,2,1,0:T(8,128)S(1)}, f32[32,6,8,128]{3,2,1,0:T(8,128)S(1)}, u32[]{:S(2)}, u32[]{:S(2)}) collective-permute-start(f32[32,6,8,128]{3,2,1,0:T(8,128)S(1)} %get-tuple-element.28.refs_0_), channel_id=1, source_target_pairs={{0,18},{1,17},{2,16},{3,19},{4,22},{5,21},{6,20},{7,23},{8,26},{9,... | collective-permute-start | bytes 2359304 | tf_op jit(solution)/shard_map/ppermute | solution.py:198
  41.7 13.0 %collective-permute-start.1 = (f32[16,6,8,128]{3,2,1,0:T(8,128)S(1)}, f32[16,6,8,128]{3,2,1,0:T(8,128)S(1)}, u32[]{:S(2)}, u32[]{:S(2)}) collective-permute-start(f32[16,6,8,128]{3,2,1,0:T(8,128)S(1)} %get-tuple-element.27), channel_id=1, source_target_pairs={{0,48},{1,51},{2,50},{3,49},{4,52},{5,55},{6,54},{7,53},{8,56},{9,... | collective-permute-start | bytes 1179656 | tf_op jit(solution)/shard_map/ppermute | solution.py:198
  41.7 24.9 %collective-permute-start = (f32[16,6,8,128]{3,2,1,0:T(8,128)S(1)}, f32[16,6,8,128]{3,2,1,0:T(8,128)S(1)}, u32[]{:S(2)}, u32[]{:S(2)}) collective-permute-start(f32[16,6,8,128]{3,2,1,0:T(8,128)S(1)} %get-tuple-element.26.refs_0_), channel_id=1, source_target_pairs={{0,16},{1,19},{2,18},{3,17},{4,20},{5,23},{6,22},{7,21},{8,24},{9,... | collective-permute-start | bytes 1179656 | tf_op jit(solution)/shard_map/ppermute | solution.py:198
  42.3 24.3 %collective-permute-start.3 = (f32[16,6,8,128]{3,2,1,0:T(8,128)S(1)}, f32[16,6,8,128]{3,2,1,0:T(8,128)S(1)}, u32[]{:S(2)}, u32[]{:S(2)}) collective-permute-start(f32[16,6,8,128]{3,2,1,0:T(8,128)S(1)} %get-tuple-element.29), channel_id=1, source_target_pairs={{0,48},{1,51},{2,50},{3,49},{4,52},{5,55},{6,54},{7,53},{8,56},{9,... | collective-permute-start | bytes 1179656 | tf_op jit(solution)/shard_map/ppermute | solution.py:198
  45.3 26.4 %collective-permute-start.4 = (f32[16,6,8,128]{3,2,1,0:T(8,128)S(1)}, f32[16,6,8,128]{3,2,1,0:T(8,128)S(1)}, u32[]{:S(2)}, u32[]{:S(2)}) collective-permute-start(f32[16,6,8,128]{3,2,1,0:T(8,128)S(1)} %get-tuple-element.30), channel_id=1, source_target_pairs={{0,16},{1,19},{2,18},{3,17},{4,20},{5,23},{6,22},{7,21},{8,24},{9,... | collective-permute-start | bytes 1179656 | tf_op jit(solution)/shard_map/ppermute | solution.py:198
  54.7 20.2 %collective-permute-start.6 = (f32[32,6,8,128]{3,2,1,0:T(8,128)S(1)}, f32[32,6,8,128]{3,2,1,0:T(8,128)S(1)}, u32[]{:S(2)}, u32[]{:S(2)}) collective-permute-start(f32[32,6,8,128]{3,2,1,0:T(8,128)S(1)} %get-tuple-element.32), channel_id=1, source_target_pairs={{0,50},{1,49},{2,48},{3,51},{4,54},{5,53},{6,52},{7,55},{8,58},{9,... | collective-permute-start | bytes 2359304 | tf_op jit(solution)/shard_map/ppermute | solution.py:198
  66.7 22.7 %collective-permute-start.7 = (f32[32,6,8,128]{3,2,1,0:T(8,128)S(1)}, f32[32,6,8,128]{3,2,1,0:T(8,128)S(1)}, u32[]{:S(2)}, u32[]{:S(2)}) collective-permute-start(f32[32,6,8,128]{3,2,1,0:T(8,128)S(1)} %get-tuple-element.33), channel_id=1, source_target_pairs={{0,49},{1,50},{2,51},{3,48},{4,53},{5,54},{6,55},{7,52},{8,57},{9,... | collective-permute-start | bytes 2359304 | tf_op jit(solution)/shard_map/ppermute | solution.py:198
  66.7 39.7 %collective-permute-start.8 = (f32[32,6,8,128]{3,2,1,0:T(8,128)S(1)}, f32[32,6,8,128]{3,2,1,0:T(8,128)S(1)}, u32[]{:S(2)}, u32[]{:S(2)}) collective-permute-start(f32[32,6,8,128]{3,2,1,0:T(8,128)S(1)} %get-tuple-element.34), channel_id=1, source_target_pairs={{0,51},{1,48},{2,49},{3,50},{4,55},{5,52},{6,53},{7,54},{8,59},{9,... | collective-permute-start | bytes 2359304 | tf_op jit(solution)/shard_map/ppermute | solution.py:198
  71.7 38.7 %collective-permute-start.9 = (f32[32,6,8,128]{3,2,1,0:T(8,128)S(1)}, f32[32,6,8,128]{3,2,1,0:T(8,128)S(1)}, u32[]{:S(2)}, u32[]{:S(2)}) collective-permute-start(f32[32,6,8,128]{3,2,1,0:T(8,128)S(1)} %get-tuple-element.35), channel_id=1, source_target_pairs={{0,1},{1,0},{2,3},{3,2},{4,5},{5,4},{6,7},{7,6},{8,9},{9,8},{10,11... | collective-permute-start | bytes 2359304 | tf_op jit(solution)/shard_map/ppermute | solution.py:198
  71.7 51.6 %collective-permute-start.10 = (f32[32,6,8,128]{3,2,1,0:T(8,128)S(1)}, f32[32,6,8,128]{3,2,1,0:T(8,128)S(1)}, u32[]{:S(2)}, u32[]{:S(2)}) collective-permute-start(f32[32,6,8,128]{3,2,1,0:T(8,128)S(1)} %get-tuple-element.36), channel_id=1, source_target_pairs={{0,35},{1,34},{2,33},{3,32},{4,39},{5,38},{6,37},{7,36},{8,43},{9,... | collective-permute-start | bytes 2359304 | tf_op jit(solution)/shard_map/ppermute | solution.py:198
  74.9 65.2 %collective-permute-start.11 = (f32[32,6,8,128]{3,2,1,0:T(8,128)S(1)}, f32[32,6,8,128]{3,2,1,0:T(8,128)S(1)}, u32[]{:S(2)}, u32[]{:S(2)}) collective-permute-start(f32[32,6,8,128]{3,2,1,0:T(8,128)S(1)} %get-tuple-element.37), channel_id=1, source_target_pairs={{0,33},{1,32},{2,35},{3,34},{4,37},{5,36},{6,39},{7,38},{8,41},{9,... | collective-permute-start | bytes 2359304 | tf_op jit(solution)/shard_map/ppermute | solution.py:198
  89.3 56.5 %collective-permute-start.12 = (f32[32,6,8,128]{3,2,1,0:T(8,128)S(1)}, f32[32,6,8,128]{3,2,1,0:T(8,128)S(1)}, u32[]{:S(2)}, u32[]{:S(2)}) collective-permute-start(f32[32,6,8,128]{3,2,1,0:T(8,128)S(1)} %get-tuple-element.38), channel_id=1, source_target_pairs={{0,17},{1,18},{2,19},{3,16},{4,21},{5,22},{6,23},{7,20},{8,25},{9,... | collective-permute-start | bytes 2359304 | tf_op jit(solution)/shard_map/ppermute | solution.py:198
  106.4 40.5 %collective-permute-start.13 = (f32[32,6,8,128]{3,2,1,0:T(8,128)S(1)}, f32[32,6,8,128]{3,2,1,0:T(8,128)S(1)}, u32[]{:S(2)}, u32[]{:S(2)}) collective-permute-start(f32[32,6,8,128]{3,2,1,0:T(8,128)S(1)} %get-tuple-element.39), channel_id=1, source_target_pairs={{0,19},{1,16},{2,17},{3,18},{4,23},{5,20},{6,21},{7,22},{8,27},{9,... | collective-permute-start | bytes 2359304 | tf_op jit(solution)/shard_map/ppermute | solution.py:198
  110.4 74.4 %collective-permute-start.5 = (f32[32,6,8,128]{3,2,1,0:T(8,128)S(1)}, f32[32,6,8,128]{3,2,1,0:T(8,128)S(1)}, u32[]{:S(2)}, u32[]{:S(2)}) collective-permute-start(f32[32,6,8,128]{3,2,1,0:T(8,128)S(1)} %get-tuple-element.31._), channel_id=1, source_target_pairs={{0,34},{1,35},{2,32},{3,33},{4,38},{5,39},{6,36},{7,37},{8,42},{9,... | collective-permute-start | bytes 2359304 | tf_op jit(solution)/shard_map/ppermute | solution.py:198
  123.3 67.7 %collective-permute-start.14 = (f32[32,6,8,128]{3,2,1,0:T(8,128)S(1)}, f32[32,6,8,128]{3,2,1,0:T(8,128)S(1)}, u32[]{:S(2)}, u32[]{:S(2)}) collective-permute-start(f32[32,6,8,128]{3,2,1,0:T(8,128)S(1)} %get-tuple-element.40), channel_id=1, source_target_pairs={{0,2},{1,3},{2,0},{3,1},{4,6},{5,7},{6,4},{7,5},{8,10},{9,11},{10,... | collective-permute-start | bytes 2359304 | tf_op jit(solution)/shard_map/ppermute | solution.py:198
  140.2 52.1 %collective-permute-start.15 = (f32[16,6,8,128]{3,2,1,0:T(8,128)S(1)}, f32[16,6,8,128]{3,2,1,0:T(8,128)S(1)}, u32[]{:S(2)}, u32[]{:S(2)}) collective-permute-start(f32[16,6,8,128]{3,2,1,0:T(8,128)S(1)} %get-tuple-element.41), channel_id=1, source_target_pairs={{0,3},{1,2},{2,1},{3,0},{4,7},{5,6},{6,5},{7,4},{8,11},{9,10},{10,... | collective-permute-start | bytes 1179656 | tf_op jit(solution)/shard_map/ppermute | solution.py:198
  145.9 46.4 %collective-permute-start.16 = (f32[16,6,8,128]{3,2,1,0:T(8,128)S(1)}, f32[16,6,8,128]{3,2,1,0:T(8,128)S(1)}, u32[]{:S(2)}, u32[]{:S(2)}) collective-permute-start(f32[16,6,8,128]{3,2,1,0:T(8,128)S(1)} %get-tuple-element.42), channel_id=1, source_target_pairs={{0,32},{1,33},{2,34},{3,35},{4,36},{5,37},{6,38},{7,39},{8,40},{9,... | collective-permute-start | bytes 1179656 | tf_op jit(solution)/shard_map/ppermute | solution.py:198
  146.9 46.3 %collective-permute-start.17 = (f32[16,6,8,128]{3,2,1,0:T(8,128)S(1)}, f32[16,6,8,128]{3,2,1,0:T(8,128)S(1)}, u32[]{:S(2)}, u32[]{:S(2)}) collective-permute-start(f32[16,6,8,128]{3,2,1,0:T(8,128)S(1)} %get-tuple-element.43), channel_id=1, source_target_pairs={{0,3},{1,2},{2,1},{3,0},{4,7},{5,6},{6,5},{7,4},{8,11},{9,10},{10,... | collective-permute-start | bytes 1179656 | tf_op jit(solution)/shard_map/ppermute | solution.py:198
  184.8 8.5 %collective-permute-start.18 = (f32[16,6,8,128]{3,2,1,0:T(8,128)S(1)}, f32[16,6,8,128]{3,2,1,0:T(8,128)S(1)}, u32[]{:S(2)}, u32[]{:S(2)}) collective-permute-start(f32[16,6,8,128]{3,2,1,0:T(8,128)S(1)} %get-tuple-element.44), channel_id=1, source_target_pairs={{0,32},{1,33},{2,34},{3,35},{4,36},{5,37},{6,38},{7,39},{8,40},{9,... | collective-permute-start | bytes 1179656 | tf_op jit(solution)/shard_map/ppermute | solution.py:198
  (7 other events, 29.1 us)
